TPU v7x, 32 devices: a whole 2x2x4 slice. The times are simulated.
32 devices in a mesh: pipe: 2 (over x), expert: 8 (over z, core), dp: 2 (over y).
Axes of the slice: x: 2, y: 2, z: 4, core: 2. Of those that a mesh axis runs over, the one named last changes fastest.
Arguments:
- tokens: bfloat16 [2, 2048, 2048], P('pipe', ('expert', 'dp')), may hold values from -6 to 6
- cotangent: bfloat16 [2, 2048, 2048], P('pipe', ('expert', 'dp')), may hold values from -6 to 6
- norm_gain: float32 [2, 2048], P('pipe'), may hold values from 0.5 to 1.5
- first_ids: int32 [2, 2048, 2], P('pipe', ('expert', 'dp')), may hold values from 0 to 3, all different within a row; in each aligned block of 128 rows (0 to 127, 128 to 255, ..., all dimensions but the last counted through in order) at most 72 rows name the same one
- first_gates: float32 [2, 2048, 2], P('pipe', ('expert', 'dp')), may hold values from 0.1 to 1
- second_ids: int32 [2, 2048, 2], P('pipe', ('expert', 'dp')), may hold values from 0 to 3, all different within a row; in each aligned block of 128 rows (0 to 127, 128 to 255, ..., all dimensions but the last counted through in order) at most 72 rows name the same one
- second_gates: float32 [2, 2048, 2], P('pipe', ('expert', 'dp')), may hold values from 0.1 to 1
- new_slot: int32 [2, 4], P('pipe'), may hold values from 0 to 3, each once within a row
- inner_weight: float32 [2, 8, 2, 2048, 384], P('pipe', 'expert', None, 'dp'), may hold values from -0.125 to 0.125
- outer_weight: float32 [2, 8, 384, 2048], P('pipe', 'expert', None, 'dp'), may hold values from -0.21875 to 0.21875
- inner_mean: bfloat16 [2, 8, 2, 2048, 384], P('pipe', 'expert', None, 'dp'), may hold values from -60 to 60
- outer_mean: bfloat16 [2, 8, 384, 2048], P('pipe', 'expert', None, 'dp'), may hold values from -60 to 60
- inner_square: bfloat16 [2, 8, 2, 2048, 384], P('pipe', 'expert', None, 'dp'), may hold values from 10 to 1000
- outer_square: bfloat16 [2, 8, 384, 2048], P('pipe', 'expert', None, 'dp'), may hold values from 10 to 1000
Outputs:
- layer_out: bfloat16 [2, 2048, 2048], P('pipe', ('expert', 'dp'))
- weight_inner: float32 [2, 8, 2, 2048, 384], P('pipe', 'expert', None, 'dp')
- weight_outer: float32 [2, 8, 384, 2048], P('pipe', 'expert', None, 'dp')
- mean_inner: bfloat16 [2, 8, 2, 2048, 384], P('pipe', 'expert', None, 'dp')
- mean_outer: bfloat16 [2, 8, 384, 2048], P('pipe', 'expert', None, 'dp')
- square_inner: bfloat16 [2, 8, 2, 2048, 384], P('pipe', 'expert', None, 'dp')
- square_outer: bfloat16 [2, 8, 384, 2048], P('pipe', 'expert', None, 'dp')
Inputs may be any that keep to these rules, and one draw needn't show every extreme that they name: `first_ids`: each token names 2 different experts. Within the rows of one device no expert is named more than 72 times, and some device names some expert exactly 72 times. `second_ids`: as first_ids. `new_slot`: for each section, a permutation of the 4 experts.
All inputs are finite; a program needn't handle non-finite values.
Results may differ from a plain program's by a relative error of at most 0.008.
Values may be sent and summed in bfloat16 or wider, within the bound.
A program may use at most 128 MiB of HBM per device.

v0:
```python
import jax
import jax.numpy as jnp
from jax import lax
from jax.sharding import PartitionSpec as P

norm_eps = 1e-06
learn_rate = 0.001
beta_one = 0.9
beta_two = 0.95
adam_eps = 1e-08
bias_one = 0.999973438601112
bias_two = 0.994079470779667


def for_sending(array):

    def short(part):
        return part.astype(jnp.bfloat16) if part.dtype == jnp.float32 else part

    return jax.tree.map(short, array)


def passed_along(block, axis, distance):
    devices = range(lax.axis_size(axis))
    route = [((i - distance) % len(devices), i) for i in devices]
    return lax.ppermute(block, axis, route)


def normed(values, gain_row):
    widened = values.astype(jnp.float32)
    inverse_rms = lax.rsqrt(jnp.mean(widened * widened, axis=-1, keepdims=True) + norm_eps)
    return (widened * inverse_rms * gain_row).astype(jnp.bfloat16)


def silu_parts(gate_proj):
    logistic = jax.nn.sigmoid(gate_proj)
    return (gate_proj * logistic, logistic * (1.0 + gate_proj * (1.0 - logistic)))


def half_forward(token_rows, inner_full, outer_full):
    gate_proj = jnp.dot(token_rows, inner_full[0], preferred_element_type=jnp.float32)
    up_proj = jnp.dot(token_rows, inner_full[1], preferred_element_type=jnp.float32)
    activity = (silu_parts(gate_proj)[0] * up_proj).astype(jnp.bfloat16)
    half_out = jnp.dot(activity, outer_full, preferred_element_type=jnp.float32).astype(
        jnp.bfloat16
    )
    return (half_out, activity, gate_proj, up_proj)


def half_backward(token_rows, grad_rows, outer_full, activity, gate_proj, up_proj):
    grad_outer = jnp.dot(activity.T, grad_rows, preferred_element_type=jnp.float32)
    d_active = jnp.dot(grad_rows, outer_full.T, preferred_element_type=jnp.float32)
    swish_value, swish_slope = silu_parts(gate_proj)
    d_gate = (d_active * up_proj * swish_slope).astype(jnp.bfloat16)
    d_upper = (d_active * swish_value).astype(jnp.bfloat16)
    grad_gate = jnp.dot(token_rows.T, d_gate, preferred_element_type=jnp.float32)
    grad_upper = jnp.dot(token_rows.T, d_upper, preferred_element_type=jnp.float32)
    return (jnp.stack([grad_gate, grad_upper]), grad_outer)


def slot_index(ids, pair_of, capacity):
    flattened = ids.reshape(-1)
    expert_row = jnp.arange(pair_of.shape[0], dtype=jnp.int32)
    onehot = (flattened[:, None] == expert_row[None, :]).astype(jnp.int32)
    ranking = jnp.sum((jnp.cumsum(onehot, axis=0) - 1) * onehot, axis=1)
    target = jnp.sum(onehot * pair_of[None, :], axis=1)
    return (target * capacity + ranking).reshape(ids.shape)


def selection(slots, values, total_slots):
    positions = jnp.arange(total_slots, dtype=jnp.int32)
    result = jnp.zeros((total_slots, slots.shape[0]), jnp.float32)
    for column in range(slots.shape[1]):
        result = result + jnp.where(
            slots[:, column][None, :] == positions[:, None], values[:, column][None, :], 0.0
        )
    return result


def across_chips(blocks):
    pairs = blocks.shape[0]
    groups = [[2 * pair + core for pair in range(pairs)] for core in range(2)]
    return lax.all_to_all(
        blocks, "expert", split_axis=0, concat_axis=0, tiled=True, axis_index_groups=groups
    )


def to_partner(block):
    devices = range(lax.axis_size("expert"))
    return lax.ppermute(block, "expert", [(i, i ^ 1) for i in devices])


def dispatched(packed, pair_count, capacity):
    own = across_chips(packed.reshape(pair_count, capacity, packed.shape[-1]))
    own = own.reshape(pair_count * capacity, -1)
    return jnp.concatenate([own, to_partner(own)], axis=0)


def gather_weights(inner_master, outer_master):
    inner_full, outer_full = (
        lax.all_gather(inner_master.astype(jnp.bfloat16), "dp", axis=3, tiled=True),
        lax.all_gather(outer_master.astype(jnp.bfloat16), "dp", axis=3, tiled=True),
    )
    return (inner_full[0, 0], outer_full[0, 0])


def pack_rows(token_rows, gain_row, ids, pair_of, capacity):
    pair_count = pair_of.shape[0]
    normal = normed(token_rows, gain_row)
    slots = slot_index(ids, pair_of, capacity)
    picker = selection(slots, jnp.ones(slots.shape, jnp.float32), pair_count * capacity).astype(
        jnp.bfloat16
    )
    packed = jnp.dot(picker, normal, preferred_element_type=jnp.float32).astype(jnp.bfloat16)
    return (slots, dispatched(packed, pair_count, capacity))


def returned_rows(token_rows, half_out, slots, gates, pair_count, capacity):
    rows = pair_count * capacity
    summed = half_out[:rows].astype(jnp.float32) + to_partner(half_out[rows:]).astype(jnp.float32)
    back = across_chips(summed.astype(jnp.bfloat16).reshape(pair_count, capacity, -1))
    weighting = selection(slots, gates, rows)
    mixed = lax.dot_general(
        weighting,
        back.reshape(rows, -1).astype(jnp.float32),
        (((0,), (0,)), ((), ())),
        precision=lax.Precision.HIGHEST,
    )
    return (token_rows.astype(jnp.float32) + mixed).astype(jnp.bfloat16)


def adam_step(weight, mean, square, grads):
    mean_new = (beta_one * mean.astype(jnp.float32) + (1.0 - beta_one) * grads).astype(jnp.bfloat16)
    square_new = (beta_two * square.astype(jnp.float32) + (1.0 - beta_two) * grads * grads).astype(
        jnp.bfloat16
    )
    mean_wide = lax.optimization_barrier(mean_new).astype(jnp.float32)
    square_wide = lax.optimization_barrier(square_new).astype(jnp.float32)
    update = mean_wide / bias_one / (jnp.sqrt(square_wide / bias_two) + adam_eps)
    return (weight - learn_rate * update, mean_new, square_new)


def relocated(inner, outer, source):
    devices = source.shape[0]

    def moved(parts):
        spread = lax.all_to_all(parts, "expert", split_axis=0, concat_axis=0, tiled=True)
        ordered = jnp.take(spread, source, axis=0)
        return lax.all_to_all(ordered, "expert", split_axis=0, concat_axis=0, tiled=True)

    two, rows, columns = inner.shape[2:]
    parts = inner.reshape(two, devices, rows // devices, columns).transpose(1, 0, 2, 3)
    inner_back = moved(parts).transpose(1, 0, 2, 3).reshape(inner.shape)
    parts = outer.reshape(devices, outer.shape[2] // devices, outer.shape[3])
    return (inner_back, moved(parts).reshape(outer.shape))


def per_device(
    tokens,
    cotangent,
    norm_gain,
    first_ids,
    first_gates,
    second_ids,
    second_gates,
    new_slot,
    inner_weight,
    outer_weight,
    inner_mean,
    outer_mean,
    inner_square,
    outer_square,
):
    pair_count = new_slot.shape[1]
    rows_here = tokens.shape[1]
    top_count = first_ids.shape[2]
    width = tokens.shape[2]
    usual = rows_here * top_count // pair_count
    capacity = min(rows_here, usual + usual // 8)
    gain_row = norm_gain[0]
    identity_map = jnp.arange(pair_count, dtype=jnp.int32)
    new_pairs = new_slot[0]
    inverse = jnp.sum(
        jnp.where(new_pairs[:, None] == identity_map[None, :], identity_map[:, None], 0), axis=0
    )
    device_ids = jnp.arange(2 * pair_count, dtype=jnp.int32)
    source = 2 * jnp.repeat(inverse, 2) + device_ids % 2
    inner_low, outer_low = relocated(*for_sending((inner_weight, outer_weight)), source)
    inner_full, outer_full = gather_weights(inner_low, outer_low)
    slots, arrived = pack_rows(tokens[0], gain_row, first_ids[0], new_pairs, capacity)
    weighting = selection(slots, first_gates[0], pair_count * capacity)
    grad_packed = jnp.dot(
        weighting, cotangent[0].astype(jnp.float32), precision=lax.Precision.HIGHEST
    ).astype(jnp.bfloat16)
    grad_arrived = dispatched(grad_packed, pair_count, capacity)
    moments = (inner_mean, outer_mean, inner_square, outer_square)
    moments, inner_low, outer_low = lax.optimization_barrier((moments, inner_low, outer_low))
    old_mean_in, old_mean_out = relocated(moments[0], moments[1], source)
    old_square_in, old_square_out = relocated(moments[2], moments[3], source)
    half_out, activity, gate_proj, up_proj = half_forward(arrived, inner_full, outer_full)
    grad_inner, grad_outer = half_backward(
        arrived, grad_arrived, outer_full, activity, gate_proj, up_proj
    )
    sum_inner, sum_outer = (
        lax.psum_scatter(
            grad_inner[None, None].astype(jnp.bfloat16), "dp", scatter_dimension=3, tiled=True
        ).astype(jnp.float32),
        lax.psum_scatter(
            grad_outer[None, None].astype(jnp.bfloat16), "dp", scatter_dimension=3, tiled=True
        ).astype(jnp.float32),
    )
    first_out = returned_rows(
        tokens[0], half_out, slots, first_gates[0], pair_count, capacity
    )
    moved_inner, moved_mean_in, moved_square_in = adam_step(
        inner_low.astype(jnp.float32), old_mean_in, old_square_in, sum_inner
    )
    moved_outer, moved_mean_out, moved_square_out = adam_step(
        outer_low.astype(jnp.float32), old_mean_out, old_square_out, sum_outer
    )
    inner_two, outer_two = gather_weights(moved_inner, moved_outer)
    shifted = passed_along(first_out, "pipe", 1)
    slots_two, arrived_two = pack_rows(shifted, gain_row, second_ids[0], new_pairs, capacity)
    half_two = half_forward(arrived_two, inner_two, outer_two)[0]
    second_out = returned_rows(
        shifted, half_two, slots_two, second_gates[0], pair_count, capacity
    )
    return (
        second_out[None],
        moved_inner,
        moved_outer,
        moved_mean_in,
        moved_mean_out,
        moved_square_in,
        moved_square_out,
    )


def solution(mesh):
    return jax.shard_map(
        per_device,
        mesh=mesh,
        in_specs=(
            P("pipe", ("expert", "dp"), None),
            P("pipe", ("expert", "dp"), None),
            P("pipe", None),
            P("pipe", ("expert", "dp"), None),
            P("pipe", ("expert", "dp"), None),
            P("pipe", ("expert", "dp"), None),
            P("pipe", ("expert", "dp"), None),
            P("pipe", None),
            P("pipe", "expert", None, "dp", None),
            P("pipe", "expert", None, "dp"),
            P("pipe", "expert", None, "dp", None),
            P("pipe", "expert", None, "dp"),
            P("pipe", "expert", None, "dp", None),
            P("pipe", "expert", None, "dp"),
        ),
        out_specs=(
            P("pipe", ("expert", "dp"), None),
            P("pipe", "expert", None, "dp", None),
            P("pipe", "expert", None, "dp"),
            P("pipe", "expert", None, "dp", None),
            P("pipe", "expert", None, "dp"),
            P("pipe", "expert", None, "dp", None),
            P("pipe", "expert", None, "dp"),
        ),
        check_vma=False,
    )
```

profile of v0, /device:TPU:0, one launch (start us, length us, event | category | flops | bytes accessed | tf_op | source)
XLA Modules:
  0.0 599.4 jit_solution(6299541725678960014)
XLA Ops:
  9.7 6.5 %all-to-all-start.3 = ((bf16[8,48,1024]{2,1,0:T(8,128)(2,1)}), bf16[8,48,1024]{2,1,0:T(8,128)(2,1)S(1)}, u32[]{:S(2)}, u32[]{:S(2)}) async-start(bf16[8,48,1024]{2,1,0:T(8,128)(2,1)} %bitcast.17), calls=%async_computation.3 | async-start | bytes 1572864 | tf_op jit(solution)/shard_map/all_to_all | solution.py:147
  22.4 14.7 %all-to-all-done.3 = bf16[8,48,1024]{2,1,0:T(8,128)(2,1)S(1)} async-done(((bf16[8,48,1024]{2,1,0:T(8,128)(2,1)}), bf16[8,48,1024]{2,1,0:T(8,128)(2,1)S(1)}, u32[]{:S(2)}, u32[]{:S(2)}) %all-to-all-start.3) | async-done | bytes 786464 | tf_op jit(solution)/shard_map/all_to_all | solution.py:147
  37.1 3.5 all-to-all-start
  44.0 25.1 %all-to-all-done = bf16[4,72,2048]{2,1,0:T(8,128)(2,1)S(1)} async-done(((bf16[4,72,2048]{2,1,0:T(8,128)(2,1)}), bf16[4,72,2048]{2,1,0:T(8,128)(2,1)S(1)}, u32[]{:S(2)}, u32[]{:S(2)}) %all-to-all-start) | async-done | bytes 1179680 | tf_op jit(solution)/shard_map/all_to_all | solution.py:83
  70.1 3.6 all-to-all-start.1
  77.6 33.8 %all-to-all-done.1 = bf16[8,2,128,384]{3,2,1,0:T(8,128)(2,1)S(1)} async-done(((bf16[8,2,128,384]{3,2,1,0:T(8,128)(2,1)}), bf16[8,2,128,384]{3,2,1,0:T(8,128)(2,1)S(1)}, u32[]{:S(2)}, u32[]{:S(2)}) %all-to-all-start.1) | async-done | bytes 1572896 | tf_op jit(solution)/shard_map/all_to_all | solution.py:147
  111.5 3.5 all-to-all-start.4
  116.9 2.8 broadcast_select_fusion.2
  119.7 16.2 %all-to-all-done.4 = bf16[8,48,1024]{2,1,0:T(8,128)(2,1)S(1)} async-done(((bf16[8,48,1024]{2,1,0:T(8,128)(2,1)}), bf16[8,48,1024]{2,1,0:T(8,128)(2,1)S(1)}, u32[]{:S(2)}, u32[]{:S(2)}) %all-to-all-start.4) | async-done | bytes 786464 | tf_op jit(solution)/shard_map/all_to_all | solution.py:149
  136.8 3.6 all-to-all-start.2
  142.5 35.6 %all-to-all-done.2 = bf16[8,2,128,384]{3,2,1,0:T(8,128)(2,1)S(1)} async-done(((bf16[8,2,128,384]{3,2,1,0:T(8,128)(2,1)}), bf16[8,2,128,384]{3,2,1,0:T(8,128)(2,1)S(1)}, u32[]{:S(2)}, u32[]{:S(2)}) %all-to-all-start.2) | async-done | bytes 1572896 | tf_op jit(solution)/shard_map/all_to_all | solution.py:149
  178.1 4.3 all-to-all-start.9
  183.7 27.3 %all-to-all-done.9 = bf16[4,72,2048]{2,1,0:T(8,128)(2,1)} async-done(((bf16[4,72,2048]{2,1,0:T(8,128)(2,1)}), bf16[4,72,2048]{2,1,0:T(8,128)(2,1)}, u32[]{:S(2)}, u32[]{:S(2)}) %all-to-all-start.9) | async-done | bytes 1179680 | tf_op jit(solution)/shard_map/all_to_all | solution.py:83
  211.0 3.5 all-to-all-start.14
  215.3 20.1 %all-to-all-done.14 = bf16[8,48,1024]{2,1,0:T(8,128)(2,1)S(1)} async-done(((bf16[8,48,1024]{2,1,0:T(8,128)(2,1)}), bf16[8,48,1024]{2,1,0:T(8,128)(2,1)S(1)}, u32[]{:S(2)}, u32[]{:S(2)}) %all-to-all-start.14) | async-done | bytes 786464 | tf_op jit(solution)/shard_map/all_to_all | solution.py:147
  235.4 3.7 all-to-all-start.12
  241.2 18.8 %all-to-all-done.12 = bf16[8,48,1024]{2,1,0:T(8,128)(2,1)S(1)} async-done(((bf16[8,48,1024]{2,1,0:T(8,128)(2,1)}), bf16[8,48,1024]{2,1,0:T(8,128)(2,1)S(1)}, u32[]{:S(2)}, u32[]{:S(2)}) %all-to-all-start.12) | async-done | bytes 786464 | tf_op jit(solution)/shard_map/all_to_all | solution.py:147
  260.8 3.6 all-to-all-start.7
  267.8 4.4 fusion.19
  273.6 28.6 %all-to-all-done.7 = bf16[8,2,128,384]{3,2,1,0:T(8,128)(2,1)S(1)} async-done(((bf16[8,2,128,384]{3,2,1,0:T(8,128)(2,1)}), bf16[8,2,128,384]{3,2,1,0:T(8,128)(2,1)S(1)}, u32[]{:S(2)}, u32[]{:S(2)}) %all-to-all-start.7) | async-done | bytes 1572896 | tf_op jit(solution)/shard_map/all_to_all | solution.py:147
  302.1 3.6 all-to-all-start.10
  306.0 3.6 fusion.17
  309.7 3.2 fusion.5
  312.9 3.4 multiply_convert_fusion.3
  316.4 3.1 fusion.4
  329.4 14.0 %all-to-all-done.10 = bf16[8,2,128,384]{3,2,1,0:T(8,128)(2,1)S(1)} async-done(((bf16[8,2,128,384]{3,2,1,0:T(8,128)(2,1)}), bf16[8,2,128,384]{3,2,1,0:T(8,128)(2,1)S(1)}, u32[]{:S(2)}, u32[]{:S(2)}) %all-to-all-start.10) | async-done | bytes 1572896 | tf_op jit(solution)/shard_map/all_to_all | solution.py:147
  343.5 4.2 all-to-all-start.13
  351.5 3.4 broadcast_select_fusion.1
  354.9 13.7 %all-to-all-done.13 = bf16[8,48,1024]{2,1,0:T(8,128)(2,1)} async-done(((bf16[8,48,1024]{2,1,0:T(8,128)(2,1)}), bf16[8,48,1024]{2,1,0:T(8,128)(2,1)}, u32[]{:S(2)}, u32[]{:S(2)}) %all-to-all-start.13) | async-done | bytes 786464 | tf_op jit(solution)/shard_map/all_to_all | solution.py:149
  368.6 40.2 %all_to_all.85 = bf16[8,2,128,384]{3,2,1,0:T(8,128)(2,1)S(1)} all-to-all(bf16[8,2,128,384]{3,2,1,0:T(8,128)(2,1)S(1)} %get-tuple-element.45), channel_id=1, replica_groups=mesh['pipe'=2,'expert'=8,'dp'=2] {'expert'}, dimensions={0} | all-to-all | bytes 3145728 | tf_op jit(solution)/shard_map/all_to_all | solution.py:149
  408.8 3.6 all-to-all-start.11
  412.5 2.9 convolution_convert_fusion.1
  418.3 4.2 fusion.6
  422.5 3.1 add_convert_fusion.1
  425.7 24.5 %all-to-all-done.11 = bf16[8,2,128,384]{3,2,1,0:T(8,128)(2,1)S(1)} async-done(((bf16[8,2,128,384]{3,2,1,0:T(8,128)(2,1)}), bf16[8,2,128,384]{3,2,1,0:T(8,128)(2,1)S(1)}, u32[]{:S(2)}, u32[]{:S(2)}) %all-to-all-start.11) | async-done | bytes 1572896 | tf_op jit(solution)/shard_map/all_to_all | solution.py:149
  450.2 4.3 all-to-all-start.5
  458.7 3.3 fusion.1
  462.1 4.0 fusion.86
  466.1 17.0 %all-to-all-done.5 = bf16[4,72,2048]{2,1,0:T(8,128)(2,1)} async-done(((bf16[4,72,2048]{2,1,0:T(8,128)(2,1)}), bf16[4,72,2048]{2,1,0:T(8,128)(2,1)}, u32[]{:S(2)}, u32[]{:S(2)}) %all-to-all-start.5) | async-done | bytes 1179680 | tf_op jit(solution)/shard_map/all_to_all | solution.py:83
  483.0 3.5 all-to-all-start.15
  490.8 12.4 %collective-permute-done.2 = bf16[128,2048]{1,0:T(8,128)(2,1)S(1)} collective-permute-done((bf16[128,2048]{1,0:T(8,128)(2,1)S(1)}, bf16[128,2048]{1,0:T(8,128)(2,1)S(1)}, u32[]{:S(2)}, u32[]{:S(2)}) %collective-permute-start.2) | collective-permute-done | bytes 524320 | tf_op jit(solution)/shard_map/ppermute | solution.py:26
  507.5 4.3 all-to-all-start.6
  517.6 22.8 %all-to-all-done.6 = bf16[4,72,2048]{2,1,0:T(8,128)(2,1)} async-done(((bf16[4,72,2048]{2,1,0:T(8,128)(2,1)}), bf16[4,72,2048]{2,1,0:T(8,128)(2,1)}, u32[]{:S(2)}, u32[]{:S(2)}) %all-to-all-start.6) | async-done | bytes 1179680 | tf_op jit(solution)/shard_map/all_to_all | solution.py:83
  540.4 3.1 collective-permute-done.3
  543.4 4.5 fusion.14
  547.9 5.5 convolution_convert_fusion
  558.0 3.7 all-to-all-start.16
  561.7 29.0 %all-to-all-done.16 = bf16[4,72,2048]{2,1,0:T(8,128)(2,1)S(1)} async-done(((bf16[4,72,2048]{2,1,0:T(8,128)(2,1)}), bf16[4,72,2048]{2,1,0:T(8,128)(2,1)S(1)}, u32[]{:S(2)}, u32[]{:S(2)}) %all-to-all-start.16) | async-done | bytes 1179680 | tf_op jit(solution)/shard_map/all_to_all | solution.py:83
  (172 shorter events, 73.3 us)
Async XLA Ops:
  7.2 133.2 %copy-start = (bf16[1,128,2048]{2,1,0:T(8,128)(2,1)S(1)}, bf16[1,128,2048]{2,1,0:T(8,128)(2,1)}, u32[]{:S(2)}) copy-start(bf16[1,128,2048]{2,1,0:T(8,128)(2,1)} %param.19) | copy-start | bytes 1572868
  7.2 9.0 %copy-start.27 = (s32[1,128,2]{1,2,0:T(2,128)S(1)}, s32[1,128,2]{1,2,0:T(2,128)}, u32[]{:S(2)}) copy-start(s32[1,128,2]{1,2,0:T(2,128)} %param.23) | copy-start | bytes 3076
  7.2 10.9 %copy-start.28 = (s32[1,128,2]{1,2,0:T(2,128)S(1)}, s32[1,128,2]{1,2,0:T(2,128)}, u32[]{:S(2)}) copy-start(s32[1,128,2]{1,2,0:T(2,128)} %param.21) | copy-start | bytes 3076
  9.7 10.6 %copy-start.31 = (s32[1,4]{1,0:T(1,128)S(1)}, s32[1,4]{1,0:T(1,128)}, u32[]{:S(2)}) copy-start(s32[1,4]{1,0:T(1,128)} %param.25) | copy-start | bytes 52
  9.7 11.0 %copy-start.9 = (bf16[1,128,2048]{2,1,0:T(8,128)(2,1)S(1)}, bf16[1,128,2048]{2,1,0:T(8,128)(2,1)}, u32[]{:S(2)}) copy-start(bf16[1,128,2048]{2,1,0:T(8,128)(2,1)} %param.18) | copy-start | bytes 1572868
  9.7 11.2 %copy-start.26 = (f32[1,2048]{1,0:T(1,128)S(1)}, f32[1,2048]{1,0:T(1,128)}, u32[]{:S(2)}) copy-start(f32[1,2048]{1,0:T(1,128)} %param.20) | copy-start | bytes 24580
  9.7 27.4 %all-to-all-start.3 = ((bf16[8,48,1024]{2,1,0:T(8,128)(2,1)}), bf16[8,48,1024]{2,1,0:T(8,128)(2,1)S(1)}, u32[]{:S(2)}, u32[]{:S(2)}) async-start(bf16[8,48,1024]{2,1,0:T(8,128)(2,1)} %bitcast.17), calls=%async_computation.3 | async-start | bytes 1572864 | tf_op jit(solution)/shard_map/all_to_all | solution.py:147
  37.1 5.6 copy-start.13
  37.1 32.0 %all-to-all-start = ((bf16[4,72,2048]{2,1,0:T(8,128)(2,1)}), bf16[4,72,2048]{2,1,0:T(8,128)(2,1)S(1)}, u32[]{:S(2)}, u32[]{:S(2)}) async-start(bf16[4,72,2048]{2,1,0:T(8,128)(2,1)} %bitcast.9), calls=%async_computation | async-start | bytes 2359296 | tf_op jit(solution)/shard_map/all_to_all | solution.py:83
  69.1 4.9 copy-start.14
  70.1 41.3 %all-to-all-start.1 = ((bf16[8,2,128,384]{3,2,1,0:T(8,128)(2,1)}), bf16[8,2,128,384]{3,2,1,0:T(8,128)(2,1)S(1)}, u32[]{:S(2)}, u32[]{:S(2)}) async-start(bf16[8,2,128,384]{3,2,1,0:T(8,128)(2,1)} %bitcast.126), calls=%async_computation.1 | async-start | bytes 3145728 | tf_op jit(solution)/shard_map/all_to_all | solution.py:147
  111.5 24.4 %all-to-all-start.4 = ((bf16[8,48,1024]{2,1,0:T(8,128)(2,1)}), bf16[8,48,1024]{2,1,0:T(8,128)(2,1)S(1)}, u32[]{:S(2)}, u32[]{:S(2)}) async-start(bf16[8,48,1024]{2,1,0:T(8,128)(2,1)} %broadcast_select_fusion.5), calls=%async_computation.4 | async-start | bytes 1572864 | tf_op jit(solution)/shard_map/all_to_all | solution.py:149
  119.7 20.6 %copy-start.29 = (f32[1,128,2]{1,2,0:T(2,128)S(1)}, f32[1,128,2]{1,2,0:T(2,128)}, u32[]{:S(2)}) copy-start(f32[1,128,2]{1,2,0:T(2,128)} %param.22) | copy-start | bytes 3076
  136.8 41.3 %all-to-all-start.2 = ((bf16[8,2,128,384]{3,2,1,0:T(8,128)(2,1)}), bf16[8,2,128,384]{3,2,1,0:T(8,128)(2,1)S(1)}, u32[]{:S(2)}, u32[]{:S(2)}) async-start(bf16[8,2,128,384]{3,2,1,0:T(8,128)(2,1)} %broadcast_select_fusion.2), calls=%async_computation.2 | async-start | bytes 3145728 | tf_op jit(solution)/shard_map/all_to_all | solution.py:149
  178.1 32.9 %all-to-all-start.9 = ((bf16[4,72,2048]{2,1,0:T(8,128)(2,1)}), bf16[4,72,2048]{2,1,0:T(8,128)(2,1)}, u32[]{:S(2)}, u32[]{:S(2)}) async-start(bf16[4,72,2048]{2,1,0:T(8,128)(2,1)} %bitcast.139), calls=%async_computation.9 | async-start | bytes 2359296 | tf_op jit(solution)/shard_map/all_to_all | solution.py:83
  211.0 24.4 %all-to-all-start.14 = ((bf16[8,48,1024]{2,1,0:T(8,128)(2,1)}), bf16[8,48,1024]{2,1,0:T(8,128)(2,1)S(1)}, u32[]{:S(2)}, u32[]{:S(2)}) async-start(bf16[8,48,1024]{2,1,0:T(8,128)(2,1)} %bitcast.147), calls=%async_computation.16 | async-start | bytes 1572864 | tf_op jit(solution)/shard_map/all_to_all | solution.py:147
  214.5 53.3 %all-gather.7.cloned.1.call-start = ((), (), s32[]{:S(2)}) async-start(), calls=%async_computation.20 | async-start | bytes 2359296 | tf_op jit(solution)/shard_map/all_gather | solution.py:102
  235.4 4.4 copy-start.15
  235.4 4.5 copy-start.22
  235.4 24.6 %all-to-all-start.12 = ((bf16[8,48,1024]{2,1,0:T(8,128)(2,1)}), bf16[8,48,1024]{2,1,0:T(8,128)(2,1)S(1)}, u32[]{:S(2)}, u32[]{:S(2)}) async-start(bf16[8,48,1024]{2,1,0:T(8,128)(2,1)} %bitcast.148), calls=%async_computation.13 | async-start | bytes 1572864 | tf_op jit(solution)/shard_map/all_to_all | solution.py:147
  239.1 66.9 %all-gather.5.cloned.1.call-start = ((), (), s32[]{:S(2)}) async-start(), calls=%async_computation.19 | async-start | bytes 4718592 | tf_op jit(solution)/shard_map/all_gather | solution.py:101
  260.8 41.3 %all-to-all-start.7 = ((bf16[8,2,128,384]{3,2,1,0:T(8,128)(2,1)}), bf16[8,2,128,384]{3,2,1,0:T(8,128)(2,1)S(1)}, u32[]{:S(2)}, u32[]{:S(2)}) async-start(bf16[8,2,128,384]{3,2,1,0:T(8,128)(2,1)} %bitcast.125), calls=%async_computation.7 | async-start | bytes 3145728 | tf_op jit(solution)/shard_map/all_to_all | solution.py:147
  264.4 3.4 collective-permute-start.4
  264.8 7.4 %copy-start.23 = (bf16[1,1,2,1024,384]{4,3,2,1,0:T(8,128)(2,1)S(1)}, bf16[1,1,2,1024,384]{4,3,2,1,0:T(8,128)(2,1)}, u32[]{:S(2)}) copy-start(bf16[1,1,2,1024,384]{4,3,2,1,0:T(8,128)(2,1)} %param.30) | copy-start | bytes 4718596
  264.8 41.1 %collective-permute-start = (bf16[288,2048]{1,0:T(8,128)(2,1)}, bf16[288,2048]{1,0:T(8,128)(2,1)}, u32[]{:S(2)}, u32[]{:S(2)}) collective-permute-start(bf16[288,2048]{1,0:T(8,128)(2,1)} %bitcast.142), channel_id=1, source_target_pairs={{0,2},{2,0},{4,6},{6,4},{8,10},{10,8},{12,14},{14,12},{1,3},{3,1},... | collective-permute-start | bytes 3538952 | tf_op jit(solution)/shard_map/ppermute | solution.py:90
  302.1 41.3 %all-to-all-start.10 = ((bf16[8,2,128,384]{3,2,1,0:T(8,128)(2,1)}), bf16[8,2,128,384]{3,2,1,0:T(8,128)(2,1)S(1)}, u32[]{:S(2)}, u32[]{:S(2)}) async-start(bf16[8,2,128,384]{3,2,1,0:T(8,128)(2,1)} %bitcast.124), calls=%async_computation.11 | async-start | bytes 3145728 | tf_op jit(solution)/shard_map/all_to_all | solution.py:147
  305.7 153.0 %reduce-scatter.3.cloned.1.call-start = ((), (), s32[]{:S(2)}) async-start(), calls=%async_computation.21 | async-start | bytes 4718592 | tf_op jit(solution)/shard_map/reduce_scatter | solution.py:205
  343.5 25.2 %all-to-all-start.13 = ((bf16[8,48,1024]{2,1,0:T(8,128)(2,1)}), bf16[8,48,1024]{2,1,0:T(8,128)(2,1)}, u32[]{:S(2)}, u32[]{:S(2)}) async-start(bf16[8,48,1024]{2,1,0:T(8,128)(2,1)} %get-tuple-element.47), calls=%async_computation.14 | async-start | bytes 1572864 | tf_op jit(solution)/shard_map/all_to_all | solution.py:149
  408.8 41.3 %all-to-all-start.11 = ((bf16[8,2,128,384]{3,2,1,0:T(8,128)(2,1)}), bf16[8,2,128,384]{3,2,1,0:T(8,128)(2,1)S(1)}, u32[]{:S(2)}, u32[]{:S(2)}) async-start(bf16[8,2,128,384]{3,2,1,0:T(8,128)(2,1)} %get-tuple-element.46), calls=%async_computation.12 | async-start | bytes 3145728 | tf_op jit(solution)/shard_map/all_to_all | solution.py:149
  412.4 101.0 %reduce-scatter.5.cloned.1.call-start = ((), (), s32[]{:S(2)}) async-start(), calls=%async_computation.23 | async-start | bytes 2359296 | tf_op jit(solution)/shard_map/reduce_scatter | solution.py:208
  417.9 4.6 collective-permute-start.1
  450.2 4.6 copy-start.5
  450.2 32.9 %all-to-all-start.5 = ((bf16[4,72,2048]{2,1,0:T(8,128)(2,1)}), bf16[4,72,2048]{2,1,0:T(8,128)(2,1)}, u32[]{:S(2)}, u32[]{:S(2)}) async-start(bf16[4,72,2048]{2,1,0:T(8,128)(2,1)} %bitcast.137), calls=%async_computation.5 | async-start | bytes 2359296 | tf_op jit(solution)/shard_map/all_to_all | solution.py:83
  454.5 89.0 %all-gather.9.cloned.1.call-start = ((), (), s32[]{:S(2)}) async-start(), calls=%async_computation.22 | async-start | bytes 4718592 | tf_op jit(solution)/shard_map/all_gather | solution.py:101
  462.0 4.0 copy-start.7
  466.1 20.5 %copy-start.10 = (bf16[1,128,2048]{2,1,0:T(8,128)(2,1)S(1)}, bf16[1,128,2048]{2,1,0:T(8,128)(2,1)}, u32[]{:S(2)}) copy-start(bf16[1,128,2048]{2,1,0:T(8,128)(2,1)} %param.18) | copy-start | bytes 1572868
  483.0 24.4 %all-to-all-start.15 = ((bf16[8,48,1024]{2,1,0:T(8,128)(2,1)}), bf16[8,48,1024]{2,1,0:T(8,128)(2,1)S(1)}, u32[]{:S(2)}, u32[]{:S(2)}) async-start(bf16[8,48,1024]{2,1,0:T(8,128)(2,1)} %get-tuple-element.48), calls=%async_computation.17 | async-start | bytes 1572864 | tf_op jit(solution)/shard_map/all_to_all | solution.py:149
  488.9 14.3 %collective-permute-start.2 = (bf16[128,2048]{1,0:T(8,128)(2,1)S(1)}, bf16[128,2048]{1,0:T(8,128)(2,1)S(1)}, u32[]{:S(2)}, u32[]{:S(2)}) collective-permute-start(bf16[128,2048]{1,0:T(8,128)(2,1)S(1)} %fusion.7), channel_id=1, source_target_pairs={{16,0},{0,16},{17,1},{1,17},{18,2},{2,18},{19,3},{3,19},{20,4},{4,... | collective-permute-start | bytes 1572872 | tf_op jit(solution)/shard_map/ppermute | solution.py:26
  503.2 4.3 copy-start.11
  507.5 4.3 copy-start.17
  507.5 32.9 %all-to-all-start.6 = ((bf16[4,72,2048]{2,1,0:T(8,128)(2,1)}), bf16[4,72,2048]{2,1,0:T(8,128)(2,1)}, u32[]{:S(2)}, u32[]{:S(2)}) async-start(bf16[4,72,2048]{2,1,0:T(8,128)(2,1)} %bitcast.27), calls=%async_computation.6 | async-start | bytes 2359296 | tf_op jit(solution)/shard_map/all_to_all | solution.py:83
  511.8 36.1 %all-gather.11.cloned.1.call-start = ((), (), s32[]{:S(2)}) async-start(), calls=%async_computation.24 | async-start | bytes 2359296 | tf_op jit(solution)/shard_map/all_gather | solution.py:102
  540.4 3.1 collective-permute-start.3
  543.4 4.5 copy-start.33
  553.5 2.9 collective-permute-start.5
  558.0 32.8 %copy-start.12 = (bf16[128,2048]{1,0:T(8,128)(2,1)S(1)}, bf16[128,2048]{1,0:T(8,128)(2,1)}, u32[]{:S(2)}) copy-start(bf16[128,2048]{1,0:T(8,128)(2,1)} %copy-done.11) | copy-start | bytes 1572868
  558.0 32.7 %all-to-all-start.16 = ((bf16[4,72,2048]{2,1,0:T(8,128)(2,1)}), bf16[4,72,2048]{2,1,0:T(8,128)(2,1)S(1)}, u32[]{:S(2)}, u32[]{:S(2)}) async-start(bf16[4,72,2048]{2,1,0:T(8,128)(2,1)} %bitcast.50), calls=%async_computation.18 | async-start | bytes 2359296 | tf_op jit(solution)/shard_map/all_to_all | solution.py:83
  561.7 30.9 %copy-start.1 = (bf16[1,128,2048]{2,1,0:T(8,128)(2,1)S(1)}, bf16[1,128,2048]{2,1,0:T(8,128)(2,1)}, u32[]{:S(2)}) copy-start(bf16[1,128,2048]{2,1,0:T(8,128)(2,1)} %param.19) | copy-start | bytes 1572868
  (16 other events, 36.5 us)
Sparse Core Ops, SparseCore 0:
  216.9 28.5 all-gather.6
  247.6 44.8 all-gather.4
  321.6 44.5 reduce-scatter.2
  422.7 27.3 reduce-scatter.4
  466.2 46.0 all-gather.8
  517.7 28.5 all-gather.10
where the time goes:
time: 601 us; the launch traced here: 599 us
  waiting for transfers between devices  366 us (61%)
  starting transfers between devices  66.3 us (11%)
  matrix products  44.4 us (7%)
  blocking collectives  40.2 us (7%)
  other arithmetic  39.1 us (7%)
  local copies, waits for them, and re-layouts  28.6 us (5%)
  between operations  14.8 us (2%)
    all_to_all x6, waiting for transfers between devices, moved(): lax.all_to_all(parts, 'expert', split_axis=0, concat_axis=0, tiled=True)  130 us
    all_to_all x5, waiting for transfers between devices, across_chips(): lax.all_to_all(blocks, 'expert', split_axis=0, concat_axis=0, tiled=True,...  121 us
    all_to_all x5, waiting for transfers between devices, moved(): lax.all_to_all(ordered, 'expert', split_axis=0, concat_axis=0, tiled=True)  92.3 us
    all_to_all x1, blocking collectives, moved(): lax.all_to_all(ordered, 'expert', split_axis=0, concat_axis=0, tiled=True)  40.2 us
    all_to_all x6, starting transfers between devices, moved(): lax.all_to_all(parts, 'expert', split_axis=0, concat_axis=0, tiled=True)  24.5 us
    all_to_all x5, starting transfers between devices, across_chips(): lax.all_to_all(blocks, 'expert', split_axis=0, concat_axis=0, tiled=True,...  20.1 us
    all_to_all x5, starting transfers between devices, moved(): lax.all_to_all(ordered, 'expert', split_axis=0, concat_axis=0, tiled=True)  18.5 us
    gather x6, local copies, waits for them, and re-layouts, moved(): ordered = jnp.take(spread, source, axis=0)  12.4 us
  transfers between devices with their start and end apart: 28, of which 20 were waited for; matrix products, arithmetic and copies ran while one was open for 16% of the time, Pallas kernels for 0%

commit v1 on v0

--- a/solution.py
+++ b/solution.py
@@ -1,7 +1,13 @@
+import functools
+
 import jax
 import jax.numpy as jnp
 from jax import lax
+from jax.experimental import pallas as pl
+from jax.experimental.pallas import tpu as pltpu
 from jax.sharding import PartitionSpec as P
+
+MESH = pl.DeviceIdType.MESH
 
 norm_eps = 1e-06
 learn_rate = 0.001
@@ -140,19 +146,227 @@
     return (weight - learn_rate * update, mean_new, square_new)
 
 
-def relocated(inner, outer, source):
-    devices = source.shape[0]
-
-    def moved(parts):
-        spread = lax.all_to_all(parts, "expert", split_axis=0, concat_axis=0, tiled=True)
-        ordered = jnp.take(spread, source, axis=0)
-        return lax.all_to_all(ordered, "expert", split_axis=0, concat_axis=0, tiled=True)
-
-    two, rows, columns = inner.shape[2:]
-    parts = inner.reshape(two, devices, rows // devices, columns).transpose(1, 0, 2, 3)
-    inner_back = moved(parts).transpose(1, 0, 2, 3).reshape(inner.shape)
-    parts = outer.reshape(devices, outer.shape[2] // devices, outer.shape[3])
-    return (inner_back, moved(parts).reshape(outer.shape))
+def crossing_counts(place):
+    count = place.shape[-1]
+    own = jnp.arange(count, dtype=jnp.int32)
+    link = own[:-1, None]
+    crosses = (own[None, :] <= link) & (place[..., None, :] > link)
+    return jnp.sum(crosses.astype(jnp.int32), axis=-1)
+
+
+def journey_rounds(place):
+    count = place.shape[0]
+    places = [place[i] for i in range(count)]
+
+    def coloured(order, overlaps):
+        rounds = [None] * count
+        for position, item in enumerate(order):
+            taken = [
+                [overlaps(before, item) & (rounds[before] == r) for before in order[:position]]
+                for r in range(count // 2)
+            ]
+            chosen = jnp.int32(0)
+            for r in reversed(range(count // 2)):
+                busy = functools.reduce(jnp.logical_or, taken[r], jnp.bool_(False))
+                chosen = jnp.where(busy, chosen, r)
+            rounds[item] = chosen
+        return rounds
+
+    up = coloured(list(range(count)), lambda b, i: (places[b] > i) & (places[i] > i))
+    down = coloured(
+        list(reversed(range(count))), lambda b, i: (places[b] < i) & (places[i] < i)
+    )
+    moved = [
+        jnp.where(places[i] > i, up[i], jnp.where(places[i] < i, down[i], -1)) for i in range(count)
+    ]
+    return jnp.stack(moved)
+
+
+def journey_flags(place, chip, this_round):
+    count = place.shape[0]
+    own = jnp.arange(count, dtype=jnp.int32)
+    active = journey_rounds(place) == this_round
+    starts = active & (own == chip)
+    ends = active & (place == chip)
+    up, down = place > own, place < own
+    return jnp.stack(
+        [jnp.any(starts & up), jnp.any(starts & down), jnp.any(ends & up), jnp.any(ends & down)]
+    ).astype(jnp.int32)
+
+
+def conveyor_kernel(chips, lag, pieces, flags, *refs):
+    count = len(pieces)
+    own = refs[:count]
+    out = refs[count : 2 * count]
+    up_in = refs[2 * count : 3 * count]
+    down_in = refs[3 * count : 4 * count]
+    up_out = refs[4 * count : 5 * count]
+    down_out = refs[5 * count : 6 * count]
+    up_sent, down_sent, up_got, down_got = refs[6 * count :]
+    place = lax.axis_index("expert")
+    chip = place // 2
+    above, below = {"expert": place + 2}, {"expert": place - 2}
+    has_above, has_below = chip < chips - 1, chip > 0
+
+    barrier = pltpu.get_barrier_semaphore()
+
+    @pl.when(has_above)
+    def _():
+        pl.semaphore_signal(barrier, inc=1, device_id=above, device_id_type=MESH)
+
+    @pl.when(has_below)
+    def _():
+        pl.semaphore_signal(barrier, inc=1, device_id=below, device_id_type=MESH)
+
+    pl.semaphore_wait(barrier, has_above.astype(jnp.int32) + has_below.astype(jnp.int32))
+
+    start_up, start_down = flags[0] == 1, flags[1] == 1
+    take_up, take_down = flags[2] == 1, flags[3] == 1
+    total = sum(number for number, _ in pieces)
+
+    def send(source, target, sent, got, k, index, device):
+        pltpu.make_async_remote_copy(
+            src_ref=source,
+            dst_ref=target,
+            send_sem=sent.at[k],
+            recv_sem=got.at[index],
+            device_id=device,
+            device_id_type=MESH,
+        ).start()
+
+    def stream(index, first, last, onward, starting, arrived, leaving, sent, got):
+        offset = 0
+        for k, (number, rows) in enumerate(pieces):
+
+            @pl.when((index >= offset) & (index < offset + number))
+            def _(k=k, rows=rows, offset=offset):
+                part = pl.ds(pl.multiple_of((index - offset) * rows, rows), rows)
+
+                @pl.when(first)
+                def _():
+                    send(own[k].at[part], arrived[k].at[part], sent, got, k, index, onward)
+
+                @pl.when(jnp.logical_not(first))
+                def _():
+                    pltpu.make_async_copy(
+                        arrived[k].at[part], arrived[k].at[part], got.at[index]
+                    ).wait()
+
+                    @pl.when(jnp.logical_not(last))
+                    def _():
+                        leaving[k][part] = jnp.where(starting, own[k][part], arrived[k][part])
+                        send(leaving[k].at[part], arrived[k].at[part], sent, got, k, index, onward)
+
+            offset += number
+
+    def settle(index):
+        offset = 0
+        for k, (number, rows) in enumerate(pieces):
+
+            @pl.when((index >= offset) & (index < offset + number))
+            def _(k=k, rows=rows, offset=offset):
+                part = pl.ds(pl.multiple_of((index - offset) * rows, rows), rows)
+
+                @pl.when(jnp.logical_not(has_below))
+                def _():
+                    out[k][part] = jnp.where(take_down, down_in[k][part], own[k][part])
+
+                @pl.when(jnp.logical_not(has_above))
+                def _():
+                    out[k][part] = jnp.where(take_up, up_in[k][part], own[k][part])
+
+                @pl.when(has_below & has_above)
+                def _():
+                    kept = jnp.where(take_down, down_in[k][part], own[k][part])
+                    out[k][part] = jnp.where(take_up, up_in[k][part], kept)
+
+            offset += number
+
+    def step(t, carry):
+        up_index = t - chip * lag
+        down_index = t - (chips - 1 - chip) * lag
+        stream(
+            up_index, chip == 0, chip == chips - 1, above, start_up, up_in, up_out, up_sent, up_got
+        )
+        stream(
+            down_index,
+            chip == chips - 1,
+            chip == 0,
+            below,
+            start_down,
+            down_in,
+            down_out,
+            down_sent,
+            down_got,
+        )
+        settle(jnp.minimum(up_index, down_index))
+        return carry
+
+    lax.fori_loop(0, total + (chips - 1) * lag, step, 0)
+
+    for k in range(count):
+
+        @pl.when(has_above)
+        def _(k=k):
+            pltpu.make_async_copy(up_in[k], up_in[k], up_sent.at[k]).wait()
+
+        @pl.when(has_below)
+        def _(k=k):
+            pltpu.make_async_copy(down_in[k], down_in[k], down_sent.at[k]).wait()
+
+
+def conveyed(arrays, flags, chips, lag, piece_bytes):
+    pieces = []
+    for array in arrays:
+        row_bytes = array.shape[1] * 2
+        rows = max(16, piece_bytes // row_bytes // 16 * 16)
+        while array.shape[0] % rows:
+            rows -= 16
+        pieces.append((array.shape[0] // rows, rows))
+    total = sum(number for number, _ in pieces)
+    whole = [pltpu.VMEM(array.shape, array.dtype) for array in arrays]
+    moved = sum(array.size * 2 for array in arrays)
+    in_vmem = pl.BlockSpec(memory_space=pltpu.VMEM)
+    return pl.pallas_call(
+        functools.partial(conveyor_kernel, chips, lag, tuple(pieces)),
+        out_shape=[jax.ShapeDtypeStruct(array.shape, array.dtype) for array in arrays],
+        in_specs=[pl.BlockSpec(memory_space=pltpu.SMEM)] + [in_vmem] * len(arrays),
+        out_specs=[in_vmem] * len(arrays),
+        scratch_shapes=whole * 4
+        + [
+            pltpu.SemaphoreType.DMA((len(arrays),)),
+            pltpu.SemaphoreType.DMA((len(arrays),)),
+            pltpu.SemaphoreType.DMA((total,)),
+            pltpu.SemaphoreType.DMA((total,)),
+        ],
+        compiler_params=pltpu.CompilerParams(
+            collective_id=1, has_side_effects=True, vmem_limit_bytes=62 << 20
+        ),
+        cost_estimate=pl.CostEstimate(
+            flops=100 * moved, bytes_accessed=2 * moved, transcendentals=0
+        ),
+    )(flags, *arrays)
+
+
+def migrated(arrays, place, need):
+    chips = place.shape[0]
+    chip = lax.axis_index("expert") // 2
+    flat = [array.reshape(-1, array.shape[-1]) for array in arrays]
+
+    def one_round(this_round):
+        flags = journey_flags(place, chip, this_round)
+        return flags, conveyed(flat, flags, chips, 2, 98304)
+
+    result = tuple(one_round(0)[1])
+    for extra in range(1, chips // 2):
+
+        def further(before, extra=extra):
+            flags, moved = one_round(extra)
+            taken = (flags[2] + flags[3]) > 0
+            return tuple(jnp.where(taken, new, old) for new, old in zip(moved, before))
+
+        result = lax.cond(need > extra, further, lambda before: before, result)
+    return [new.reshape(array.shape) for new, array in zip(result, arrays)]
 
 
 def per_device(
@@ -174,29 +388,18 @@
     pair_count = new_slot.shape[1]
     rows_here = tokens.shape[1]
     top_count = first_ids.shape[2]
-    width = tokens.shape[2]
     usual = rows_here * top_count // pair_count
     capacity = min(rows_here, usual + usual // 8)
     gain_row = norm_gain[0]
-    identity_map = jnp.arange(pair_count, dtype=jnp.int32)
-    new_pairs = new_slot[0]
-    inverse = jnp.sum(
-        jnp.where(new_pairs[:, None] == identity_map[None, :], identity_map[:, None], 0), axis=0
-    )
-    device_ids = jnp.arange(2 * pair_count, dtype=jnp.int32)
-    source = 2 * jnp.repeat(inverse, 2) + device_ids % 2
-    inner_low, outer_low = relocated(*for_sending((inner_weight, outer_weight)), source)
-    inner_full, outer_full = gather_weights(inner_low, outer_low)
-    slots, arrived = pack_rows(tokens[0], gain_row, first_ids[0], new_pairs, capacity)
+    homes = jnp.arange(pair_count, dtype=jnp.int32)
+    need = lax.pmax(jnp.max(crossing_counts(new_slot[0])), "pipe")
+    inner_full, outer_full = gather_weights(inner_weight, outer_weight)
+    slots, arrived = pack_rows(tokens[0], gain_row, first_ids[0], homes, capacity)
     weighting = selection(slots, first_gates[0], pair_count * capacity)
     grad_packed = jnp.dot(
         weighting, cotangent[0].astype(jnp.float32), precision=lax.Precision.HIGHEST
     ).astype(jnp.bfloat16)
     grad_arrived = dispatched(grad_packed, pair_count, capacity)
-    moments = (inner_mean, outer_mean, inner_square, outer_square)
-    moments, inner_low, outer_low = lax.optimization_barrier((moments, inner_low, outer_low))
-    old_mean_in, old_mean_out = relocated(moments[0], moments[1], source)
-    old_square_in, old_square_out = relocated(moments[2], moments[3], source)
     half_out, activity, gate_proj, up_proj = half_forward(arrived, inner_full, outer_full)
     grad_inner, grad_outer = half_backward(
         arrived, grad_arrived, outer_full, activity, gate_proj, up_proj
@@ -212,27 +415,33 @@
     first_out = returned_rows(
         tokens[0], half_out, slots, first_gates[0], pair_count, capacity
     )
-    moved_inner, moved_mean_in, moved_square_in = adam_step(
-        inner_low.astype(jnp.float32), old_mean_in, old_square_in, sum_inner
-    )
-    moved_outer, moved_mean_out, moved_square_out = adam_step(
-        outer_low.astype(jnp.float32), old_mean_out, old_square_out, sum_outer
-    )
-    inner_two, outer_two = gather_weights(moved_inner, moved_outer)
+    new_inner, new_mean_in, new_square_in = adam_step(
+        inner_weight, inner_mean, inner_square, sum_inner
+    )
+    new_outer, new_mean_out, new_square_out = adam_step(
+        outer_weight, outer_mean, outer_square, sum_outer
+    )
+    low_inner, low_outer = for_sending((new_inner, new_outer))
+    inner_two, outer_two = gather_weights(low_inner, low_outer)
     shifted = passed_along(first_out, "pipe", 1)
-    slots_two, arrived_two = pack_rows(shifted, gain_row, second_ids[0], new_pairs, capacity)
+    slots_two, arrived_two = pack_rows(shifted, gain_row, second_ids[0], homes, capacity)
+    moved = migrated(
+        [low_outer, new_mean_out, new_square_out, low_inner, new_mean_in, new_square_in],
+        new_slot[0],
+        need,
+    )
     half_two = half_forward(arrived_two, inner_two, outer_two)[0]
     second_out = returned_rows(
         shifted, half_two, slots_two, second_gates[0], pair_count, capacity
     )
     return (
         second_out[None],
-        moved_inner,
-        moved_outer,
-        moved_mean_in,
-        moved_mean_out,
-        moved_square_in,
-        moved_square_out,
+        moved[3].astype(jnp.float32),
+        moved[0].astype(jnp.float32),
+        moved[4],
+        moved[1],
+        moved[5],
+        moved[2],
     )
 
 

time: 601 us -> 518 us (0.86)
  Pallas kernels: 0 us -> 170 us
  waiting for transfers between devices: 366 us -> 197 us
  starting transfers between devices: 66.3 us -> 26 us
  blocking collectives: 40.2 us -> 4.89 us
  local copies, waits for them, and re-layouts: 28.6 us -> 14.1 us
  between operations: 14.8 us -> 27.7 us
  other arithmetic: 39.1 us -> 32.3 us
    all_to_all x11 -> x0, waiting for transfers between devices: 222 us -> none  [the longest x6 130 us: moved(): lax.all_to_all(parts, 'expert', split_axis=0, concat_axis=0, tiled=True)]
    pallas_call x0 -> x1, Pallas kernels: none -> 170 us  [conveyed(): pl.pallas_call(functools.partial(conveyor_kernel, chips, lag, tuple(piece...]
    all_gather x2, waiting for transfers between devices: 0.01 us -> 43.8 us  [gather_weights(): lax.all_gather(outer_master.astype(jnp.bfloat16), 'dp', axis=3, tiled=True)]
    all_to_all x5, waiting for transfers between devices: 121 us -> 77.5 us  [across_chips(): lax.all_to_all(blocks, 'expert', split_axis=0, concat_axis=0, tiled=True,...]
    all_to_all x11 -> x0, starting transfers between devices: 42.9 us -> none  [the longest x6 24.5 us: moved(): lax.all_to_all(parts, 'expert', split_axis=0, concat_axis=0, tiled=True)]
    all_to_all x1 -> x0, blocking collectives: 40.2 us -> none  [moved(): lax.all_to_all(ordered, 'expert', split_axis=0, concat_axis=0, tiled=True)]
    reduce_scatter x1, waiting for transfers between devices: 0.01 us -> 29.7 us  [per_device(): lax.psum_scatter(grad_inner[None, None].astype(jnp.bfloat16), 'dp', scatt...]
    reduce_scatter x1, waiting for transfers between devices: 0.02 us -> 25.3 us  [per_device(): lax.psum_scatter(grad_outer[None, None].astype(jnp.bfloat16), 'dp', scatt...]
  transfers between devices with their start and end apart: 28 -> 17, of which waited for: 20 -> 11; matrix products, arithmetic and copies ran while one was open for 16% -> 8% of each run, Pallas kernels for 0% -> 33%
where the time goes in v1:
time: 518 us; the launch traced here: 517 us
  waiting for transfers between devices  197 us (38%)
  Pallas kernels  170 us (33%)
  matrix products  44.9 us (9%)
  other arithmetic  32.3 us (6%)
  between operations  27.7 us (5%)
  starting transfers between devices  26 us (5%)
  local copies, waits for them, and re-layouts  14.1 us (3%)
    pallas_call x1, Pallas kernels, conveyed(): pl.pallas_call(functools.partial(conveyor_kernel, chips, lag, tuple(piece...  170 us
    all_to_all x5, waiting for transfers between devices, across_chips(): lax.all_to_all(blocks, 'expert', split_axis=0, concat_axis=0, tiled=True,...  77.5 us
    all_gather x2, waiting for transfers between devices, gather_weights(): lax.all_gather(outer_master.astype(jnp.bfloat16), 'dp', axis=3, tiled=True)  43.8 us
    reduce_scatter x1, waiting for transfers between devices, per_device(): lax.psum_scatter(grad_inner[None, None].astype(jnp.bfloat16), 'dp', scatt...  29.7 us
    reduce_scatter x1, waiting for transfers between devices, per_device(): lax.psum_scatter(grad_outer[None, None].astype(jnp.bfloat16), 'dp', scatt...  25.3 us
    all_to_all x5, starting transfers between devices, across_chips(): lax.all_to_all(blocks, 'expert', split_axis=0, concat_axis=0, tiled=True,...  23.9 us
    ppermute x1, waiting for transfers between devices, passed_along(): return lax.ppermute(block, axis, route)  11.5 us
  transfers between devices with their start and end apart: 17, of which 11 were waited for; matrix products, arithmetic and copies ran while one was open for 8% of the time, Pallas kernels for 33%

profile of v1, /device:TPU:0, one launch (start us, length us, event | category | flops | bytes accessed | tf_op | source)
XLA Modules:
  0.0 517.1 jit_solution(2893758760545914490)
XLA Ops:
  8.3 1.2 fusion.25
  11.5 2.6 convolution_convert_fusion.7
  14.2 6.3 %all-to-all-start = ((bf16[4,72,2048]{2,1,0:T(8,128)(2,1)}), bf16[4,72,2048]{2,1,0:T(8,128)(2,1)S(1)}, u32[]{:S(2)}, u32[]{:S(2)}) async-start(bf16[4,72,2048]{2,1,0:T(8,128)(2,1)} %bitcast.49), calls=%async_computation | async-start | bytes 2359296 | tf_op jit(solution)/shard_map/all_to_all | solution.py:89
  20.5 3.2 convert_element_type.202
  24.4 2.1 convolution_convert_fusion.5
  26.5 22.6 %all-to-all-done = bf16[4,72,2048]{2,1,0:T(8,128)(2,1)S(1)} async-done(((bf16[4,72,2048]{2,1,0:T(8,128)(2,1)}), bf16[4,72,2048]{2,1,0:T(8,128)(2,1)S(1)}, u32[]{:S(2)}, u32[]{:S(2)}) %all-to-all-start) | async-done | bytes 1179680 | tf_op jit(solution)/shard_map/all_to_all | solution.py:89
  49.0 3.5 all-to-all-start.3
  52.7 27.9 %all-to-all-done.3 = bf16[4,72,2048]{2,1,0:T(8,128)(2,1)S(1)} async-done(((bf16[4,72,2048]{2,1,0:T(8,128)(2,1)}), bf16[4,72,2048]{2,1,0:T(8,128)(2,1)S(1)}, u32[]{:S(2)}, u32[]{:S(2)}) %all-to-all-start.3) | async-done | bytes 1179680 | tf_op jit(solution)/shard_map/all_to_all | solution.py:89
  80.7 3.6 fusion.17
  84.3 3.9 multiply_convert_fusion.3
  88.2 4.0 fusion.6
  92.3 25.3 %reduce-scatter.5.cloned.1.call-done = bf16[1,1,384,1024]{3,2,1,0:T(8,128)(2,1)} async-done(((bf16[1,1,384,2048]{3,2,1,0:T(8,128)(2,1)}), bf16[1,1,384,1024]{3,2,1,0:T(8,128)(2,1)}) %reduce-scatter.5.cloned.1.call-update) | async-done | bytes 786448 | tf_op jit(solution)/shard_map/reduce_scatter | solution.py:411
  117.7 2.2 fusion.11
  119.9 2.0 fusion.88
  122.2 27.1 %all-gather.7.cloned.1.call-done = bf16[1,1,384,2048]{3,2,1,0:T(8,128)(2,1)} async-done(((bf16[1,1,384,1024]{3,2,1,0:T(8,128)(2,1)}), bf16[1,1,384,2048]{3,2,1,0:T(8,128)(2,1)}) %all-gather.7.cloned.1.call-update) | async-done | bytes 1572880 | tf_op jit(solution)/shard_map/all_gather | solution.py:108
  149.3 3.5 fusion.19
  152.9 3.4 fusion.5
  156.3 3.1 fusion.4
  159.4 2.0 pad_maximum_fusion
  161.5 1.4 copy-done.38
  162.9 1.4 convolution_convert_fusion.1
  164.5 2.8 collective-permute-done.1
  167.3 1.5 add_convert_fusion.2
  168.8 4.7 all-to-all-start.1
  175.4 29.7 %reduce-scatter.3.cloned.1.call-done = bf16[1,1,2,1024,384]{4,3,2,1,0:T(8,128)(2,1)} async-done(((bf16[1,1,2,2048,384]{4,3,2,1,0:T(8,128)(2,1)}), bf16[1,1,2,1024,384]{4,3,2,1,0:T(8,128)(2,1)}) %reduce-scatter.3.cloned.1.call-update) | async-done | bytes 1572880 | tf_op jit(solution)/shard_map/reduce_scatter | solution.py:408
  205.0 3.7 fusion.1
  208.8 2.8 subtract_convert_fusion
  212.7 2.3 fusion.7
  215.0 1.6 collective-permute-start.2
  217.1 11.5 %collective-permute-done.2 = bf16[128,2048]{1,0:T(8,128)(2,1)S(1)} collective-permute-done((bf16[128,2048]{1,0:T(8,128)(2,1)S(1)}, bf16[128,2048]{1,0:T(8,128)(2,1)S(1)}, u32[]{:S(2)}, u32[]{:S(2)}) %collective-permute-start.2) | collective-permute-done | bytes 524320 | tf_op jit(solution)/shard_map/ppermute | solution.py:32
  228.8 1.6 convolution_convert_fusion.6
  230.3 4.6 all-to-all-start.2
  235.5 27.0 %all-to-all-done.2 = bf16[4,72,2048]{2,1,0:T(8,128)(2,1)S(1)} async-done(((bf16[4,72,2048]{2,1,0:T(8,128)(2,1)}), bf16[4,72,2048]{2,1,0:T(8,128)(2,1)S(1)}, u32[]{:S(2)}, u32[]{:S(2)}) %all-to-all-start.2) | async-done | bytes 1179680 | tf_op jit(solution)/shard_map/all_to_all | solution.py:89
  262.5 2.8 collective-permute-done.3
  265.3 3.8 fusion.14
  269.2 16.8 %all-gather.11.cloned.1.call-done = bf16[1,1,384,2048]{3,2,1,0:T(8,128)(2,1)} async-done(((bf16[1,1,384,1024]{3,2,1,0:T(8,128)(2,1)}), bf16[1,1,384,2048]{3,2,1,0:T(8,128)(2,1)}) %all-gather.11.cloned.1.call-update) | async-done | bytes 1572880 | tf_op jit(solution)/shard_map/all_gather | solution.py:108
  285.9 6.2 %convolution_convert_fusion = bf16[576,2048]{1,0:T(8,128)(2,1)} fusion(bf16[1,1,384,2048]{3,2,1,0:T(8,128)(2,1)} %all-gather.11.cloned.1.call-done, f32[576,384]{1,0:T(8,128)} %fusion.14, bf16[1,1,2,2048,384]{4,3,2,1,0:T(8,128)(2,1)} %all-gather.9.cloned.1.call-done, bf16[288,2048]{1,0:T(8,128)(2,1)S(1)} %collective-permute-done.3, ...), kind=kOutput, calls=%fused_computation.25 | convolution fusion | flops 1819164672 | bytes 8749056 | tf_op jit(solution)/shard_map/dot_general | solution.py:50
  292.1 1.5 slice.149
  293.8 2.8 collective-permute-done.5
  296.6 1.5 add_convert_fusion.1
  298.1 4.7 all-to-all-start.4
  303.7 4.9 pmax.7
  323.2 3.0 add_convert_fusion.7.flags
  326.2 170.3 %shard_map.189 = (bf16[384,1024]{1,0:T(8,128)(2,1)}, bf16[384,1024]{1,0:T(8,128)(2,1)}, bf16[384,1024]{1,0:T(8,128)(2,1)}, bf16[2048,384]{1,0:T(8,128)(2,1)}, bf...) custom-call(s32[4]{0:T(128)} %add_convert_fusion.7.flags, bf16[384,1024]{1,0:T(8,128)(2,1)} %bitcast.200, ...), custom_call_target="tpu_custom_call" | custom-call | flops 707788800 | bytes 14155776 | tf_op jit(solution)/shard_map/pallas_call | solution.py:330
  496.6 4.5 conditional.1
  496.6 2.6 bitcast_convert_fusion
  499.1 1.9 convert.14
  501.0 3.3 fusion.9
  (131 shorter events, 16.9 us)
Async XLA Ops:
  7.2 17.2 %copy-start = (bf16[1,128,2048]{2,1,0:T(8,128)(2,1)S(1)}, bf16[1,128,2048]{2,1,0:T(8,128)(2,1)}, u32[]{:S(2)}) copy-start(bf16[1,128,2048]{2,1,0:T(8,128)(2,1)} %param.17) | copy-start | bytes 1572868
  14.2 34.9 %all-to-all-start = ((bf16[4,72,2048]{2,1,0:T(8,128)(2,1)}), bf16[4,72,2048]{2,1,0:T(8,128)(2,1)S(1)}, u32[]{:S(2)}, u32[]{:S(2)}) async-start(bf16[4,72,2048]{2,1,0:T(8,128)(2,1)} %bitcast.49), calls=%async_computation | async-start | bytes 2359296 | tf_op jit(solution)/shard_map/all_to_all | solution.py:89
  20.5 60.2 %all-gather.5.cloned.1.call-start = ((), (), s32[]{:S(2)}) async-start(), calls=%async_computation.7 | async-start | bytes 4718592 | tf_op jit(solution)/shard_map/all_gather | solution.py:107
  49.0 35.2 %copy-start.25 = (bf16[4,72,2048]{2,1,0:T(8,128)(2,1)}, bf16[4,72,2048]{2,1,0:T(8,128)(2,1)S(1)}, u32[]{:S(2)}) copy-start(bf16[4,72,2048]{2,1,0:T(8,128)(2,1)S(1)} %all-to-all-done) | copy-start | bytes 3538948
  49.0 31.6 %all-to-all-start.3 = ((bf16[4,72,2048]{2,1,0:T(8,128)(2,1)}), bf16[4,72,2048]{2,1,0:T(8,128)(2,1)S(1)}, u32[]{:S(2)}, u32[]{:S(2)}) async-start(bf16[4,72,2048]{2,1,0:T(8,128)(2,1)} %bitcast.64), calls=%async_computation.3 | async-start | bytes 2359296 | tf_op jit(solution)/shard_map/all_to_all | solution.py:89
  52.6 65.1 %reduce-scatter.5.cloned.1.call-start = ((), (), s32[]{:S(2)}) async-start(), calls=%async_computation.11 | async-start | bytes 2359296 | tf_op jit(solution)/shard_map/reduce_scatter | solution.py:411
  52.6 28.0 %collective-permute-start = (bf16[288,2048]{1,0:T(8,128)(2,1)S(1)}, bf16[288,2048]{1,0:T(8,128)(2,1)}, u32[]{:S(2)}, u32[]{:S(2)}) collective-permute-start(bf16[288,2048]{1,0:T(8,128)(2,1)S(1)} %bitcast.214), channel_id=1, source_target_pairs={{0,2},{2,0},{4,6},{6,4},{8,10},{10,8},{12,14},{14,12},{1,3},{3,1},... | collective-permute-start | bytes 3538952 | tf_op jit(solution)/shard_map/ppermute | solution.py:96
  80.6 7.6 %copy-start.27 = (bf16[4,72,2048]{2,1,0:T(8,128)(2,1)}, bf16[4,72,2048]{2,1,0:T(8,128)(2,1)S(1)}, u32[]{:S(2)}) copy-start(bf16[4,72,2048]{2,1,0:T(8,128)(2,1)S(1)} %all-to-all-done.3) | copy-start | bytes 3538948
  80.6 7.6 %collective-permute-start.4 = (bf16[288,2048]{1,0:T(8,128)(2,1)S(1)}, bf16[288,2048]{1,0:T(8,128)(2,1)}, u32[]{:S(2)}, u32[]{:S(2)}) collective-permute-start(bf16[288,2048]{1,0:T(8,128)(2,1)S(1)} %bitcast.219), channel_id=1, source_target_pairs={{0,2},{2,0},{4,6},{6,4},{8,10},{10,8},{12,14},{14,12},{1,3},{3,1},... | collective-permute-start | bytes 3538952 | tf_op jit(solution)/shard_map/ppermute | solution.py:96
  80.7 3.6 copy-start.37
  84.3 3.9 copy-start.41
  88.2 4.0 copy-start.39
  92.3 27.7 %copy-start.24 = (f32[1,1,384,1024]{3,2,1,0:T(8,128)S(1)}, f32[1,1,384,1024]{3,2,1,0:T(8,128)}, u32[]{:S(2)}) copy-start(f32[1,1,384,1024]{3,2,1,0:T(8,128)} %param.25) | copy-start | bytes 4718596
  92.3 57.0 %all-gather.7.cloned.1.call-start = ((), (), s32[]{:S(2)}) async-start(), calls=%async_computation.8 | async-start | bytes 2359296 | tf_op jit(solution)/shard_map/all_gather | solution.py:108
  119.9 2.1 copy-start.5
  119.9 2.1 copy-start.6
  122.0 30.9 %copy-start.26 = (bf16[4,72,2048]{2,1,0:T(8,128)(2,1)S(1)}, bf16[4,72,2048]{2,1,0:T(8,128)(2,1)}, u32[]{:S(2)}) copy-start(bf16[4,72,2048]{2,1,0:T(8,128)(2,1)} %copy-done.25) | copy-start | bytes 3538948
  122.0 83.0 %reduce-scatter.3.cloned.1.call-start = ((), (), s32[]{:S(2)}) async-start(), calls=%async_computation.9 | async-start | bytes 4718592 | tf_op jit(solution)/shard_map/reduce_scatter | solution.py:408
  152.9 3.4 copy-start.42
  152.9 3.4 copy-start.43
  161.4 1.4 copy-start.38
  161.4 1.5 copy-start.40
  164.4 2.9 collective-permute-start.1
  168.8 4.7 copy-start.34
  168.8 42.9 %all-to-all-start.1 = ((bf16[4,72,2048]{2,1,0:T(8,128)(2,1)}), bf16[4,72,2048]{2,1,0:T(8,128)(2,1)}, u32[]{:S(2)}, u32[]{:S(2)}) async-start(bf16[4,72,2048]{2,1,0:T(8,128)(2,1)} %bitcast.54), calls=%async_computation.1 | async-start | bytes 2359296 | tf_op jit(solution)/shard_map/all_to_all | solution.py:89
  173.5 91.8 %all-gather.9.cloned.1.call-start = ((), (), s32[]{:S(2)}) async-start(), calls=%async_computation.10 | async-start | bytes 4718592 | tf_op jit(solution)/shard_map/all_gather | solution.py:107
  205.0 3.7 copy-start.7
  208.7 2.9 copy-start.4
  208.7 2.9 copy-start.3
  211.6 1.0 copy-start.13
  211.7 17.1 %copy-start.32 = (f32[1,2048]{1,0:T(1,128)S(1)}, f32[1,2048]{1,0:T(1,128)}, u32[]{:S(2)}) copy-start(f32[1,2048]{1,0:T(1,128)} %param.18) | copy-start | bytes 24580
  215.0 13.6 %collective-permute-start.2 = (bf16[128,2048]{1,0:T(8,128)(2,1)S(1)}, bf16[128,2048]{1,0:T(8,128)(2,1)S(1)}, u32[]{:S(2)}, u32[]{:S(2)}) collective-permute-start(bf16[128,2048]{1,0:T(8,128)(2,1)S(1)} %fusion.7), channel_id=1, source_target_pairs={{16,0},{0,16},{17,1},{1,17},{18,2},{2,18},{19,3},{3,19},{20,4},{4,... | collective-permute-start | bytes 1572872 | tf_op jit(solution)/shard_map/ppermute | solution.py:32
  228.6 1.8 copy-start.14
  230.3 32.1 %all-to-all-start.2 = ((bf16[4,72,2048]{2,1,0:T(8,128)(2,1)}), bf16[4,72,2048]{2,1,0:T(8,128)(2,1)S(1)}, u32[]{:S(2)}, u32[]{:S(2)}) async-start(bf16[4,72,2048]{2,1,0:T(8,128)(2,1)} %bitcast.61), calls=%async_computation.2 | async-start | bytes 2359296 | tf_op jit(solution)/shard_map/all_to_all | solution.py:89
  234.9 51.0 %all-gather.11.cloned.1.call-start = ((), (), s32[]{:S(2)}) async-start(), calls=%async_computation.12 | async-start | bytes 2359296 | tf_op jit(solution)/shard_map/all_gather | solution.py:108
  262.5 2.8 collective-permute-start.3
  292.1 4.5 copy-start.22
  293.7 2.9 collective-permute-start.5
  298.1 4.7 copy-start.31
  298.1 28.1 %copy-start.36 = (f32[1,128,2]{1,2,0:T(2,128)S(1)}, f32[1,128,2]{1,2,0:T(2,128)}, u32[]{:S(2)}) copy-start(f32[1,128,2]{1,2,0:T(2,128)} %param.22) | copy-start | bytes 3076
  298.1 28.1 %copy-start.2 = (bf16[1,1,2,1024,384]{4,3,2,1,0:T(8,128)(2,1)S(1)}, bf16[1,1,2,1024,384]{4,3,2,1,0:T(8,128)(2,1)}, u32[]{:S(2)}) copy-start(bf16[1,1,2,1024,384]{4,3,2,1,0:T(8,128)(2,1)} %subtract_convert_fusion) | copy-start | bytes 4718596
  298.1 202.9 %all-to-all-start.4 = ((bf16[4,72,2048]{2,1,0:T(8,128)(2,1)}), bf16[4,72,2048]{2,1,0:T(8,128)(2,1)}, u32[]{:S(2)}, u32[]{:S(2)}) async-start(bf16[4,72,2048]{2,1,0:T(8,128)(2,1)} %bitcast.72), calls=%async_computation.6 | async-start | bytes 2359296 | tf_op jit(solution)/shard_map/all_to_all | solution.py:89
  496.6 2.6 copy-start.8
  501.0 3.4 copy-start.11
  504.4 1.7 copy-start.17
  506.0 1.7 copy-start.12
  507.7 1.7 copy-start.20
  507.7 2.6 copy-start.1
  (1 other events, 0.7 us)
Sparse Core Ops, SparseCore 0:
  23.9 46.3 all-gather.4
  92.4 25.2 reduce-scatter.4
  122.1 27.1 all-gather.6
  161.6 43.3 reduce-scatter.2
  211.8 44.9 all-gather.8
  258.7 27.1 all-gather.10

commit v2 on v1

v2 whole, which is shorter than its diff:
```python
import functools

import jax
import jax.numpy as jnp
from jax import lax
from jax.experimental import pallas as pl
from jax.experimental.pallas import tpu as pltpu
from jax.sharding import PartitionSpec as P


MESH = pl.DeviceIdType.MESH

norm_eps = 1e-06
learn_rate = 0.001
beta_one = 0.9
beta_two = 0.95
adam_eps = 1e-08
bias_one = 0.999973438601112
bias_two = 0.994079470779667


def for_sending(array):

    def short(part):
        return part.astype(jnp.bfloat16) if part.dtype == jnp.float32 else part

    return jax.tree.map(short, array)


def passed_along(block, axis, distance):
    devices = range(lax.axis_size(axis))
    route = [((i - distance) % len(devices), i) for i in devices]
    return lax.ppermute(block, axis, route)


def normed(values, gain_row):
    widened = values.astype(jnp.float32)
    inverse_rms = lax.rsqrt(jnp.mean(widened * widened, axis=-1, keepdims=True) + norm_eps)
    return (widened * inverse_rms * gain_row).astype(jnp.bfloat16)


def silu_parts(gate_proj):
    logistic = jax.nn.sigmoid(gate_proj)
    return (gate_proj * logistic, logistic * (1.0 + gate_proj * (1.0 - logistic)))


def columns(rows, part, parts):
    width = rows.shape[-1] // parts
    return rows[..., part * width : (part + 1) * width]


def half_forward(token_rows, inner_parts, outer_parts):
    count = len(inner_parts)

    def projected(which):
        return sum(
            jnp.dot(
                columns(token_rows, part, count),
                inner_parts[part][which],
                preferred_element_type=jnp.float32,
            )
            for part in range(count)
        )

    gate_proj, up_proj = projected(0), projected(1)
    activity = (silu_parts(gate_proj)[0] * up_proj).astype(jnp.bfloat16)
    half_out = [
        jnp.dot(activity, outer, preferred_element_type=jnp.float32).astype(jnp.bfloat16)
        for outer in outer_parts
    ]
    return (jnp.concatenate(half_out, axis=-1), activity, gate_proj, up_proj)


def half_backward(token_rows, grad_rows, outer_parts, activity, gate_proj, up_proj):
    count = len(outer_parts)

    def outer_part(part):
        return jnp.dot(
            activity.T, columns(grad_rows, part, count), preferred_element_type=jnp.float32
        ).astype(jnp.bfloat16)

    grad_outer = [outer_part(part) for part in range(count)]
    d_active = sum(
        jnp.dot(
            columns(grad_rows, part, count),
            outer_parts[part].T,
            preferred_element_type=jnp.float32,
        )
        for part in range(count)
    )
    swish_value, swish_slope = silu_parts(gate_proj)
    d_gate = (d_active * up_proj * swish_slope).astype(jnp.bfloat16)
    d_upper = (d_active * swish_value).astype(jnp.bfloat16)

    def inner_part(part):
        rows = columns(token_rows, part, count).T
        return jnp.stack(
            [
                jnp.dot(rows, d_gate, preferred_element_type=jnp.float32).astype(jnp.bfloat16),
                jnp.dot(rows, d_upper, preferred_element_type=jnp.float32).astype(jnp.bfloat16),
            ]
        )

    return ([inner_part(part) for part in range(count)], grad_outer)


def slot_index(ids, target, capacity):
    count, tokens = target.shape[0], ids.shape[0]
    experts = jnp.arange(count, dtype=jnp.int32)[None, :, None]
    chosen = (ids.T[:, None, :] == experts).astype(jnp.bfloat16)
    places = jnp.arange(tokens, dtype=jnp.int32)
    earlier = (places[:, None] < places[None, :]).astype(jnp.bfloat16)
    ranks = jnp.dot(
        chosen.reshape(-1, tokens), earlier, preferred_element_type=jnp.float32
    ).reshape(chosen.shape)
    chosen = chosen.astype(jnp.float32)
    totals = jnp.sum(chosen, axis=2, keepdims=True)
    before = jnp.cumsum(totals, axis=0) - totals
    starts = (target * capacity).astype(jnp.float32)[None, :, None]
    return jnp.sum(chosen * (starts + before + ranks), axis=1).astype(jnp.int32)


def selection(slots, values, total_slots):
    positions = jnp.arange(total_slots, dtype=jnp.int32)
    result = jnp.zeros((total_slots, slots.shape[1]), jnp.float32)
    for choice in range(slots.shape[0]):
        result = result + jnp.where(
            slots[choice][None, :] == positions[:, None], values[choice][None, :], 0.0
        )
    return result


def across_chips(blocks):
    devices = lax.axis_size("expert")
    arrived = [blocks[0]]
    for distance in range(1, len(blocks)):
        route = [(i, (i + 2 * distance) % devices) for i in range(devices)]
        arrived.append(lax.ppermute(blocks[distance], "expert", route))
    return arrived


def back_across_chips(blocks):
    devices = lax.axis_size("expert")
    arrived = [blocks[0]]
    for distance in range(1, len(blocks)):
        route = [(i, (i - 2 * distance) % devices) for i in range(devices)]
        arrived.append(lax.ppermute(blocks[distance], "expert", route))
    return arrived


def to_partner(block):
    devices = range(lax.axis_size("expert"))
    return lax.ppermute(block, "expert", [(i, i ^ 1) for i in devices])


def blocks_of(rows, count):
    size = rows.shape[0] // count
    return [rows[k * size : (k + 1) * size] for k in range(count)]


def dispatched(packed, pair_count):
    own = jnp.concatenate(across_chips(blocks_of(packed, pair_count)), axis=0)
    return jnp.concatenate([own, to_partner(own)], axis=0)


def from_ahead(block, axis, distance):
    return passed_along(block, axis, lax.axis_size(axis) - distance)


def turned(rows, back=False):
    share = rows.shape[-1] // lax.axis_size("dp")
    own = lax.axis_index("dp") * share
    return jnp.roll(rows, own if back else -own, axis=-1)


def gathered_parts(block):
    return [block] + [
        from_ahead(block, "dp", distance) for distance in range(1, lax.axis_size("dp"))
    ]


def summed_own(parts):
    total = parts[0].astype(jnp.float32)
    for distance in range(1, len(parts)):
        total = total + passed_along(parts[distance], "dp", distance).astype(jnp.float32)
    return total


def pack_rows(normal, slots, rows):
    picker = selection(slots, jnp.ones(slots.shape, jnp.float32), rows).astype(jnp.bfloat16)
    packed = jnp.dot(picker, normal, preferred_element_type=jnp.float32)
    return packed


def returned_rows(token_rows, half_out, slots, gates, pair_count):
    rows = half_out.shape[0] // 2
    other = to_partner(half_out[rows:])
    summed = (half_out[:rows].astype(jnp.float32) + other.astype(jnp.float32)).astype(jnp.bfloat16)
    back = jnp.concatenate(back_across_chips(blocks_of(summed, pair_count)), axis=0)
    weighting = selection(slots, gates, rows)
    high = weighting.astype(jnp.bfloat16)
    rest = (weighting - high.astype(jnp.float32)).astype(jnp.bfloat16)

    def weighted(share):
        return lax.dot_general(
            share, back, (((0,), (0,)), ((), ())), preferred_element_type=jnp.float32
        )

    mixed = weighted(high) + weighted(rest)
    return (token_rows.astype(jnp.float32) + mixed).astype(jnp.bfloat16)


def adam_step(weight, mean, square, grads):
    mean_new = (beta_one * mean.astype(jnp.float32) + (1.0 - beta_one) * grads).astype(jnp.bfloat16)
    square_new = (beta_two * square.astype(jnp.float32) + (1.0 - beta_two) * grads * grads).astype(
        jnp.bfloat16
    )
    mean_wide = lax.optimization_barrier(mean_new).astype(jnp.float32)
    square_wide = lax.optimization_barrier(square_new).astype(jnp.float32)
    update = mean_wide / bias_one / (jnp.sqrt(square_wide / bias_two) + adam_eps)
    return (weight - learn_rate * update, mean_new, square_new)


def crossing_counts(place):
    count = place.shape[-1]
    own = jnp.arange(count, dtype=jnp.int32)
    link = own[:-1, None]
    crosses = (own[None, :] <= link) & (place[..., None, :] > link)
    return jnp.sum(crosses.astype(jnp.int32), axis=-1)


def journey_flags(places, chip, this_round):
    count = len(places)

    def coloured(order, upward):
        moves = [(places[i] > i) if upward else (places[i] < i) for i in range(count)]
        rounds = [None] * count
        for position, item in enumerate(order):
            chosen = jnp.int32(0)
            for r in reversed(range(count // 2)):
                busy = jnp.bool_(False)
                for before in order[:position]:
                    passes = (places[before] > item) if upward else (places[before] < item)
                    busy = busy | (moves[before] & passes & (rounds[before] == r))
                chosen = jnp.where(busy, chosen, r)
            rounds[item] = chosen
        active = [moves[i] & (rounds[i] == this_round) for i in range(count)]
        starts, ends = jnp.bool_(False), jnp.bool_(False)
        for i in range(count):
            starts = starts | (active[i] & (chip == i))
            ends = ends | (active[i] & (places[i] == chip))
        return starts, ends

    start_up, take_up = coloured(list(range(count)), True)
    start_down, take_down = coloured(list(reversed(range(count))), False)
    return start_up, start_down, take_up, take_down


def conveyor_kernel(chips, lag, pieces, this_round, places, *refs):
    count = len(pieces)
    own = refs[:count]
    out = refs[count : 2 * count]
    up_in = refs[2 * count : 3 * count]
    down_in = refs[3 * count : 4 * count]
    up_out = refs[4 * count : 5 * count]
    down_out = refs[5 * count : 6 * count]
    up_sent, down_sent, up_got, down_got = refs[6 * count :]
    place = lax.axis_index("expert")
    chip = place // 2
    above, below = {"expert": place + 2}, {"expert": place - 2}
    has_above, has_below = chip < chips - 1, chip > 0

    barrier = pltpu.get_barrier_semaphore()

    @pl.when(has_above)
    def _():
        pl.semaphore_signal(barrier, inc=1, device_id=above, device_id_type=MESH)

    @pl.when(has_below)
    def _():
        pl.semaphore_signal(barrier, inc=1, device_id=below, device_id_type=MESH)

    pl.semaphore_wait(barrier, has_above.astype(jnp.int32) + has_below.astype(jnp.int32))

    start_up, start_down, take_up, take_down = journey_flags(
        [places[i] for i in range(chips)], chip, this_round
    )
    total = sum(number for number, _ in pieces)

    def send(source, target, sent, got, k, index, device):
        pltpu.make_async_remote_copy(
            src_ref=source,
            dst_ref=target,
            send_sem=sent.at[k],
            recv_sem=got.at[index],
            device_id=device,
            device_id_type=MESH,
        ).start()

    def stream(index, first, last, onward, starting, arrived, leaving, sent, got):
        offset = 0
        for k, (number, rows) in enumerate(pieces):

            @pl.when((index >= offset) & (index < offset + number))
            def _(k=k, rows=rows, offset=offset):
                part = pl.ds(pl.multiple_of((index - offset) * rows, rows), rows)

                @pl.when(first)
                def _():
                    send(own[k].at[part], arrived[k].at[part], sent, got, k, index, onward)

                @pl.when(jnp.logical_not(first))
                def _():
                    pltpu.make_async_copy(
                        arrived[k].at[part], arrived[k].at[part], got.at[index]
                    ).wait()

                    @pl.when(jnp.logical_not(last))
                    def _():
                        leaving[k][part] = jnp.where(starting, own[k][part], arrived[k][part])
                        send(leaving[k].at[part], arrived[k].at[part], sent, got, k, index, onward)

            offset += number

    def settle(index):
        offset = 0
        for k, (number, rows) in enumerate(pieces):

            @pl.when((index >= offset) & (index < offset + number))
            def _(k=k, rows=rows, offset=offset):
                part = pl.ds(pl.multiple_of((index - offset) * rows, rows), rows)

                @pl.when(jnp.logical_not(has_below))
                def _():
                    out[k][part] = jnp.where(take_down, down_in[k][part], own[k][part])

                @pl.when(jnp.logical_not(has_above))
                def _():
                    out[k][part] = jnp.where(take_up, up_in[k][part], own[k][part])

                @pl.when(has_below & has_above)
                def _():
                    kept = jnp.where(take_down, down_in[k][part], own[k][part])
                    out[k][part] = jnp.where(take_up, up_in[k][part], kept)

            offset += number

    def step(t, carry):
        up_index = t - chip * lag
        down_index = t - (chips - 1 - chip) * lag
        stream(
            up_index, chip == 0, chip == chips - 1, above, start_up, up_in, up_out, up_sent, up_got
        )
        stream(
            down_index,
            chip == chips - 1,
            chip == 0,
            below,
            start_down,
            down_in,
            down_out,
            down_sent,
            down_got,
        )
        settle(jnp.minimum(up_index, down_index))
        return carry

    lax.fori_loop(0, total + (chips - 1) * lag, step, 0)

    for k in range(count):

        @pl.when(has_above)
        def _(k=k):
            pltpu.make_async_copy(up_in[k], up_in[k], up_sent.at[k]).wait()

        @pl.when(has_below)
        def _(k=k):
            pltpu.make_async_copy(down_in[k], down_in[k], down_sent.at[k]).wait()


def conveyed(arrays, place, this_round, lag, piece_bytes):
    chips = place.shape[0]
    pieces = []
    for array in arrays:
        row_bytes = array.shape[1] * 2
        rows = max(16, piece_bytes // row_bytes // 16 * 16)
        while array.shape[0] % rows:
            rows -= 16
        pieces.append((array.shape[0] // rows, rows))
    total = sum(number for number, _ in pieces)
    whole = [pltpu.VMEM(array.shape, array.dtype) for array in arrays]
    moved = sum(array.size * 2 for array in arrays)
    in_vmem = pl.BlockSpec(memory_space=pltpu.VMEM)
    return pl.pallas_call(
        functools.partial(conveyor_kernel, chips, lag, tuple(pieces), this_round),
        out_shape=[jax.ShapeDtypeStruct(array.shape, array.dtype) for array in arrays],
        in_specs=[pl.BlockSpec(memory_space=pltpu.SMEM)] + [in_vmem] * len(arrays),
        out_specs=[in_vmem] * len(arrays),
        scratch_shapes=whole * 4
        + [
            pltpu.SemaphoreType.DMA((len(arrays),)),
            pltpu.SemaphoreType.DMA((len(arrays),)),
            pltpu.SemaphoreType.DMA((total,)),
            pltpu.SemaphoreType.DMA((total,)),
        ],
        compiler_params=pltpu.CompilerParams(
            collective_id=1 + this_round, has_side_effects=True, vmem_limit_bytes=62 << 20
        ),
        cost_estimate=pl.CostEstimate(
            flops=100 * moved, bytes_accessed=2 * moved, transcendentals=0
        ),
    )(place, *arrays)


def first_journey(arrays, place):
    flat = [array.reshape(-1, array.shape[-1]) for array in arrays]
    return flat, tuple(conveyed(flat, place, 0, 2, 98304))


def further_journeys(flat, result, place, need):
    chips = place.shape[0]
    chip = lax.axis_index("expert") // 2

    def rounds_from(this_round, before):
        if this_round == chips // 2:
            return before

        def further(before):
            _, _, take_up, take_down = journey_flags(
                [place[i] for i in range(chips)], chip, this_round
            )
            moved = conveyed(flat, place, this_round, 2, 98304)
            merged = tuple(
                jnp.where(take_up | take_down, new, old) for new, old in zip(moved, before)
            )
            return rounds_from(this_round + 1, merged)

        return lax.cond(need > this_round, further, lambda before: before, before)

    return rounds_from(1, result)


def whole_step(
    tokens,
    cotangent,
    norm_gain,
    first_ids,
    first_gates,
    second_ids,
    second_gates,
    new_slot,
    inner_weight,
    outer_weight,
    inner_mean,
    outer_mean,
    inner_square,
    outer_square,
):
    pair_count = new_slot.shape[1]
    rows_here = tokens.shape[1]
    top_count = first_ids.shape[2]
    usual = rows_here * top_count // pair_count
    capacity = min(rows_here, usual + usual // 8)
    rows = pair_count * capacity
    chip = lax.axis_index("expert") // 2
    ahead = (jnp.arange(pair_count, dtype=jnp.int32) - chip) % pair_count
    need = jnp.max(crossing_counts(new_slot[0]))
    for distance in range(1, lax.axis_size("pipe")):
        need = jnp.maximum(
            need, jnp.max(crossing_counts(passed_along(new_slot, "pipe", distance)[0]))
        )
    inner_parts = gathered_parts(inner_weight[0, 0].astype(jnp.bfloat16))
    outer_parts = gathered_parts(outer_weight[0, 0].astype(jnp.bfloat16))
    gain_row = turned(norm_gain[0])
    token_rows = turned(tokens[0])
    slots = slot_index(first_ids[0], ahead, capacity)
    packed = pack_rows(normed(token_rows, gain_row), slots, rows).astype(jnp.bfloat16)
    arrived = dispatched(packed, pair_count)
    gates = first_gates[0].T
    slot_gates = jnp.sum(selection(slots, gates, rows), axis=1, keepdims=True)
    grad_packed = (pack_rows(turned(cotangent[0]), slots, rows) * slot_gates).astype(jnp.bfloat16)
    grad_arrived = dispatched(grad_packed, pair_count)
    half_out, *kept = half_forward(arrived, inner_parts, outer_parts)
    activity, gate_proj, up_proj = lax.optimization_barrier(kept)
    grad_inner, grad_outer = half_backward(
        arrived, grad_arrived, outer_parts, activity, gate_proj, up_proj
    )
    sum_inner = summed_own(grad_inner)
    sum_outer = summed_own(grad_outer)
    first_out = returned_rows(token_rows, half_out, slots, gates, pair_count)
    shifted = passed_along(first_out, "pipe", 1)
    new_inner, new_mean_in, new_square_in = adam_step(
        inner_weight[0, 0], inner_mean[0, 0], inner_square[0, 0], sum_inner
    )
    new_outer, new_mean_out, new_square_out = adam_step(
        outer_weight[0, 0], outer_mean[0, 0], outer_square[0, 0], sum_outer
    )
    low_inner, low_outer = for_sending((new_inner, new_outer))
    inner_two, outer_two = gathered_parts(low_inner), gathered_parts(low_outer)
    slots_two = slot_index(second_ids[0], ahead, capacity)
    packed_two = pack_rows(normed(shifted, gain_row), slots_two, rows).astype(jnp.bfloat16)
    stepped = (low_outer, new_mean_out, new_square_out, low_inner, new_mean_in, new_square_in)
    packed_two, need = lax.optimization_barrier((packed_two, need))
    arrived_two = dispatched(packed_two, pair_count)
    stepped, arrived_two = lax.optimization_barrier((stepped, arrived_two))
    flat, moved = first_journey(stepped, new_slot[0])
    moved, arrived_two, inner_two, outer_two = lax.optimization_barrier(
        (moved, arrived_two, inner_two, outer_two)
    )
    half_two = half_forward(arrived_two, inner_two, outer_two)[0]
    second_out = turned(
        returned_rows(shifted, half_two, slots_two, second_gates[0].T, pair_count),
        back=True,
    )
    moved = further_journeys(flat, moved, new_slot[0], need)
    moved = [
        jnp.where(need < 0, 0.0, array.astype(jnp.float32)).astype(
            jnp.bfloat16 if position % 3 else jnp.float32
        )
        for position, array in enumerate(moved)
    ]
    outer_shape, inner_shape = outer_weight.shape, inner_weight.shape
    return (
        second_out[None],
        moved[3].reshape(inner_shape),
        moved[0].reshape(outer_shape),
        moved[4].reshape(inner_shape),
        moved[1].reshape(outer_shape),
        moved[5].reshape(inner_shape),
        moved[2].reshape(outer_shape),
    )


def solution(mesh):
    return jax.shard_map(
        whole_step,
        mesh=mesh,
        in_specs=(
            P("pipe", ("expert", "dp"), None),
            P("pipe", ("expert", "dp"), None),
            P("pipe", None),
            P("pipe", ("expert", "dp"), None),
            P("pipe", ("expert", "dp"), None),
            P("pipe", ("expert", "dp"), None),
            P("pipe", ("expert", "dp"), None),
            P("pipe", None),
            P("pipe", "expert", None, "dp", None),
            P("pipe", "expert", None, "dp"),
            P("pipe", "expert", None, "dp", None),
            P("pipe", "expert", None, "dp"),
            P("pipe", "expert", None, "dp", None),
            P("pipe", "expert", None, "dp"),
        ),
        out_specs=(
            P("pipe", ("expert", "dp"), None),
            P("pipe", "expert", None, "dp", None),
            P("pipe", "expert", None, "dp"),
            P("pipe", "expert", None, "dp", None),
            P("pipe", "expert", None, "dp"),
            P("pipe", "expert", None, "dp", None),
            P("pipe", "expert", None, "dp"),
        ),
        check_vma=False,
    )
```

time: 518 us -> 409 us (0.79)
  waiting for transfers between devices: 197 us -> 106 us
  between operations: 27.7 us -> 2.74 us
  matrix products: 44.9 us -> 29 us
  starting transfers between devices: 26 us -> 39.1 us
  Pallas kernels: 170 us -> 176 us
    all_to_all x5 -> x0, waiting for transfers between devices: 77.5 us -> none  [across_chips(): lax.all_to_all(blocks, 'expert', split_axis=0, concat_axis=0, tiled=True,...]
    ppermute x0 -> x15, waiting for transfers between devices: none -> 73.4 us  [the longest x9 40.6 us: across_chips(): arrived.append(lax.ppermute(blocks[distance], 'expert', route))]
    reduce_scatter x2 -> x0, waiting for transfers between devices: 55 us -> none  [the longest x1 29.7 us: per_device(): lax.psum_scatter(grad_inner[None, None].astype(jnp.bfloat16), 'dp', scatt...]
    all_gather x4 -> x0, waiting for transfers between devices: 43.9 us -> none  [the longest x2 43.8 us: gather_weights(): lax.all_gather(outer_master.astype(jnp.bfloat16), 'dp', axis=3, tiled=True)]
    ppermute x0 -> x15, starting transfers between devices: none -> 30.5 us  [the longest x9 20.1 us: across_chips(): arrived.append(lax.ppermute(blocks[distance], 'expert', route))]
    all_to_all x5 -> x0, starting transfers between devices: 23.9 us -> none  [across_chips(): lax.all_to_all(blocks, 'expert', split_axis=0, concat_axis=0, tiled=True,...]
    ppermute x1 -> x8, waiting for transfers between devices: 11.5 us -> 33.1 us  [passed_along(): return lax.ppermute(block, axis, route)]
    dot_general x14 -> x29, matrix products: 44.9 us -> 29 us  [the longest x8 11.5 us: projected(): jnp.dot(columns(token_rows, part, count), inner_parts[part][which], prefe...]
  transfers between devices with their start and end apart: 17 -> 28, of which waited for: 11 -> 14; matrix products, arithmetic and copies ran while one was open for 8% -> 12% of each run, Pallas kernels for 33% -> 44%
where the time goes in v2:
time: 409 us; the launch traced here: 404 us
  Pallas kernels  176 us (43%)
  waiting for transfers between devices  106 us (26%)
  starting transfers between devices  39.1 us (10%)
  other arithmetic  36.9 us (9%)
  matrix products  29 us (7%)
  local copies, waits for them, and re-layouts  14.1 us (3%)
    pallas_call x1, Pallas kernels, conveyed(): pl.pallas_call(functools.partial(conveyor_kernel, chips, lag, tuple(piece...  176 us
    ppermute x9, waiting for transfers between devices, across_chips(): arrived.append(lax.ppermute(blocks[distance], 'expert', route))  40.6 us
    ppermute x8, waiting for transfers between devices, passed_along(): return lax.ppermute(block, axis, route)  33.1 us
    ppermute x6, waiting for transfers between devices, back_across_chips(): arrived.append(lax.ppermute(blocks[distance], 'expert', route))  32.9 us
    ppermute x9, starting transfers between devices, across_chips(): arrived.append(lax.ppermute(blocks[distance], 'expert', route))  20.1 us
    dot_general x8, matrix products, projected(): jnp.dot(columns(token_rows, part, count), inner_parts[part][which], prefe...  11.5 us
    ppermute x6, starting transfers between devices, back_across_chips(): arrived.append(lax.ppermute(blocks[distance], 'expert', route))  10.5 us
    ppermute x8, starting transfers between devices, passed_along(): return lax.ppermute(block, axis, route)  8.47 us
  transfers between devices with their start and end apart: 28, of which 14 were waited for; matrix products, arithmetic and copies ran while one was open for 12% of the time, Pallas kernels for 44%

profile of v2, /device:TPU:0, one launch (start us, length us, event | category | flops | bytes accessed | tf_op | source)
XLA Modules:
  0.0 404.4 jit_solution(1834656045675699393)
XLA Ops:
  0.7 1.4 fusion.30
  6.4 3.1 collective-permute-start
  9.4 2.6 collective-permute-start.1
  12.0 1.4 collective-permute-start.2
  14.1 1.2 fusion.135
  15.9 1.5 collective-permute-start.17
  19.8 2.8 collective-permute-start.13
  25.5 6.8 %collective-permute-done.1 = bf16[72,2048]{1,0:T(8,128)(2,1)S(1)} collective-permute-done((bf16[72,2048]{1,0:T(8,128)(2,1)}, bf16[72,2048]{1,0:T(8,128)(2,1)S(1)}, u32[]{:S(2)}, u32[]{:S(2)}) %collective-permute-start.1) | collective-permute-done | bytes 294944 | tf_op jit(solution)/shard_map/ppermute | solution.py:138
  32.3 1.7 collective-permute-start.4
  34.4 1.3 pad_maximum_fusion.4
  35.6 3.1 collective-permute-done.11
  38.8 18.1 %collective-permute-done.12 = bf16[72,2048]{1,0:T(8,128)(2,1)} collective-permute-done((bf16[72,2048]{1,0:T(8,128)(2,1)}, bf16[72,2048]{1,0:T(8,128)(2,1)}, u32[]{:S(2)}, u32[]{:S(2)}) %collective-permute-start.12) | collective-permute-done | bytes 294944 | tf_op jit(solution)/shard_map/ppermute | solution.py:138
  56.9 1.4 pad_maximum_fusion.6
  62.5 22.8 %collective-permute-done.5 = bf16[384,1024]{1,0:T(8,128)(2,1)S(1)} collective-permute-done((bf16[384,1024]{1,0:T(8,128)(2,1)S(1)}, bf16[384,1024]{1,0:T(8,128)(2,1)S(1)}, u32[]{:S(2)}, u32[]{:S(2)}) %collective-permute-start.5) | collective-permute-done | bytes 786464 | tf_op jit(solution)/shard_map/ppermute | solution.py:33
  94.6 1.8 collective-permute-start.16
  97.8 3.2 collective-permute-start.9
  101.1 3.3 collective-permute-start.8
  106.2 5.7 %collective-permute-done.9 = bf16[72,2048]{1,0:T(8,128)(2,1)S(1)} collective-permute-done((bf16[72,2048]{1,0:T(8,128)(2,1)S(1)}, bf16[72,2048]{1,0:T(8,128)(2,1)S(1)}, u32[]{:S(2)}, u32[]{:S(2)}) %collective-permute-start.9) | collective-permute-done | bytes 294944 | tf_op jit(solution)/shard_map/ppermute | solution.py:147
  111.8 12.1 %collective-permute-done.8 = bf16[72,2048]{1,0:T(8,128)(2,1)S(1)} collective-permute-done((bf16[72,2048]{1,0:T(8,128)(2,1)S(1)}, bf16[72,2048]{1,0:T(8,128)(2,1)S(1)}, u32[]{:S(2)}, u32[]{:S(2)}) %collective-permute-start.8) | collective-permute-done | bytes 294944 | tf_op jit(solution)/shard_map/ppermute | solution.py:147
  125.0 1.5 collective-permute-start.10
  128.1 3.8 collective-permute-done.16
  132.0 1.4 fusion.4
  133.4 5.4 %collective-permute-done.10 = bf16[128,2048]{1,0:T(8,128)(2,1)S(1)} collective-permute-done((bf16[128,2048]{1,0:T(8,128)(2,1)S(1)}, bf16[128,2048]{1,0:T(8,128)(2,1)S(1)}, u32[]{:S(2)}, u32[]{:S(2)}) %collective-permute-start.10) | collective-permute-done | bytes 524320 | tf_op jit(solution)/shard_map/ppermute | solution.py:33
  140.5 6.9 %collective-permute-start.18 = (bf16[72,2048]{1,0:T(8,128)(2,1)S(1)}, bf16[72,2048]{1,0:T(8,128)(2,1)S(1)}, u32[]{:S(2)}, u32[]{:S(2)}) collective-permute-start(bf16[72,2048]{1,0:T(8,128)(2,1)S(1)} %get-tuple-element.218), channel_id=1, source_target_pairs={{0,4},{2,6},{4,8},{6,10},{8,12},{10,14},{12,0},{14,2},{1,5},{3,7},... | collective-permute-start | bytes 884744 | tf_op jit(solution)/shard_map/ppermute | solution.py:138
  147.4 2.4 collective-permute-start.20
  149.7 2.9 fusion.5
  153.1 1.7 collective-permute-done.18
  154.7 9.8 %collective-permute-done.19 = bf16[72,2048]{1,0:T(8,128)(2,1)S(1)} collective-permute-done((bf16[72,2048]{1,0:T(8,128)(2,1)S(1)}, bf16[72,2048]{1,0:T(8,128)(2,1)S(1)}, u32[]{:S(2)}, u32[]{:S(2)}) %collective-permute-start.19) | collective-permute-done | bytes 294944 | tf_op jit(solution)/shard_map/ppermute | solution.py:138
  168.2 1.7 fusion.17.refs_0_
  172.6 2.4 constant_dynamic-update-slice_fusion.10
  175.0 176.0 %shard_map.189 = (bf16[384,1024]{1,0:T(8,128)(2,1)}, bf16[384,1024]{1,0:T(8,128)(2,1)}, bf16[384,1024]{1,0:T(8,128)(2,1)}, bf16[2048,384]{1,0:T(8,128)(2,1)}, bf...) custom-call(s32[4]{0:T(128)S(1)} %bitcast.137, bf16[384,1024]{1,0:T(8,128)(2,1)} %fusion.17.refs_0_, ...), custom_call_target="tpu_custom_call" | custom-call | flops 707788800 | bytes 14155776 | tf_op jit(solution)/shard_map/pallas_call | solution.py:394
  351.1 2.4 fusion.41
  353.5 1.9 fusion.43
  355.4 1.9 convolution_add_fusion.3
  357.4 2.0 fusion.23
  359.4 1.9 convolution_convert_fusion.2
  361.3 2.3 convolution_convert_fusion.3
  363.7 1.2 pad_maximum_fusion.2
  365.1 2.8 fusion.2
  367.9 2.2 fusion.48
  370.1 2.8 fusion.3
  373.0 3.4 convert_select_fusion
  376.4 1.7 add_convert_fusion
  379.2 2.9 collective-permute-start.25
  382.1 2.2 fusion.47
  384.3 2.5 fusion.13
  386.7 3.4 collective-permute-done.27
  390.1 11.7 %collective-permute-done.26 = bf16[72,2048]{1,0:T(8,128)(2,1)S(1)} collective-permute-done((bf16[72,2048]{1,0:T(8,128)(2,1)S(1)}, bf16[72,2048]{1,0:T(8,128)(2,1)S(1)}, u32[]{:S(2)}, u32[]{:S(2)}) %collective-permute-start.26) | collective-permute-done | bytes 294944 | tf_op jit(solution)/shard_map/ppermute | solution.py:147
  (151 shorter events, 41.1 us)
Async XLA Ops:
  5.2 8.2 %copy-start.27 = (f32[1,128,2]{1,2,0:T(2,128)S(1)}, f32[1,128,2]{1,2,0:T(2,128)}, u32[]{:S(2)}) copy-start(f32[1,128,2]{1,2,0:T(2,128)} %param.22) | copy-start | bytes 3076
  5.2 8.3 %copy-start.30 = (bf16[1,128,2048]{2,1,0:T(8,128)(2,1)S(1)}, bf16[1,128,2048]{2,1,0:T(8,128)(2,1)}, u32[]{:S(2)}) copy-start(bf16[1,128,2048]{2,1,0:T(8,128)(2,1)} %param.19) | copy-start | bytes 1572868
  6.4 13.5 %collective-permute-start = (bf16[72,2048]{1,0:T(8,128)(2,1)}, bf16[72,2048]{1,0:T(8,128)(2,1)S(1)}, u32[]{:S(2)}, u32[]{:S(2)}) collective-permute-start(bf16[72,2048]{1,0:T(8,128)(2,1)} %get-tuple-element.232), channel_id=1, source_target_pairs={{0,4},{2,6},{4,8},{6,10},{8,12},{10,14},{12,0},{14,2},{1,5},{3,7},... | collective-permute-start | bytes 884744 | tf_op jit(solution)/shard_map/ppermute | solution.py:138
  9.4 22.9 %collective-permute-start.1 = (bf16[72,2048]{1,0:T(8,128)(2,1)}, bf16[72,2048]{1,0:T(8,128)(2,1)S(1)}, u32[]{:S(2)}, u32[]{:S(2)}) collective-permute-start(bf16[72,2048]{1,0:T(8,128)(2,1)} %get-tuple-element.231), channel_id=1, source_target_pairs={{0,8},{2,10},{4,12},{6,14},{8,0},{10,2},{12,4},{14,6},{1,9},{3,11}... | collective-permute-start | bytes 884744 | tf_op jit(solution)/shard_map/ppermute | solution.py:138
  12.0 22.1 %collective-permute-start.2 = (bf16[72,2048]{1,0:T(8,128)(2,1)}, bf16[72,2048]{1,0:T(8,128)(2,1)}, u32[]{:S(2)}, u32[]{:S(2)}) collective-permute-start(bf16[72,2048]{1,0:T(8,128)(2,1)} %get-tuple-element.230), channel_id=1, source_target_pairs={{0,12},{2,14},{4,0},{6,2},{8,4},{10,6},{12,8},{14,10},{1,13},{3,15... | collective-permute-start | bytes 884744 | tf_op jit(solution)/shard_map/ppermute | solution.py:138
  13.5 3.9 copy-start.3
  14.0 1.9 copy-start.26
  15.2 2.4 copy-start.9
  15.2 23.5 %collective-permute-start.11 = (bf16[72,2048]{1,0:T(8,128)(2,1)}, bf16[72,2048]{1,0:T(8,128)(2,1)}, u32[]{:S(2)}, u32[]{:S(2)}) collective-permute-start(bf16[72,2048]{1,0:T(8,128)(2,1)} %get-tuple-element.227), channel_id=1, source_target_pairs={{0,4},{2,6},{4,8},{6,10},{8,12},{10,14},{12,0},{14,2},{1,5},{3,7},... | collective-permute-start | bytes 884744 | tf_op jit(solution)/shard_map/ppermute | solution.py:138
  15.9 3.6 collective-permute-start.17
  19.5 37.4 %collective-permute-start.12 = (bf16[72,2048]{1,0:T(8,128)(2,1)}, bf16[72,2048]{1,0:T(8,128)(2,1)}, u32[]{:S(2)}, u32[]{:S(2)}) collective-permute-start(bf16[72,2048]{1,0:T(8,128)(2,1)} %get-tuple-element.226), channel_id=1, source_target_pairs={{0,8},{2,10},{4,12},{6,14},{8,0},{10,2},{12,4},{14,6},{1,9},{3,11}... | collective-permute-start | bytes 884744 | tf_op jit(solution)/shard_map/ppermute | solution.py:138
  19.8 37.0 %collective-permute-start.13 = (bf16[72,2048]{1,0:T(8,128)(2,1)}, bf16[72,2048]{1,0:T(8,128)(2,1)}, u32[]{:S(2)}, u32[]{:S(2)}) collective-permute-start(bf16[72,2048]{1,0:T(8,128)(2,1)} %get-tuple-element.225), channel_id=1, source_target_pairs={{0,12},{2,14},{4,0},{6,2},{8,4},{10,6},{12,8},{14,10},{1,13},{3,15... | collective-permute-start | bytes 884744 | tf_op jit(solution)/shard_map/ppermute | solution.py:138
  25.5 31.3 %copy-start.17 = (bf16[72,2048]{1,0:T(8,128)(2,1)S(1)}, bf16[72,2048]{1,0:T(8,128)(2,1)}, u32[]{:S(2)}) copy-start(bf16[72,2048]{1,0:T(8,128)(2,1)} %get-tuple-element.223) | copy-start | bytes 884740
  32.3 54.6 %collective-permute-start.4 = (bf16[2,1024,384]{2,1,0:T(8,128)(2,1)S(1)}, bf16[2,1024,384]{2,1,0:T(8,128)(2,1)S(1)}, u32[]{:S(2)}, u32[]{:S(2)}) collective-permute-start(bf16[2,1024,384]{2,1,0:T(8,128)(2,1)S(1)} %bitcast_convert_fusion), channel_id=1, source_target_pairs={{1,0},{0,1},{3,2},{2,3},{5,4},{4,5},{7,6},{6,7},{9,8},{8,9},{11,10... | collective-permute-start | bytes 4718600 | tf_op jit(solution)/shard_map/ppermute | solution.py:33
  34.1 51.2 %collective-permute-start.5 = (bf16[384,1024]{1,0:T(8,128)(2,1)S(1)}, bf16[384,1024]{1,0:T(8,128)(2,1)S(1)}, u32[]{:S(2)}, u32[]{:S(2)}) collective-permute-start(bf16[384,1024]{1,0:T(8,128)(2,1)S(1)} %bitcast_convert_fusion.1), channel_id=1, source_target_pairs={{1,0},{0,1},{3,2},{2,3},{5,4},{4,5},{7,6},{6,7},{9,8},{8,9},{11,10... | collective-permute-start | bytes 2359304 | tf_op jit(solution)/shard_map/ppermute | solution.py:33
  34.4 24.0 %copy-start.24 = (bf16[576,2048]{1,0:T(8,128)(2,1)S(1)}, bf16[576,2048]{1,0:T(8,128)(2,1)}, u32[]{:S(2)}) copy-start(bf16[576,2048]{1,0:T(8,128)(2,1)} %get-tuple-element.229) | copy-start | bytes 7077892
  38.7 23.6 %collective-permute-start.3 = (bf16[288,2048]{1,0:T(8,128)(2,1)S(1)}, bf16[288,2048]{1,0:T(8,128)(2,1)S(1)}, u32[]{:S(2)}, u32[]{:S(2)}) collective-permute-start(bf16[288,2048]{1,0:T(8,128)(2,1)S(1)} %pad_maximum_fusion.4), channel_id=1, source_target_pairs={{0,2},{2,0},{4,6},{6,4},{8,10},{10,8},{12,14},{14,12},{1,3},{3,1},... | collective-permute-start | bytes 3538952 | tf_op jit(solution)/shard_map/ppermute | solution.py:153
  56.9 2.5 copy-start.18
  58.2 4.2 %collective-permute-start.14 = (bf16[288,2048]{1,0:T(8,128)(2,1)S(1)}, bf16[288,2048]{1,0:T(8,128)(2,1)S(1)}, u32[]{:S(2)}, u32[]{:S(2)}) collective-permute-start(bf16[288,2048]{1,0:T(8,128)(2,1)S(1)} %pad_maximum_fusion.6), channel_id=1, source_target_pairs={{0,2},{2,0},{4,6},{6,4},{8,10},{10,8},{12,14},{14,12},{1,3},{3,1},... | collective-permute-start | bytes 3538952 | tf_op jit(solution)/shard_map/ppermute | solution.py:153
  91.9 5.4 %collective-permute-start.6 = (bf16[288,2048]{1,0:T(8,128)(2,1)S(1)}, bf16[288,2048]{1,0:T(8,128)(2,1)S(1)}, u32[]{:S(2)}, u32[]{:S(2)}) collective-permute-start(bf16[288,2048]{1,0:T(8,128)(2,1)S(1)} %pad_maximum_fusion.3), channel_id=1, source_target_pairs={{0,2},{2,0},{4,6},{6,4},{8,10},{10,8},{12,14},{14,12},{1,3},{3,1},... | collective-permute-start | bytes 3538952 | tf_op jit(solution)/shard_map/ppermute | solution.py:153
  94.6 37.3 %collective-permute-start.16 = (bf16[2,1024,384]{2,1,0:T(8,128)(2,1)S(1)}, bf16[2,1024,384]{2,1,0:T(8,128)(2,1)S(1)}, u32[]{:S(2)}, u32[]{:S(2)}) collective-permute-start(bf16[2,1024,384]{2,1,0:T(8,128)(2,1)S(1)} %pad_maximum_fusion.1), channel_id=1, source_target_pairs={{1,0},{0,1},{3,2},{2,3},{5,4},{4,5},{7,6},{6,7},{9,8},{8,9},{11,10... | collective-permute-start | bytes 4718600 | tf_op jit(solution)/shard_map/ppermute | solution.py:33
  97.8 14.0 %collective-permute-start.9 = (bf16[72,2048]{1,0:T(8,128)(2,1)S(1)}, bf16[72,2048]{1,0:T(8,128)(2,1)S(1)}, u32[]{:S(2)}, u32[]{:S(2)}) collective-permute-start(bf16[72,2048]{1,0:T(8,128)(2,1)S(1)} %get-tuple-element.220), channel_id=1, source_target_pairs={{0,4},{2,6},{4,8},{6,10},{8,12},{10,14},{12,0},{14,2},{1,5},{3,7},... | collective-permute-start | bytes 884744 | tf_op jit(solution)/shard_map/ppermute | solution.py:147
  101.1 22.9 %collective-permute-start.8 = (bf16[72,2048]{1,0:T(8,128)(2,1)S(1)}, bf16[72,2048]{1,0:T(8,128)(2,1)S(1)}, u32[]{:S(2)}, u32[]{:S(2)}) collective-permute-start(bf16[72,2048]{1,0:T(8,128)(2,1)S(1)} %get-tuple-element.221), channel_id=1, source_target_pairs={{0,8},{2,10},{4,12},{6,14},{8,0},{10,2},{12,4},{14,6},{1,9},{3,11}... | collective-permute-start | bytes 884744 | tf_op jit(solution)/shard_map/ppermute | solution.py:147
  104.4 19.6 %collective-permute-start.7 = (bf16[72,2048]{1,0:T(8,128)(2,1)S(1)}, bf16[72,2048]{1,0:T(8,128)(2,1)S(1)}, u32[]{:S(2)}, u32[]{:S(2)}) collective-permute-start(bf16[72,2048]{1,0:T(8,128)(2,1)S(1)} %get-tuple-element.222), channel_id=1, source_target_pairs={{0,12},{2,14},{4,0},{6,2},{8,4},{10,6},{12,8},{14,10},{1,13},{3,15... | collective-permute-start | bytes 884744 | tf_op jit(solution)/shard_map/ppermute | solution.py:147
  125.0 7.0 %copy-start.13 = (bf16[1,1,2,1024,384]{4,3,2,1,0:T(8,128)(2,1)S(1)}, bf16[1,1,2,1024,384]{4,3,2,1,0:T(8,128)(2,1)}, u32[]{:S(2)}) copy-start(bf16[1,1,2,1024,384]{4,3,2,1,0:T(8,128)(2,1)} %param.28) | copy-start | bytes 4718596
  125.0 7.0 %copy-start.14 = (bf16[1,1,2,1024,384]{4,3,2,1,0:T(8,128)(2,1)S(1)}, bf16[1,1,2,1024,384]{4,3,2,1,0:T(8,128)(2,1)}, u32[]{:S(2)}) copy-start(bf16[1,1,2,1024,384]{4,3,2,1,0:T(8,128)(2,1)} %param.30) | copy-start | bytes 4718596
  125.0 13.9 %collective-permute-start.10 = (bf16[128,2048]{1,0:T(8,128)(2,1)S(1)}, bf16[128,2048]{1,0:T(8,128)(2,1)S(1)}, u32[]{:S(2)}, u32[]{:S(2)}) collective-permute-start(bf16[128,2048]{1,0:T(8,128)(2,1)S(1)} %fusion.9), channel_id=1, source_target_pairs={{16,0},{0,16},{17,1},{1,17},{18,2},{2,18},{19,3},{3,19},{20,4},{4,... | collective-permute-start | bytes 1572872 | tf_op jit(solution)/shard_map/ppermute | solution.py:33
  127.5 39.3 %collective-permute-start.15 = (bf16[384,1024]{1,0:T(8,128)(2,1)S(1)}, bf16[384,1024]{1,0:T(8,128)(2,1)S(1)}, u32[]{:S(2)}, u32[]{:S(2)}) collective-permute-start(bf16[384,1024]{1,0:T(8,128)(2,1)S(1)} %convolution_convert_fusion.10), channel_id=1, source_target_pairs={{1,0},{0,1},{3,2},{2,3},{5,4},{4,5},{7,6},{6,7},{9,8},{8,9},{11,10... | collective-permute-start | bytes 2359304 | tf_op jit(solution)/shard_map/ppermute | solution.py:33
  133.4 16.3 %copy-start = (bf16[2,1024,384]{2,1,0:T(8,128)(2,1)}, bf16[2,1024,384]{2,1,0:T(8,128)(2,1)S(1)}, u32[]{:S(2)}) copy-start(bf16[2,1024,384]{2,1,0:T(8,128)(2,1)S(1)} %get-tuple-element.148) | copy-start | bytes 4718596
  139.1 10.7 %copy-start.4 = (f32[1,1,2,1024,384]{4,3,2,1,0:T(8,128)S(1)}, f32[1,1,2,1024,384]{4,3,2,1,0:T(8,128)}, u32[]{:S(2)}) copy-start(f32[1,1,2,1024,384]{4,3,2,1,0:T(8,128)} %param.26) | copy-start | bytes 9437188
  140.5 14.3 %collective-permute-start.18 = (bf16[72,2048]{1,0:T(8,128)(2,1)S(1)}, bf16[72,2048]{1,0:T(8,128)(2,1)S(1)}, u32[]{:S(2)}, u32[]{:S(2)}) collective-permute-start(bf16[72,2048]{1,0:T(8,128)(2,1)S(1)} %get-tuple-element.218), channel_id=1, source_target_pairs={{0,4},{2,6},{4,8},{6,10},{8,12},{10,14},{12,0},{14,2},{1,5},{3,7},... | collective-permute-start | bytes 884744 | tf_op jit(solution)/shard_map/ppermute | solution.py:138
  147.3 17.2 %collective-permute-start.19 = (bf16[72,2048]{1,0:T(8,128)(2,1)S(1)}, bf16[72,2048]{1,0:T(8,128)(2,1)S(1)}, u32[]{:S(2)}, u32[]{:S(2)}) collective-permute-start(bf16[72,2048]{1,0:T(8,128)(2,1)S(1)} %get-tuple-element.217), channel_id=1, source_target_pairs={{0,8},{2,10},{4,12},{6,14},{8,0},{10,2},{12,4},{14,6},{1,9},{3,11}... | collective-permute-start | bytes 884744 | tf_op jit(solution)/shard_map/ppermute | solution.py:138
  147.4 18.3 %collective-permute-start.20 = (bf16[72,2048]{1,0:T(8,128)(2,1)S(1)}, bf16[72,2048]{1,0:T(8,128)(2,1)S(1)}, u32[]{:S(2)}, u32[]{:S(2)}) collective-permute-start(bf16[72,2048]{1,0:T(8,128)(2,1)S(1)} %get-tuple-element.216), channel_id=1, source_target_pairs={{0,12},{2,14},{4,0},{6,2},{8,4},{10,6},{12,8},{14,10},{1,13},{3,15... | collective-permute-start | bytes 884744 | tf_op jit(solution)/shard_map/ppermute | solution.py:138
  152.6 14.2 %copy-start.19 = (bf16[1,1,384,1024]{3,2,1,0:T(8,128)(2,1)S(1)}, bf16[1,1,384,1024]{3,2,1,0:T(8,128)(2,1)}, u32[]{:S(2)}) copy-start(bf16[1,1,384,1024]{3,2,1,0:T(8,128)(2,1)} %param.29) | copy-start | bytes 2359300
  152.6 14.2 %copy-start.20 = (bf16[1,1,384,1024]{3,2,1,0:T(8,128)(2,1)S(1)}, bf16[1,1,384,1024]{3,2,1,0:T(8,128)(2,1)}, u32[]{:S(2)}) copy-start(bf16[1,1,384,1024]{3,2,1,0:T(8,128)(2,1)} %param.31) | copy-start | bytes 2359300
  152.6 198.5 %collective-permute-start.22 = (bf16[2,1024,384]{2,1,0:T(8,128)(2,1)}, bf16[2,1024,384]{2,1,0:T(8,128)(2,1)}, u32[]{:S(2)}, u32[]{:S(2)}) collective-permute-start(bf16[2,1024,384]{2,1,0:T(8,128)(2,1)} %fusion.5), channel_id=1, source_target_pairs={{1,0},{0,1},{3,2},{2,3},{5,4},{4,5},{7,6},{6,7},{9,8},{8,9},{11,10... | collective-permute-start | bytes 4718600 | tf_op jit(solution)/shard_map/ppermute | solution.py:33
  166.8 5.8 %collective-permute-start.21 = (bf16[288,2048]{1,0:T(8,128)(2,1)}, bf16[288,2048]{1,0:T(8,128)(2,1)}, u32[]{:S(2)}, u32[]{:S(2)}) collective-permute-start(bf16[288,2048]{1,0:T(8,128)(2,1)} %pad_maximum_fusion.7), channel_id=1, source_target_pairs={{0,2},{2,0},{4,6},{6,4},{8,10},{10,8},{12,14},{14,12},{1,3},{3,1},... | collective-permute-start | bytes 3538952 | tf_op jit(solution)/shard_map/ppermute | solution.py:153
  167.6 2.3 copy-start.1
  167.6 2.3 copy-start.2
  169.9 181.2 %collective-permute-start.23 = (bf16[384,1024]{1,0:T(8,128)(2,1)}, bf16[384,1024]{1,0:T(8,128)(2,1)}, u32[]{:S(2)}, u32[]{:S(2)}) collective-permute-start(bf16[384,1024]{1,0:T(8,128)(2,1)} %fusion.17.refs_0_), channel_id=1, source_target_pairs={{1,0},{0,1},{3,2},{2,3},{5,4},{4,5},{7,6},{6,7},{9,8},{8,9},{11,10... | collective-permute-start | bytes 2359304 | tf_op jit(solution)/shard_map/ppermute | solution.py:33
  351.1 2.4 copy-start.25
  361.3 3.6 copy-start.5
  365.1 11.3 %collective-permute-start.24 = (bf16[288,2048]{1,0:T(8,128)(2,1)}, bf16[288,2048]{1,0:T(8,128)(2,1)}, u32[]{:S(2)}, u32[]{:S(2)}) collective-permute-start(bf16[288,2048]{1,0:T(8,128)(2,1)} %pad_maximum_fusion.2), channel_id=1, source_target_pairs={{0,2},{2,0},{4,6},{6,4},{8,10},{10,8},{12,14},{14,12},{1,3},{3,1},... | collective-permute-start | bytes 3538952 | tf_op jit(solution)/shard_map/ppermute | solution.py:153
  373.0 3.4 copy-start.6
  373.0 3.4 copy-start.8
  378.2 11.9 %collective-permute-start.27 = (bf16[72,2048]{1,0:T(8,128)(2,1)S(1)}, bf16[72,2048]{1,0:T(8,128)(2,1)S(1)}, u32[]{:S(2)}, u32[]{:S(2)}) collective-permute-start(bf16[72,2048]{1,0:T(8,128)(2,1)S(1)} %get-tuple-element.211), channel_id=1, source_target_pairs={{0,4},{2,6},{4,8},{6,10},{8,12},{10,14},{12,0},{14,2},{1,5},{3,7},... | collective-permute-start | bytes 884744 | tf_op jit(solution)/shard_map/ppermute | solution.py:147
  378.3 23.5 %collective-permute-start.26 = (bf16[72,2048]{1,0:T(8,128)(2,1)S(1)}, bf16[72,2048]{1,0:T(8,128)(2,1)S(1)}, u32[]{:S(2)}, u32[]{:S(2)}) collective-permute-start(bf16[72,2048]{1,0:T(8,128)(2,1)S(1)} %get-tuple-element.212), channel_id=1, source_target_pairs={{0,8},{2,10},{4,12},{6,14},{8,0},{10,2},{12,4},{14,6},{1,9},{3,11}... | collective-permute-start | bytes 884744 | tf_op jit(solution)/shard_map/ppermute | solution.py:147
  379.2 22.7 %collective-permute-start.25 = (bf16[72,2048]{1,0:T(8,128)(2,1)S(1)}, bf16[72,2048]{1,0:T(8,128)(2,1)S(1)}, u32[]{:S(2)}, u32[]{:S(2)}) collective-permute-start(bf16[72,2048]{1,0:T(8,128)(2,1)S(1)} %get-tuple-element.213), channel_id=1, source_target_pairs={{0,12},{2,14},{4,0},{6,2},{8,4},{10,6},{12,8},{14,10},{1,13},{3,15... | collective-permute-start | bytes 884744 | tf_op jit(solution)/shard_map/ppermute | solution.py:147
  (6 other events, 7.0 us)

commit v3 on v2

--- a/solution.py
+++ b/solution.py
@@ -17,6 +17,8 @@
 adam_eps = 1e-08
 bias_one = 0.999973438601112
 bias_two = 0.994079470779667
+LAG = 2
+PIECE = 98304
 
 
 def for_sending(array):
@@ -64,11 +66,20 @@
 
     gate_proj, up_proj = projected(0), projected(1)
     activity = (silu_parts(gate_proj)[0] * up_proj).astype(jnp.bfloat16)
-    half_out = [
-        jnp.dot(activity, outer, preferred_element_type=jnp.float32).astype(jnp.bfloat16)
-        for outer in outer_parts
-    ]
-    return (jnp.concatenate(half_out, axis=-1), activity, gate_proj, up_proj)
+
+    def half_out(rows):
+        return jnp.concatenate(
+            [
+                jnp.dot(rows, outer, preferred_element_type=jnp.float32).astype(jnp.bfloat16)
+                for outer in outer_parts
+            ],
+            axis=-1,
+        )
+
+    middle = activity.shape[0] // 2
+    for_partner = half_out(activity[middle:])
+    for_own = half_out(activity[:middle])
+    return ((for_own, for_partner), activity, gate_proj, up_proj)
 
 
 def half_backward(token_rows, grad_rows, outer_parts, activity, gate_proj, up_proj):
@@ -193,9 +204,10 @@
 
 
 def returned_rows(token_rows, half_out, slots, gates, pair_count):
-    rows = half_out.shape[0] // 2
-    other = to_partner(half_out[rows:])
-    summed = (half_out[:rows].astype(jnp.float32) + other.astype(jnp.float32)).astype(jnp.bfloat16)
+    for_own, for_partner = half_out
+    rows = for_own.shape[0]
+    other = to_partner(for_partner)
+    summed = (for_own.astype(jnp.float32) + other.astype(jnp.float32)).astype(jnp.bfloat16)
     back = jnp.concatenate(back_across_chips(blocks_of(summed, pair_count)), axis=0)
     weighting = selection(slots, gates, rows)
     high = weighting.astype(jnp.bfloat16)
@@ -258,18 +270,31 @@
 
 def conveyor_kernel(chips, lag, pieces, this_round, places, *refs):
     count = len(pieces)
-    own = refs[:count]
-    out = refs[count : 2 * count]
-    up_in = refs[2 * count : 3 * count]
-    down_in = refs[3 * count : 4 * count]
-    up_out = refs[4 * count : 5 * count]
-    down_out = refs[5 * count : 6 * count]
-    up_sent, down_sent, up_got, down_got = refs[6 * count :]
+    source = refs[:count]
+    result = refs[count : 2 * count]
+    own = refs[2 * count : 3 * count]
+    out = refs[3 * count : 4 * count]
+    up_in = refs[4 * count : 5 * count]
+    down_in = refs[5 * count : 6 * count]
+    up_out = refs[6 * count : 7 * count]
+    down_out = refs[7 * count : 8 * count]
+    loaded, stored, up_sent, down_sent, up_got, down_got = refs[8 * count :]
     place = lax.axis_index("expert")
     chip = place // 2
     above, below = {"expert": place + 2}, {"expert": place - 2}
     has_above, has_below = chip < chips - 1, chip > 0
 
+    offset = 0
+    for k, (number, rows) in enumerate(pieces):
+
+        def load(i, carry, k=k, rows=rows, offset=offset):
+            part = pl.ds(pl.multiple_of(i * rows, rows), rows)
+            pltpu.make_async_copy(source[k].at[part], own[k].at[part], loaded.at[offset + i]).start()
+            return carry
+
+        lax.fori_loop(0, number, load, 0)
+        offset += number
+
     barrier = pltpu.get_barrier_semaphore()
 
     @pl.when(has_above)
@@ -287,9 +312,9 @@
     )
     total = sum(number for number, _ in pieces)
 
-    def send(source, target, sent, got, k, index, device):
+    def send(block, target, sent, got, k, index, device):
         pltpu.make_async_remote_copy(
-            src_ref=source,
+            src_ref=block,
             dst_ref=target,
             send_sem=sent.at[k],
             recv_sem=got.at[index],
@@ -345,9 +370,26 @@
 
             offset += number
 
+    def each_piece(index, action):
+        offset = 0
+        for k, (number, rows) in enumerate(pieces):
+
+            @pl.when((index >= offset) & (index < offset + number))
+            def _(k=k, rows=rows, offset=offset):
+                action(k, pl.ds(pl.multiple_of((index - offset) * rows, rows), rows), index)
+
+            offset += number
+
+    def await_own(k, part, index):
+        pltpu.make_async_copy(source[k].at[part], own[k].at[part], loaded.at[index]).wait()
+
+    def store(k, part, index):
+        pltpu.make_async_copy(out[k].at[part], result[k].at[part], stored.at[k]).start()
+
     def step(t, carry):
         up_index = t - chip * lag
         down_index = t - (chips - 1 - chip) * lag
+        each_piece(jnp.maximum(up_index, down_index), await_own)
         stream(
             up_index, chip == 0, chip == chips - 1, above, start_up, up_in, up_out, up_sent, up_got
         )
@@ -362,12 +404,15 @@
             down_sent,
             down_got,
         )
-        settle(jnp.minimum(up_index, down_index))
+        settled = jnp.minimum(up_index, down_index)
+        settle(settled)
+        each_piece(settled - 1, store)
         return carry
 
-    lax.fori_loop(0, total + (chips - 1) * lag, step, 0)
+    lax.fori_loop(0, total + (chips - 1) * lag + 1, step, 0)
 
     for k in range(count):
+        pltpu.make_async_copy(out[k], result[k], stored.at[k]).wait()
 
         @pl.when(has_above)
         def _(k=k):
@@ -390,14 +435,16 @@
     total = sum(number for number, _ in pieces)
     whole = [pltpu.VMEM(array.shape, array.dtype) for array in arrays]
     moved = sum(array.size * 2 for array in arrays)
-    in_vmem = pl.BlockSpec(memory_space=pltpu.VMEM)
+    in_place = pl.BlockSpec(memory_space=pl.ANY)
     return pl.pallas_call(
         functools.partial(conveyor_kernel, chips, lag, tuple(pieces), this_round),
         out_shape=[jax.ShapeDtypeStruct(array.shape, array.dtype) for array in arrays],
-        in_specs=[pl.BlockSpec(memory_space=pltpu.SMEM)] + [in_vmem] * len(arrays),
-        out_specs=[in_vmem] * len(arrays),
-        scratch_shapes=whole * 4
+        in_specs=[pl.BlockSpec(memory_space=pltpu.SMEM)] + [in_place] * len(arrays),
+        out_specs=[in_place] * len(arrays),
+        scratch_shapes=whole * 6
         + [
+            pltpu.SemaphoreType.DMA((total,)),
+            pltpu.SemaphoreType.DMA((len(arrays),)),
             pltpu.SemaphoreType.DMA((len(arrays),)),
             pltpu.SemaphoreType.DMA((len(arrays),)),
             pltpu.SemaphoreType.DMA((total,)),
@@ -414,7 +461,7 @@
 
 def first_journey(arrays, place):
     flat = [array.reshape(-1, array.shape[-1]) for array in arrays]
-    return flat, tuple(conveyed(flat, place, 0, 2, 98304))
+    return flat, tuple(conveyed(flat, place, 0, LAG, PIECE))
 
 
 def further_journeys(flat, result, place, need):
@@ -429,7 +476,7 @@
             _, _, take_up, take_down = journey_flags(
                 [place[i] for i in range(chips)], chip, this_round
             )
-            moved = conveyed(flat, place, this_round, 2, 98304)
+            moved = conveyed(flat, place, this_round, LAG, PIECE)
             merged = tuple(
                 jnp.where(take_up | take_down, new, old) for new, old in zip(moved, before)
             )

time: 409 us -> 412 us (level)
    dot_general x4 -> x8, matrix products: 5.83 us -> 9.95 us  [half_out(): jnp.dot(rows, outer, preferred_element_type=jnp.float32)]
  transfers between devices with their start and end apart: 28 -> 28, of which waited for: 14 -> 14; matrix products, arithmetic and copies ran while one was open for 12% -> 12% of each run, Pallas kernels for 44% -> 43%
where the time goes in v3:
time: 412 us; the launch traced here: 407 us
  Pallas kernels  175 us (42%)
  waiting for transfers between devices  107 us (26%)
  starting transfers between devices  39.2 us (10%)
  other arithmetic  36.8 us (9%)
  matrix products  33.1 us (8%)
  local copies, waits for them, and re-layouts  13.9 us (3%)
    pallas_call x1, Pallas kernels, conveyed(): pl.pallas_call(functools.partial(conveyor_kernel, chips, lag, tuple(piece...  175 us
    ppermute x9, waiting for transfers between devices, across_chips(): arrived.append(lax.ppermute(blocks[distance], 'expert', route))  40.6 us
    ppermute x8, waiting for transfers between devices, passed_along(): return lax.ppermute(block, axis, route)  33.1 us
    ppermute x6, waiting for transfers between devices, back_across_chips(): arrived.append(lax.ppermute(blocks[distance], 'expert', route))  32.9 us
    ppermute x9, starting transfers between devices, across_chips(): arrived.append(lax.ppermute(blocks[distance], 'expert', route))  20 us
    dot_general x8, matrix products, projected(): jnp.dot(columns(token_rows, part, count), inner_parts[part][which], prefe...  11.5 us
    ppermute x6, starting transfers between devices, back_across_chips(): arrived.append(lax.ppermute(blocks[distance], 'expert', route))  10.5 us
    dot_general x8, matrix products, half_out(): jnp.dot(rows, outer, preferred_element_type=jnp.float32)  9.95 us
  transfers between devices with their start and end apart: 28, of which 14 were waited for; matrix products, arithmetic and copies ran while one was open for 12% of the time, Pallas kernels for 43%

profile of v3, /device:TPU:0, one launch (start us, length us, event | category | flops | bytes accessed | tf_op | source)
XLA Modules:
  0.0 407.4 jit_solution(9864261654579570020)
XLA Ops:
  0.7 1.4 fusion.28
  6.4 3.1 collective-permute-start
  9.4 2.6 collective-permute-start.1
  12.0 1.4 collective-permute-start.2
  15.9 1.5 collective-permute-start.17
  19.8 2.8 collective-permute-start.13
  25.5 6.9 %collective-permute-done.1 = bf16[72,2048]{1,0:T(8,128)(2,1)S(1)} collective-permute-done((bf16[72,2048]{1,0:T(8,128)(2,1)}, bf16[72,2048]{1,0:T(8,128)(2,1)S(1)}, u32[]{:S(2)}, u32[]{:S(2)}) %collective-permute-start.1) | collective-permute-done | bytes 294944 | tf_op jit(solution)/shard_map/ppermute | solution.py:149
  32.3 1.7 collective-permute-start.4
  34.4 1.3 pad_maximum_fusion.2
  35.6 3.1 collective-permute-done.11
  38.8 18.1 %collective-permute-done.12 = bf16[72,2048]{1,0:T(8,128)(2,1)} collective-permute-done((bf16[72,2048]{1,0:T(8,128)(2,1)}, bf16[72,2048]{1,0:T(8,128)(2,1)}, u32[]{:S(2)}, u32[]{:S(2)}) %collective-permute-start.12) | collective-permute-done | bytes 294944 | tf_op jit(solution)/shard_map/ppermute | solution.py:149
  56.9 1.4 pad_maximum_fusion.5
  62.5 22.8 %collective-permute-done.5 = bf16[384,1024]{1,0:T(8,128)(2,1)S(1)} collective-permute-done((bf16[384,1024]{1,0:T(8,128)(2,1)S(1)}, bf16[384,1024]{1,0:T(8,128)(2,1)S(1)}, u32[]{:S(2)}, u32[]{:S(2)}) %collective-permute-start.5) | collective-permute-done | bytes 786464 | tf_op jit(solution)/shard_map/ppermute | solution.py:35
  94.0 1.8 collective-permute-start.16
  98.2 3.2 collective-permute-start.9
  101.4 3.3 collective-permute-start.8
  106.5 5.7 %collective-permute-done.9 = bf16[72,2048]{1,0:T(8,128)(2,1)S(1)} collective-permute-done((bf16[72,2048]{1,0:T(8,128)(2,1)S(1)}, bf16[72,2048]{1,0:T(8,128)(2,1)S(1)}, u32[]{:S(2)}, u32[]{:S(2)}) %collective-permute-start.9) | collective-permute-done | bytes 294944 | tf_op jit(solution)/shard_map/ppermute | solution.py:158
  112.2 12.1 %collective-permute-done.8 = bf16[72,2048]{1,0:T(8,128)(2,1)S(1)} collective-permute-done((bf16[72,2048]{1,0:T(8,128)(2,1)S(1)}, bf16[72,2048]{1,0:T(8,128)(2,1)S(1)}, u32[]{:S(2)}, u32[]{:S(2)}) %collective-permute-start.8) | collective-permute-done | bytes 294944 | tf_op jit(solution)/shard_map/ppermute | solution.py:158
  125.4 1.5 collective-permute-start.10
  128.5 2.9 collective-permute-done.16
  131.4 1.4 fusion.4
  132.8 6.4 %collective-permute-done.10 = bf16[128,2048]{1,0:T(8,128)(2,1)S(1)} collective-permute-done((bf16[128,2048]{1,0:T(8,128)(2,1)S(1)}, bf16[128,2048]{1,0:T(8,128)(2,1)S(1)}, u32[]{:S(2)}, u32[]{:S(2)}) %collective-permute-start.10) | collective-permute-done | bytes 524320 | tf_op jit(solution)/shard_map/ppermute | solution.py:35
  140.9 6.9 %collective-permute-start.18 = (bf16[72,2048]{1,0:T(8,128)(2,1)S(1)}, bf16[72,2048]{1,0:T(8,128)(2,1)S(1)}, u32[]{:S(2)}, u32[]{:S(2)}) collective-permute-start(bf16[72,2048]{1,0:T(8,128)(2,1)S(1)} %get-tuple-element.218), channel_id=1, source_target_pairs={{0,4},{2,6},{4,8},{6,10},{8,12},{10,14},{12,0},{14,2},{1,5},{3,7},... | collective-permute-start | bytes 884744 | tf_op jit(solution)/shard_map/ppermute | solution.py:149
  147.7 2.4 collective-permute-start.20
  150.1 2.9 fusion.5
  153.5 1.6 collective-permute-done.18
  155.1 9.9 %collective-permute-done.19 = bf16[72,2048]{1,0:T(8,128)(2,1)S(1)} collective-permute-done((bf16[72,2048]{1,0:T(8,128)(2,1)S(1)}, bf16[72,2048]{1,0:T(8,128)(2,1)S(1)}, u32[]{:S(2)}, u32[]{:S(2)}) %collective-permute-start.19) | collective-permute-done | bytes 294944 | tf_op jit(solution)/shard_map/ppermute | solution.py:149
  168.5 1.7 fusion.17.refs_0_
  173.0 2.4 constant_dynamic-update-slice_fusion.10
  175.4 175.2 %shard_map.189 = (bf16[384,1024]{1,0:T(8,128)(2,1)}, bf16[384,1024]{1,0:T(8,128)(2,1)}, bf16[384,1024]{1,0:T(8,128)(2,1)}, bf16[2048,384]{1,0:T(8,128)(2,1)}, bf...) custom-call(s32[4]{0:T(128)S(1)} %bitcast.137, bf16[384,1024]{1,0:T(8,128)(2,1)} %fusion.17.refs_0_, ...), custom_call_target="tpu_custom_call" | custom-call | flops 707788800 | bytes 14155776 | tf_op jit(solution)/shard_map/pallas_call | solution.py:439
  350.6 2.4 fusion.39
  353.0 1.9 fusion.41
  354.9 1.9 convolution_add_fusion.3
  356.9 2.0 fusion.23
  358.9 1.6 convolution_convert_fusion.8
  360.5 2.4 convolution_convert_fusion.10
  363.0 1.6 convolution_convert_fusion.9
  364.6 2.4 convolution_convert_fusion.11
  368.1 2.8 fusion.2
  371.0 2.2 fusion.46
  373.1 2.8 fusion.3
  376.0 3.4 convert_select_fusion
  379.4 1.7 add_convert_fusion
  382.2 2.9 collective-permute-start.25
  385.1 2.2 fusion.45
  387.2 2.5 fusion.13
  389.7 3.4 collective-permute-done.27
  393.1 11.7 %collective-permute-done.26 = bf16[72,2048]{1,0:T(8,128)(2,1)S(1)} collective-permute-done((bf16[72,2048]{1,0:T(8,128)(2,1)S(1)}, bf16[72,2048]{1,0:T(8,128)(2,1)S(1)}, u32[]{:S(2)}, u32[]{:S(2)}) %collective-permute-start.26) | collective-permute-done | bytes 294944 | tf_op jit(solution)/shard_map/ppermute | solution.py:158
  (151 shorter events, 43.6 us)
Async XLA Ops:
  5.2 8.2 %copy-start.25 = (f32[1,128,2]{1,2,0:T(2,128)S(1)}, f32[1,128,2]{1,2,0:T(2,128)}, u32[]{:S(2)}) copy-start(f32[1,128,2]{1,2,0:T(2,128)} %param.22) | copy-start | bytes 3076
  5.2 8.3 %copy-start.28 = (bf16[1,128,2048]{2,1,0:T(8,128)(2,1)S(1)}, bf16[1,128,2048]{2,1,0:T(8,128)(2,1)}, u32[]{:S(2)}) copy-start(bf16[1,128,2048]{2,1,0:T(8,128)(2,1)} %param.19) | copy-start | bytes 1572868
  6.4 13.5 %collective-permute-start = (bf16[72,2048]{1,0:T(8,128)(2,1)}, bf16[72,2048]{1,0:T(8,128)(2,1)S(1)}, u32[]{:S(2)}, u32[]{:S(2)}) collective-permute-start(bf16[72,2048]{1,0:T(8,128)(2,1)} %get-tuple-element.232), channel_id=1, source_target_pairs={{0,4},{2,6},{4,8},{6,10},{8,12},{10,14},{12,0},{14,2},{1,5},{3,7},... | collective-permute-start | bytes 884744 | tf_op jit(solution)/shard_map/ppermute | solution.py:149
  9.4 22.9 %collective-permute-start.1 = (bf16[72,2048]{1,0:T(8,128)(2,1)}, bf16[72,2048]{1,0:T(8,128)(2,1)S(1)}, u32[]{:S(2)}, u32[]{:S(2)}) collective-permute-start(bf16[72,2048]{1,0:T(8,128)(2,1)} %get-tuple-element.231), channel_id=1, source_target_pairs={{0,8},{2,10},{4,12},{6,14},{8,0},{10,2},{12,4},{14,6},{1,9},{3,11}... | collective-permute-start | bytes 884744 | tf_op jit(solution)/shard_map/ppermute | solution.py:149
  12.0 22.1 %collective-permute-start.2 = (bf16[72,2048]{1,0:T(8,128)(2,1)}, bf16[72,2048]{1,0:T(8,128)(2,1)}, u32[]{:S(2)}, u32[]{:S(2)}) collective-permute-start(bf16[72,2048]{1,0:T(8,128)(2,1)} %get-tuple-element.230), channel_id=1, source_target_pairs={{0,12},{2,14},{4,0},{6,2},{8,4},{10,6},{12,8},{14,10},{1,13},{3,15... | collective-permute-start | bytes 884744 | tf_op jit(solution)/shard_map/ppermute | solution.py:149
  13.5 3.9 copy-start.3
  14.0 1.9 copy-start.24
  15.2 2.4 copy-start.5
  15.2 23.5 %collective-permute-start.11 = (bf16[72,2048]{1,0:T(8,128)(2,1)}, bf16[72,2048]{1,0:T(8,128)(2,1)}, u32[]{:S(2)}, u32[]{:S(2)}) collective-permute-start(bf16[72,2048]{1,0:T(8,128)(2,1)} %get-tuple-element.227), channel_id=1, source_target_pairs={{0,4},{2,6},{4,8},{6,10},{8,12},{10,14},{12,0},{14,2},{1,5},{3,7},... | collective-permute-start | bytes 884744 | tf_op jit(solution)/shard_map/ppermute | solution.py:149
  15.9 3.6 collective-permute-start.17
  19.5 37.4 %collective-permute-start.12 = (bf16[72,2048]{1,0:T(8,128)(2,1)}, bf16[72,2048]{1,0:T(8,128)(2,1)}, u32[]{:S(2)}, u32[]{:S(2)}) collective-permute-start(bf16[72,2048]{1,0:T(8,128)(2,1)} %get-tuple-element.226), channel_id=1, source_target_pairs={{0,8},{2,10},{4,12},{6,14},{8,0},{10,2},{12,4},{14,6},{1,9},{3,11}... | collective-permute-start | bytes 884744 | tf_op jit(solution)/shard_map/ppermute | solution.py:149
  19.8 37.0 %collective-permute-start.13 = (bf16[72,2048]{1,0:T(8,128)(2,1)}, bf16[72,2048]{1,0:T(8,128)(2,1)}, u32[]{:S(2)}, u32[]{:S(2)}) collective-permute-start(bf16[72,2048]{1,0:T(8,128)(2,1)} %get-tuple-element.225), channel_id=1, source_target_pairs={{0,12},{2,14},{4,0},{6,2},{8,4},{10,6},{12,8},{14,10},{1,13},{3,15... | collective-permute-start | bytes 884744 | tf_op jit(solution)/shard_map/ppermute | solution.py:149
  25.4 31.4 %copy-start.15 = (bf16[72,2048]{1,0:T(8,128)(2,1)S(1)}, bf16[72,2048]{1,0:T(8,128)(2,1)}, u32[]{:S(2)}) copy-start(bf16[72,2048]{1,0:T(8,128)(2,1)} %get-tuple-element.223) | copy-start | bytes 884740
  32.3 54.6 %collective-permute-start.4 = (bf16[2,1024,384]{2,1,0:T(8,128)(2,1)S(1)}, bf16[2,1024,384]{2,1,0:T(8,128)(2,1)S(1)}, u32[]{:S(2)}, u32[]{:S(2)}) collective-permute-start(bf16[2,1024,384]{2,1,0:T(8,128)(2,1)S(1)} %bitcast_convert_fusion), channel_id=1, source_target_pairs={{1,0},{0,1},{3,2},{2,3},{5,4},{4,5},{7,6},{6,7},{9,8},{8,9},{11,10... | collective-permute-start | bytes 4718600 | tf_op jit(solution)/shard_map/ppermute | solution.py:35
  34.1 51.2 %collective-permute-start.5 = (bf16[384,1024]{1,0:T(8,128)(2,1)S(1)}, bf16[384,1024]{1,0:T(8,128)(2,1)S(1)}, u32[]{:S(2)}, u32[]{:S(2)}) collective-permute-start(bf16[384,1024]{1,0:T(8,128)(2,1)S(1)} %bitcast_convert_fusion.1), channel_id=1, source_target_pairs={{1,0},{0,1},{3,2},{2,3},{5,4},{4,5},{7,6},{6,7},{9,8},{8,9},{11,10... | collective-permute-start | bytes 2359304 | tf_op jit(solution)/shard_map/ppermute | solution.py:35
  34.4 24.0 %copy-start.22 = (bf16[576,2048]{1,0:T(8,128)(2,1)S(1)}, bf16[576,2048]{1,0:T(8,128)(2,1)}, u32[]{:S(2)}) copy-start(bf16[576,2048]{1,0:T(8,128)(2,1)} %get-tuple-element.229) | copy-start | bytes 7077892
  38.7 23.6 %collective-permute-start.3 = (bf16[288,2048]{1,0:T(8,128)(2,1)S(1)}, bf16[288,2048]{1,0:T(8,128)(2,1)S(1)}, u32[]{:S(2)}, u32[]{:S(2)}) collective-permute-start(bf16[288,2048]{1,0:T(8,128)(2,1)S(1)} %pad_maximum_fusion.2), channel_id=1, source_target_pairs={{0,2},{2,0},{4,6},{6,4},{8,10},{10,8},{12,14},{14,12},{1,3},{3,1},... | collective-permute-start | bytes 3538952 | tf_op jit(solution)/shard_map/ppermute | solution.py:164
  56.9 2.5 copy-start.16
  58.2 4.2 %collective-permute-start.14 = (bf16[288,2048]{1,0:T(8,128)(2,1)S(1)}, bf16[288,2048]{1,0:T(8,128)(2,1)S(1)}, u32[]{:S(2)}, u32[]{:S(2)}) collective-permute-start(bf16[288,2048]{1,0:T(8,128)(2,1)S(1)} %pad_maximum_fusion.5), channel_id=1, source_target_pairs={{0,2},{2,0},{4,6},{6,4},{8,10},{10,8},{12,14},{14,12},{1,3},{3,1},... | collective-permute-start | bytes 3538952 | tf_op jit(solution)/shard_map/ppermute | solution.py:164
  92.8 4.8 %collective-permute-start.6 = (bf16[288,2048]{1,0:T(8,128)(2,1)S(1)}, bf16[288,2048]{1,0:T(8,128)(2,1)S(1)}, u32[]{:S(2)}, u32[]{:S(2)}) collective-permute-start(bf16[288,2048]{1,0:T(8,128)(2,1)S(1)} %pad_maximum_fusion.3), channel_id=1, source_target_pairs={{0,2},{2,0},{4,6},{6,4},{8,10},{10,8},{12,14},{14,12},{1,3},{3,1},... | collective-permute-start | bytes 3538952 | tf_op jit(solution)/shard_map/ppermute | solution.py:164
  94.0 37.3 %collective-permute-start.16 = (bf16[2,1024,384]{2,1,0:T(8,128)(2,1)S(1)}, bf16[2,1024,384]{2,1,0:T(8,128)(2,1)S(1)}, u32[]{:S(2)}, u32[]{:S(2)}) collective-permute-start(bf16[2,1024,384]{2,1,0:T(8,128)(2,1)S(1)} %pad_maximum_fusion.1), channel_id=1, source_target_pairs={{1,0},{0,1},{3,2},{2,3},{5,4},{4,5},{7,6},{6,7},{9,8},{8,9},{11,10... | collective-permute-start | bytes 4718600 | tf_op jit(solution)/shard_map/ppermute | solution.py:35
  98.2 14.0 %collective-permute-start.9 = (bf16[72,2048]{1,0:T(8,128)(2,1)S(1)}, bf16[72,2048]{1,0:T(8,128)(2,1)S(1)}, u32[]{:S(2)}, u32[]{:S(2)}) collective-permute-start(bf16[72,2048]{1,0:T(8,128)(2,1)S(1)} %get-tuple-element.220), channel_id=1, source_target_pairs={{0,4},{2,6},{4,8},{6,10},{8,12},{10,14},{12,0},{14,2},{1,5},{3,7},... | collective-permute-start | bytes 884744 | tf_op jit(solution)/shard_map/ppermute | solution.py:158
  101.4 22.9 %collective-permute-start.8 = (bf16[72,2048]{1,0:T(8,128)(2,1)S(1)}, bf16[72,2048]{1,0:T(8,128)(2,1)S(1)}, u32[]{:S(2)}, u32[]{:S(2)}) collective-permute-start(bf16[72,2048]{1,0:T(8,128)(2,1)S(1)} %get-tuple-element.221), channel_id=1, source_target_pairs={{0,8},{2,10},{4,12},{6,14},{8,0},{10,2},{12,4},{14,6},{1,9},{3,11}... | collective-permute-start | bytes 884744 | tf_op jit(solution)/shard_map/ppermute | solution.py:158
  104.8 19.6 %collective-permute-start.7 = (bf16[72,2048]{1,0:T(8,128)(2,1)S(1)}, bf16[72,2048]{1,0:T(8,128)(2,1)S(1)}, u32[]{:S(2)}, u32[]{:S(2)}) collective-permute-start(bf16[72,2048]{1,0:T(8,128)(2,1)S(1)} %get-tuple-element.222), channel_id=1, source_target_pairs={{0,12},{2,14},{4,0},{6,2},{8,4},{10,6},{12,8},{14,10},{1,13},{3,15... | collective-permute-start | bytes 884744 | tf_op jit(solution)/shard_map/ppermute | solution.py:158
  125.3 6.0 %copy-start.11 = (bf16[1,1,2,1024,384]{4,3,2,1,0:T(8,128)(2,1)S(1)}, bf16[1,1,2,1024,384]{4,3,2,1,0:T(8,128)(2,1)}, u32[]{:S(2)}) copy-start(bf16[1,1,2,1024,384]{4,3,2,1,0:T(8,128)(2,1)} %param.28) | copy-start | bytes 4718596
  125.4 6.0 %copy-start.12 = (bf16[1,1,2,1024,384]{4,3,2,1,0:T(8,128)(2,1)S(1)}, bf16[1,1,2,1024,384]{4,3,2,1,0:T(8,128)(2,1)}, u32[]{:S(2)}) copy-start(bf16[1,1,2,1024,384]{4,3,2,1,0:T(8,128)(2,1)} %param.30) | copy-start | bytes 4718596
  125.4 13.9 %collective-permute-start.10 = (bf16[128,2048]{1,0:T(8,128)(2,1)S(1)}, bf16[128,2048]{1,0:T(8,128)(2,1)S(1)}, u32[]{:S(2)}, u32[]{:S(2)}) collective-permute-start(bf16[128,2048]{1,0:T(8,128)(2,1)S(1)} %fusion.9), channel_id=1, source_target_pairs={{16,0},{0,16},{17,1},{1,17},{18,2},{2,18},{19,3},{3,19},{20,4},{4,... | collective-permute-start | bytes 1572872 | tf_op jit(solution)/shard_map/ppermute | solution.py:35
  127.9 39.2 %collective-permute-start.15 = (bf16[384,1024]{1,0:T(8,128)(2,1)S(1)}, bf16[384,1024]{1,0:T(8,128)(2,1)S(1)}, u32[]{:S(2)}, u32[]{:S(2)}) collective-permute-start(bf16[384,1024]{1,0:T(8,128)(2,1)S(1)} %convolution_convert_fusion.6), channel_id=1, source_target_pairs={{1,0},{0,1},{3,2},{2,3},{5,4},{4,5},{7,6},{6,7},{9,8},{8,9},{11,10... | collective-permute-start | bytes 2359304 | tf_op jit(solution)/shard_map/ppermute | solution.py:35
  132.8 17.3 %copy-start = (bf16[2,1024,384]{2,1,0:T(8,128)(2,1)}, bf16[2,1024,384]{2,1,0:T(8,128)(2,1)S(1)}, u32[]{:S(2)}) copy-start(bf16[2,1024,384]{2,1,0:T(8,128)(2,1)S(1)} %get-tuple-element.148) | copy-start | bytes 4718596
  139.3 1.6 copy-start.9
  139.5 10.6 %copy-start.4 = (f32[1,1,2,1024,384]{4,3,2,1,0:T(8,128)S(1)}, f32[1,1,2,1024,384]{4,3,2,1,0:T(8,128)}, u32[]{:S(2)}) copy-start(f32[1,1,2,1024,384]{4,3,2,1,0:T(8,128)} %param.26) | copy-start | bytes 9437188
  140.9 14.3 %collective-permute-start.18 = (bf16[72,2048]{1,0:T(8,128)(2,1)S(1)}, bf16[72,2048]{1,0:T(8,128)(2,1)S(1)}, u32[]{:S(2)}, u32[]{:S(2)}) collective-permute-start(bf16[72,2048]{1,0:T(8,128)(2,1)S(1)} %get-tuple-element.218), channel_id=1, source_target_pairs={{0,4},{2,6},{4,8},{6,10},{8,12},{10,14},{12,0},{14,2},{1,5},{3,7},... | collective-permute-start | bytes 884744 | tf_op jit(solution)/shard_map/ppermute | solution.py:149
  147.7 17.3 %collective-permute-start.19 = (bf16[72,2048]{1,0:T(8,128)(2,1)S(1)}, bf16[72,2048]{1,0:T(8,128)(2,1)S(1)}, u32[]{:S(2)}, u32[]{:S(2)}) collective-permute-start(bf16[72,2048]{1,0:T(8,128)(2,1)S(1)} %get-tuple-element.217), channel_id=1, source_target_pairs={{0,8},{2,10},{4,12},{6,14},{8,0},{10,2},{12,4},{14,6},{1,9},{3,11}... | collective-permute-start | bytes 884744 | tf_op jit(solution)/shard_map/ppermute | solution.py:149
  147.7 18.3 %collective-permute-start.20 = (bf16[72,2048]{1,0:T(8,128)(2,1)S(1)}, bf16[72,2048]{1,0:T(8,128)(2,1)S(1)}, u32[]{:S(2)}, u32[]{:S(2)}) collective-permute-start(bf16[72,2048]{1,0:T(8,128)(2,1)S(1)} %get-tuple-element.216), channel_id=1, source_target_pairs={{0,12},{2,14},{4,0},{6,2},{8,4},{10,6},{12,8},{14,10},{1,13},{3,15... | collective-permute-start | bytes 884744 | tf_op jit(solution)/shard_map/ppermute | solution.py:149
  152.9 14.2 %copy-start.17 = (bf16[1,1,384,1024]{3,2,1,0:T(8,128)(2,1)S(1)}, bf16[1,1,384,1024]{3,2,1,0:T(8,128)(2,1)}, u32[]{:S(2)}) copy-start(bf16[1,1,384,1024]{3,2,1,0:T(8,128)(2,1)} %param.29) | copy-start | bytes 2359300
  153.0 14.2 %copy-start.18 = (bf16[1,1,384,1024]{3,2,1,0:T(8,128)(2,1)S(1)}, bf16[1,1,384,1024]{3,2,1,0:T(8,128)(2,1)}, u32[]{:S(2)}) copy-start(bf16[1,1,384,1024]{3,2,1,0:T(8,128)(2,1)} %param.31) | copy-start | bytes 2359300
  153.0 197.6 %collective-permute-start.22 = (bf16[2,1024,384]{2,1,0:T(8,128)(2,1)}, bf16[2,1024,384]{2,1,0:T(8,128)(2,1)}, u32[]{:S(2)}, u32[]{:S(2)}) collective-permute-start(bf16[2,1024,384]{2,1,0:T(8,128)(2,1)} %fusion.5), channel_id=1, source_target_pairs={{1,0},{0,1},{3,2},{2,3},{5,4},{4,5},{7,6},{6,7},{9,8},{8,9},{11,10... | collective-permute-start | bytes 4718600 | tf_op jit(solution)/shard_map/ppermute | solution.py:35
  167.1 5.9 %collective-permute-start.21 = (bf16[288,2048]{1,0:T(8,128)(2,1)}, bf16[288,2048]{1,0:T(8,128)(2,1)}, u32[]{:S(2)}, u32[]{:S(2)}) collective-permute-start(bf16[288,2048]{1,0:T(8,128)(2,1)} %pad_maximum_fusion.6), channel_id=1, source_target_pairs={{0,2},{2,0},{4,6},{6,4},{8,10},{10,8},{12,14},{14,12},{1,3},{3,1},... | collective-permute-start | bytes 3538952 | tf_op jit(solution)/shard_map/ppermute | solution.py:164
  167.9 2.3 copy-start.1
  167.9 2.3 copy-start.2
  170.2 180.3 %collective-permute-start.23 = (bf16[384,1024]{1,0:T(8,128)(2,1)}, bf16[384,1024]{1,0:T(8,128)(2,1)}, u32[]{:S(2)}, u32[]{:S(2)}) collective-permute-start(bf16[384,1024]{1,0:T(8,128)(2,1)} %fusion.17.refs_0_), channel_id=1, source_target_pairs={{1,0},{0,1},{3,2},{2,3},{5,4},{4,5},{7,6},{6,7},{9,8},{8,9},{11,10... | collective-permute-start | bytes 2359304 | tf_op jit(solution)/shard_map/ppermute | solution.py:35
  350.6 2.4 copy-start.23
  368.1 11.2 %collective-permute-start.24 = (bf16[288,2048]{1,0:T(8,128)(2,1)}, bf16[288,2048]{1,0:T(8,128)(2,1)}, u32[]{:S(2)}, u32[]{:S(2)}) collective-permute-start(bf16[288,2048]{1,0:T(8,128)(2,1)} %pad_maximum_fusion.7), channel_id=1, source_target_pairs={{0,2},{2,0},{4,6},{6,4},{8,10},{10,8},{12,14},{14,12},{1,3},{3,1},... | collective-permute-start | bytes 3538952 | tf_op jit(solution)/shard_map/ppermute | solution.py:164
  376.0 3.4 copy-start.7
  376.0 3.4 copy-start.8
  381.2 11.9 %collective-permute-start.27 = (bf16[72,2048]{1,0:T(8,128)(2,1)S(1)}, bf16[72,2048]{1,0:T(8,128)(2,1)S(1)}, u32[]{:S(2)}, u32[]{:S(2)}) collective-permute-start(bf16[72,2048]{1,0:T(8,128)(2,1)S(1)} %get-tuple-element.211), channel_id=1, source_target_pairs={{0,4},{2,6},{4,8},{6,10},{8,12},{10,14},{12,0},{14,2},{1,5},{3,7},... | collective-permute-start | bytes 884744 | tf_op jit(solution)/shard_map/ppermute | solution.py:158
  381.2 23.5 %collective-permute-start.26 = (bf16[72,2048]{1,0:T(8,128)(2,1)S(1)}, bf16[72,2048]{1,0:T(8,128)(2,1)S(1)}, u32[]{:S(2)}, u32[]{:S(2)}) collective-permute-start(bf16[72,2048]{1,0:T(8,128)(2,1)S(1)} %get-tuple-element.212), channel_id=1, source_target_pairs={{0,8},{2,10},{4,12},{6,14},{8,0},{10,2},{12,4},{14,6},{1,9},{3,11}... | collective-permute-start | bytes 884744 | tf_op jit(solution)/shard_map/ppermute | solution.py:158
  382.2 22.6 %collective-permute-start.25 = (bf16[72,2048]{1,0:T(8,128)(2,1)S(1)}, bf16[72,2048]{1,0:T(8,128)(2,1)S(1)}, u32[]{:S(2)}, u32[]{:S(2)}) collective-permute-start(bf16[72,2048]{1,0:T(8,128)(2,1)S(1)} %get-tuple-element.213), channel_id=1, source_target_pairs={{0,12},{2,14},{4,0},{6,2},{8,4},{10,6},{12,8},{14,10},{1,13},{3,15... | collective-permute-start | bytes 884744 | tf_op jit(solution)/shard_map/ppermute | solution.py:158
  (4 other events, 4.0 us)

commit v4 on v3

--- a/solution.py
+++ b/solution.py
@@ -271,6 +271,9 @@
 def conveyor_kernel(chips, lag, pieces, this_round, places, *refs):
     count = len(pieces)
     source = refs[:count]
+    prior = ()
+    if this_round:
+        prior, refs = refs[count : 2 * count], refs[:count] + refs[2 * count :]
     result = refs[count : 2 * count]
     own = refs[2 * count : 3 * count]
     out = refs[3 * count : 4 * count]
@@ -278,7 +281,8 @@
     down_in = refs[5 * count : 6 * count]
     up_out = refs[6 * count : 7 * count]
     down_out = refs[7 * count : 8 * count]
-    loaded, stored, up_sent, down_sent, up_got, down_got = refs[8 * count :]
+    loaded, stored, up_sent, down_sent, up_got, down_got, *primed = refs[8 * count :]
+    kept = out if prior else own
     place = lax.axis_index("expert")
     chip = place // 2
     above, below = {"expert": place + 2}, {"expert": place - 2}
@@ -290,6 +294,10 @@
         def load(i, carry, k=k, rows=rows, offset=offset):
             part = pl.ds(pl.multiple_of(i * rows, rows), rows)
             pltpu.make_async_copy(source[k].at[part], own[k].at[part], loaded.at[offset + i]).start()
+            if prior:
+                pltpu.make_async_copy(
+                    prior[k].at[part], out[k].at[part], primed[0].at[offset + i]
+                ).start()
             return carry
 
         lax.fori_loop(0, number, load, 0)
@@ -354,19 +362,23 @@
             @pl.when((index >= offset) & (index < offset + number))
             def _(k=k, rows=rows, offset=offset):
                 part = pl.ds(pl.multiple_of((index - offset) * rows, rows), rows)
+                if prior:
+                    pltpu.make_async_copy(
+                        prior[k].at[part], out[k].at[part], primed[0].at[index]
+                    ).wait()
 
                 @pl.when(jnp.logical_not(has_below))
                 def _():
-                    out[k][part] = jnp.where(take_down, down_in[k][part], own[k][part])
+                    out[k][part] = jnp.where(take_down, down_in[k][part], kept[k][part])
 
                 @pl.when(jnp.logical_not(has_above))
                 def _():
-                    out[k][part] = jnp.where(take_up, up_in[k][part], own[k][part])
+                    out[k][part] = jnp.where(take_up, up_in[k][part], kept[k][part])
 
                 @pl.when(has_below & has_above)
                 def _():
-                    kept = jnp.where(take_down, down_in[k][part], own[k][part])
-                    out[k][part] = jnp.where(take_up, up_in[k][part], kept)
+                    other = jnp.where(take_down, down_in[k][part], kept[k][part])
+                    out[k][part] = jnp.where(take_up, up_in[k][part], other)
 
             offset += number
 
@@ -423,7 +435,7 @@
             pltpu.make_async_copy(down_in[k], down_in[k], down_sent.at[k]).wait()
 
 
-def conveyed(arrays, place, this_round, lag, piece_bytes):
+def conveyed(arrays, place, this_round, lag, piece_bytes, before=()):
     chips = place.shape[0]
     pieces = []
     for array in arrays:
@@ -439,7 +451,7 @@
     return pl.pallas_call(
         functools.partial(conveyor_kernel, chips, lag, tuple(pieces), this_round),
         out_shape=[jax.ShapeDtypeStruct(array.shape, array.dtype) for array in arrays],
-        in_specs=[pl.BlockSpec(memory_space=pltpu.SMEM)] + [in_place] * len(arrays),
+        in_specs=[pl.BlockSpec(memory_space=pltpu.SMEM)] + [in_place] * len(arrays + list(before)),
         out_specs=[in_place] * len(arrays),
         scratch_shapes=whole * 6
         + [
@@ -449,14 +461,15 @@
             pltpu.SemaphoreType.DMA((len(arrays),)),
             pltpu.SemaphoreType.DMA((total,)),
             pltpu.SemaphoreType.DMA((total,)),
-        ],
+        ]
+        + [pltpu.SemaphoreType.DMA((total,))] * bool(before),
         compiler_params=pltpu.CompilerParams(
             collective_id=1 + this_round, has_side_effects=True, vmem_limit_bytes=62 << 20
         ),
         cost_estimate=pl.CostEstimate(
             flops=100 * moved, bytes_accessed=2 * moved, transcendentals=0
         ),
-    )(place, *arrays)
+    )(place, *arrays, *before)
 
 
 def first_journey(arrays, place):
@@ -466,21 +479,14 @@
 
 def further_journeys(flat, result, place, need):
     chips = place.shape[0]
-    chip = lax.axis_index("expert") // 2
 
     def rounds_from(this_round, before):
         if this_round == chips // 2:
             return before
 
         def further(before):
-            _, _, take_up, take_down = journey_flags(
-                [place[i] for i in range(chips)], chip, this_round
-            )
-            moved = conveyed(flat, place, this_round, LAG, PIECE)
-            merged = tuple(
-                jnp.where(take_up | take_down, new, old) for new, old in zip(moved, before)
-            )
-            return rounds_from(this_round + 1, merged)
+            merged = conveyed(flat, place, this_round, LAG, PIECE, before)
+            return rounds_from(this_round + 1, tuple(merged))
 
         return lax.cond(need > this_round, further, lambda before: before, before)
 

time: 412 us -> 412 us (level)
  no operation moved by 1% of the time
where the time goes in v4:
time: 412 us; the launch traced here: 407 us
  Pallas kernels  175 us (42%)
  waiting for transfers between devices  107 us (26%)
  starting transfers between devices  39.2 us (10%)
  other arithmetic  36.8 us (9%)
  matrix products  33.2 us (8%)
  local copies, waits for them, and re-layouts  13.9 us (3%)
    pallas_call x1, Pallas kernels, conveyed(): pl.pallas_call(functools.partial(conveyor_kernel, chips, lag, tuple(piece...  175 us
    ppermute x9, waiting for transfers between devices, across_chips(): arrived.append(lax.ppermute(blocks[distance], 'expert', route))  40.7 us
    ppermute x8, waiting for transfers between devices, passed_along(): return lax.ppermute(block, axis, route)  33.1 us
    ppermute x6, waiting for transfers between devices, back_across_chips(): arrived.append(lax.ppermute(blocks[distance], 'expert', route))  32.9 us
    ppermute x9, starting transfers between devices, across_chips(): arrived.append(lax.ppermute(blocks[distance], 'expert', route))  20 us
    dot_general x8, matrix products, projected(): jnp.dot(columns(token_rows, part, count), inner_parts[part][which], prefe...  11.6 us
    ppermute x6, starting transfers between devices, back_across_chips(): arrived.append(lax.ppermute(blocks[distance], 'expert', route))  10.4 us
    dot_general x8, matrix products, half_out(): jnp.dot(rows, outer, preferred_element_type=jnp.float32)  9.97 us
  transfers between devices with their start and end apart: 28, of which 14 were waited for; matrix products, arithmetic and copies ran while one was open for 12% of the time, Pallas kernels for 43%

profile of v4, /device:TPU:0, one launch (start us, length us, event | category | flops | bytes accessed | tf_op | source)
XLA Modules:
  0.0 407.5 jit_solution(4681090729774912701)
XLA Ops:
  0.7 1.4 fusion.28
  6.4 3.1 collective-permute-start
  9.4 2.6 collective-permute-start.1
  12.0 1.3 collective-permute-start.2
  15.9 1.5 collective-permute-start.17
  19.8 2.8 collective-permute-start.13
  25.3 7.0 %collective-permute-done.1 = bf16[72,2048]{1,0:T(8,128)(2,1)S(1)} collective-permute-done((bf16[72,2048]{1,0:T(8,128)(2,1)}, bf16[72,2048]{1,0:T(8,128)(2,1)S(1)}, u32[]{:S(2)}, u32[]{:S(2)}) %collective-permute-start.1) | collective-permute-done | bytes 294944 | tf_op jit(solution)/shard_map/ppermute | solution.py:149
  32.3 1.7 collective-permute-start.4
  34.4 1.3 pad_maximum_fusion.2
  35.6 3.1 collective-permute-done.11
  38.8 18.1 %collective-permute-done.12 = bf16[72,2048]{1,0:T(8,128)(2,1)} collective-permute-done((bf16[72,2048]{1,0:T(8,128)(2,1)}, bf16[72,2048]{1,0:T(8,128)(2,1)}, u32[]{:S(2)}, u32[]{:S(2)}) %collective-permute-start.12) | collective-permute-done | bytes 294944 | tf_op jit(solution)/shard_map/ppermute | solution.py:149
  56.9 1.4 pad_maximum_fusion.5
  62.6 22.7 %collective-permute-done.5 = bf16[384,1024]{1,0:T(8,128)(2,1)S(1)} collective-permute-done((bf16[384,1024]{1,0:T(8,128)(2,1)S(1)}, bf16[384,1024]{1,0:T(8,128)(2,1)S(1)}, u32[]{:S(2)}, u32[]{:S(2)}) %collective-permute-start.5) | collective-permute-done | bytes 786464 | tf_op jit(solution)/shard_map/ppermute | solution.py:35
  94.0 1.8 collective-permute-start.16
  98.1 3.2 collective-permute-start.9
  101.4 3.3 collective-permute-start.8
  106.5 5.7 %collective-permute-done.9 = bf16[72,2048]{1,0:T(8,128)(2,1)S(1)} collective-permute-done((bf16[72,2048]{1,0:T(8,128)(2,1)S(1)}, bf16[72,2048]{1,0:T(8,128)(2,1)S(1)}, u32[]{:S(2)}, u32[]{:S(2)}) %collective-permute-start.9) | collective-permute-done | bytes 294944 | tf_op jit(solution)/shard_map/ppermute | solution.py:158
  112.2 12.1 %collective-permute-done.8 = bf16[72,2048]{1,0:T(8,128)(2,1)S(1)} collective-permute-done((bf16[72,2048]{1,0:T(8,128)(2,1)S(1)}, bf16[72,2048]{1,0:T(8,128)(2,1)S(1)}, u32[]{:S(2)}, u32[]{:S(2)}) %collective-permute-start.8) | collective-permute-done | bytes 294944 | tf_op jit(solution)/shard_map/ppermute | solution.py:158
  125.3 1.5 collective-permute-start.10
  128.4 2.9 collective-permute-done.16
  131.4 1.4 fusion.4
  132.8 6.4 %collective-permute-done.10 = bf16[128,2048]{1,0:T(8,128)(2,1)S(1)} collective-permute-done((bf16[128,2048]{1,0:T(8,128)(2,1)S(1)}, bf16[128,2048]{1,0:T(8,128)(2,1)S(1)}, u32[]{:S(2)}, u32[]{:S(2)}) %collective-permute-start.10) | collective-permute-done | bytes 524320 | tf_op jit(solution)/shard_map/ppermute | solution.py:35
  140.8 6.9 %collective-permute-start.18 = (bf16[72,2048]{1,0:T(8,128)(2,1)S(1)}, bf16[72,2048]{1,0:T(8,128)(2,1)S(1)}, u32[]{:S(2)}, u32[]{:S(2)}) collective-permute-start(bf16[72,2048]{1,0:T(8,128)(2,1)S(1)} %get-tuple-element.219), channel_id=1, source_target_pairs={{0,4},{2,6},{4,8},{6,10},{8,12},{10,14},{12,0},{14,2},{1,5},{3,7},... | collective-permute-start | bytes 884744 | tf_op jit(solution)/shard_map/ppermute | solution.py:149
  147.7 2.4 collective-permute-start.20
  150.1 2.9 fusion.5
  153.5 1.6 collective-permute-done.18
  155.1 9.9 %collective-permute-done.19 = bf16[72,2048]{1,0:T(8,128)(2,1)S(1)} collective-permute-done((bf16[72,2048]{1,0:T(8,128)(2,1)S(1)}, bf16[72,2048]{1,0:T(8,128)(2,1)S(1)}, u32[]{:S(2)}, u32[]{:S(2)}) %collective-permute-start.19) | collective-permute-done | bytes 294944 | tf_op jit(solution)/shard_map/ppermute | solution.py:149
  168.5 1.7 fusion.17.refs_0_
  173.0 2.4 constant_dynamic-update-slice_fusion.10
  175.4 175.1 %shard_map.189 = (bf16[384,1024]{1,0:T(8,128)(2,1)}, bf16[384,1024]{1,0:T(8,128)(2,1)}, bf16[384,1024]{1,0:T(8,128)(2,1)}, bf16[2048,384]{1,0:T(8,128)(2,1)}, bf...) custom-call(s32[4]{0:T(128)S(1)} %bitcast.134, bf16[384,1024]{1,0:T(8,128)(2,1)} %fusion.17.refs_0_, ...), custom_call_target="tpu_custom_call" | custom-call | flops 707788800 | bytes 14155776 | tf_op jit(solution)/shard_map/pallas_call | solution.py:451
  350.6 2.4 fusion.39
  353.0 1.9 fusion.41
  354.9 1.9 convolution_add_fusion.3
  356.8 2.0 fusion.23
  358.9 1.6 convolution_convert_fusion.8
  360.5 2.4 convolution_convert_fusion.10
  363.0 1.6 convolution_convert_fusion.9
  364.6 2.4 convolution_convert_fusion.11
  368.2 2.8 fusion.2
  371.0 2.2 fusion.46
  373.2 2.8 fusion.3
  376.1 3.4 convert_select_fusion
  379.4 1.7 add_convert_fusion
  382.2 2.9 collective-permute-start.25
  385.1 2.2 fusion.45
  387.3 2.5 fusion.13
  389.8 3.4 collective-permute-done.27
  393.1 11.7 %collective-permute-done.26 = bf16[72,2048]{1,0:T(8,128)(2,1)S(1)} collective-permute-done((bf16[72,2048]{1,0:T(8,128)(2,1)S(1)}, bf16[72,2048]{1,0:T(8,128)(2,1)S(1)}, u32[]{:S(2)}, u32[]{:S(2)}) %collective-permute-start.26) | collective-permute-done | bytes 294944 | tf_op jit(solution)/shard_map/ppermute | solution.py:158
  (151 shorter events, 43.7 us)
Async XLA Ops:
  5.2 8.2 %copy-start.20 = (f32[1,128,2]{1,2,0:T(2,128)S(1)}, f32[1,128,2]{1,2,0:T(2,128)}, u32[]{:S(2)}) copy-start(f32[1,128,2]{1,2,0:T(2,128)} %param.22) | copy-start | bytes 3076
  5.2 8.3 %copy-start.23 = (bf16[1,128,2048]{2,1,0:T(8,128)(2,1)S(1)}, bf16[1,128,2048]{2,1,0:T(8,128)(2,1)}, u32[]{:S(2)}) copy-start(bf16[1,128,2048]{2,1,0:T(8,128)(2,1)} %param.19) | copy-start | bytes 1572868
  6.4 13.5 %collective-permute-start = (bf16[72,2048]{1,0:T(8,128)(2,1)}, bf16[72,2048]{1,0:T(8,128)(2,1)S(1)}, u32[]{:S(2)}, u32[]{:S(2)}) collective-permute-start(bf16[72,2048]{1,0:T(8,128)(2,1)} %get-tuple-element.233), channel_id=1, source_target_pairs={{0,4},{2,6},{4,8},{6,10},{8,12},{10,14},{12,0},{14,2},{1,5},{3,7},... | collective-permute-start | bytes 884744 | tf_op jit(solution)/shard_map/ppermute | solution.py:149
  9.4 22.9 %collective-permute-start.1 = (bf16[72,2048]{1,0:T(8,128)(2,1)}, bf16[72,2048]{1,0:T(8,128)(2,1)S(1)}, u32[]{:S(2)}, u32[]{:S(2)}) collective-permute-start(bf16[72,2048]{1,0:T(8,128)(2,1)} %get-tuple-element.232), channel_id=1, source_target_pairs={{0,8},{2,10},{4,12},{6,14},{8,0},{10,2},{12,4},{14,6},{1,9},{3,11}... | collective-permute-start | bytes 884744 | tf_op jit(solution)/shard_map/ppermute | solution.py:149
  12.0 22.1 %collective-permute-start.2 = (bf16[72,2048]{1,0:T(8,128)(2,1)}, bf16[72,2048]{1,0:T(8,128)(2,1)}, u32[]{:S(2)}, u32[]{:S(2)}) collective-permute-start(bf16[72,2048]{1,0:T(8,128)(2,1)} %get-tuple-element.231), channel_id=1, source_target_pairs={{0,12},{2,14},{4,0},{6,2},{8,4},{10,6},{12,8},{14,10},{1,13},{3,15... | collective-permute-start | bytes 884744 | tf_op jit(solution)/shard_map/ppermute | solution.py:149
  13.5 3.9 copy-start.3
  14.0 1.9 copy-start.19
  15.2 2.4 copy-start.5
  15.2 23.5 %collective-permute-start.11 = (bf16[72,2048]{1,0:T(8,128)(2,1)}, bf16[72,2048]{1,0:T(8,128)(2,1)}, u32[]{:S(2)}, u32[]{:S(2)}) collective-permute-start(bf16[72,2048]{1,0:T(8,128)(2,1)} %get-tuple-element.228), channel_id=1, source_target_pairs={{0,4},{2,6},{4,8},{6,10},{8,12},{10,14},{12,0},{14,2},{1,5},{3,7},... | collective-permute-start | bytes 884744 | tf_op jit(solution)/shard_map/ppermute | solution.py:149
  15.9 3.6 collective-permute-start.17
  19.5 37.4 %collective-permute-start.12 = (bf16[72,2048]{1,0:T(8,128)(2,1)}, bf16[72,2048]{1,0:T(8,128)(2,1)}, u32[]{:S(2)}, u32[]{:S(2)}) collective-permute-start(bf16[72,2048]{1,0:T(8,128)(2,1)} %get-tuple-element.227), channel_id=1, source_target_pairs={{0,8},{2,10},{4,12},{6,14},{8,0},{10,2},{12,4},{14,6},{1,9},{3,11}... | collective-permute-start | bytes 884744 | tf_op jit(solution)/shard_map/ppermute | solution.py:149
  19.8 37.0 %collective-permute-start.13 = (bf16[72,2048]{1,0:T(8,128)(2,1)}, bf16[72,2048]{1,0:T(8,128)(2,1)}, u32[]{:S(2)}, u32[]{:S(2)}) collective-permute-start(bf16[72,2048]{1,0:T(8,128)(2,1)} %get-tuple-element.226), channel_id=1, source_target_pairs={{0,12},{2,14},{4,0},{6,2},{8,4},{10,6},{12,8},{14,10},{1,13},{3,15... | collective-permute-start | bytes 884744 | tf_op jit(solution)/shard_map/ppermute | solution.py:149
  25.3 31.5 %copy-start.13 = (bf16[72,2048]{1,0:T(8,128)(2,1)S(1)}, bf16[72,2048]{1,0:T(8,128)(2,1)}, u32[]{:S(2)}) copy-start(bf16[72,2048]{1,0:T(8,128)(2,1)} %get-tuple-element.224) | copy-start | bytes 884740
  32.3 54.6 %collective-permute-start.4 = (bf16[2,1024,384]{2,1,0:T(8,128)(2,1)S(1)}, bf16[2,1024,384]{2,1,0:T(8,128)(2,1)S(1)}, u32[]{:S(2)}, u32[]{:S(2)}) collective-permute-start(bf16[2,1024,384]{2,1,0:T(8,128)(2,1)S(1)} %bitcast_convert_fusion), channel_id=1, source_target_pairs={{1,0},{0,1},{3,2},{2,3},{5,4},{4,5},{7,6},{6,7},{9,8},{8,9},{11,10... | collective-permute-start | bytes 4718600 | tf_op jit(solution)/shard_map/ppermute | solution.py:35
  34.1 51.2 %collective-permute-start.5 = (bf16[384,1024]{1,0:T(8,128)(2,1)S(1)}, bf16[384,1024]{1,0:T(8,128)(2,1)S(1)}, u32[]{:S(2)}, u32[]{:S(2)}) collective-permute-start(bf16[384,1024]{1,0:T(8,128)(2,1)S(1)} %bitcast_convert_fusion.1), channel_id=1, source_target_pairs={{1,0},{0,1},{3,2},{2,3},{5,4},{4,5},{7,6},{6,7},{9,8},{8,9},{11,10... | collective-permute-start | bytes 2359304 | tf_op jit(solution)/shard_map/ppermute | solution.py:35
  34.4 24.0 %copy-start.17 = (bf16[576,2048]{1,0:T(8,128)(2,1)S(1)}, bf16[576,2048]{1,0:T(8,128)(2,1)}, u32[]{:S(2)}) copy-start(bf16[576,2048]{1,0:T(8,128)(2,1)} %get-tuple-element.230) | copy-start | bytes 7077892
  38.7 23.6 %collective-permute-start.3 = (bf16[288,2048]{1,0:T(8,128)(2,1)S(1)}, bf16[288,2048]{1,0:T(8,128)(2,1)S(1)}, u32[]{:S(2)}, u32[]{:S(2)}) collective-permute-start(bf16[288,2048]{1,0:T(8,128)(2,1)S(1)} %pad_maximum_fusion.2), channel_id=1, source_target_pairs={{0,2},{2,0},{4,6},{6,4},{8,10},{10,8},{12,14},{14,12},{1,3},{3,1},... | collective-permute-start | bytes 3538952 | tf_op jit(solution)/shard_map/ppermute | solution.py:164
  56.9 2.5 copy-start.14
  58.2 4.2 %collective-permute-start.14 = (bf16[288,2048]{1,0:T(8,128)(2,1)S(1)}, bf16[288,2048]{1,0:T(8,128)(2,1)S(1)}, u32[]{:S(2)}, u32[]{:S(2)}) collective-permute-start(bf16[288,2048]{1,0:T(8,128)(2,1)S(1)} %pad_maximum_fusion.5), channel_id=1, source_target_pairs={{0,2},{2,0},{4,6},{6,4},{8,10},{10,8},{12,14},{14,12},{1,3},{3,1},... | collective-permute-start | bytes 3538952 | tf_op jit(solution)/shard_map/ppermute | solution.py:164
  92.8 4.8 %collective-permute-start.6 = (bf16[288,2048]{1,0:T(8,128)(2,1)S(1)}, bf16[288,2048]{1,0:T(8,128)(2,1)S(1)}, u32[]{:S(2)}, u32[]{:S(2)}) collective-permute-start(bf16[288,2048]{1,0:T(8,128)(2,1)S(1)} %pad_maximum_fusion.3), channel_id=1, source_target_pairs={{0,2},{2,0},{4,6},{6,4},{8,10},{10,8},{12,14},{14,12},{1,3},{3,1},... | collective-permute-start | bytes 3538952 | tf_op jit(solution)/shard_map/ppermute | solution.py:164
  94.0 37.3 %collective-permute-start.16 = (bf16[2,1024,384]{2,1,0:T(8,128)(2,1)S(1)}, bf16[2,1024,384]{2,1,0:T(8,128)(2,1)S(1)}, u32[]{:S(2)}, u32[]{:S(2)}) collective-permute-start(bf16[2,1024,384]{2,1,0:T(8,128)(2,1)S(1)} %pad_maximum_fusion.1), channel_id=1, source_target_pairs={{1,0},{0,1},{3,2},{2,3},{5,4},{4,5},{7,6},{6,7},{9,8},{8,9},{11,10... | collective-permute-start | bytes 4718600 | tf_op jit(solution)/shard_map/ppermute | solution.py:35
  98.1 14.0 %collective-permute-start.9 = (bf16[72,2048]{1,0:T(8,128)(2,1)S(1)}, bf16[72,2048]{1,0:T(8,128)(2,1)S(1)}, u32[]{:S(2)}, u32[]{:S(2)}) collective-permute-start(bf16[72,2048]{1,0:T(8,128)(2,1)S(1)} %get-tuple-element.221), channel_id=1, source_target_pairs={{0,4},{2,6},{4,8},{6,10},{8,12},{10,14},{12,0},{14,2},{1,5},{3,7},... | collective-permute-start | bytes 884744 | tf_op jit(solution)/shard_map/ppermute | solution.py:158
  101.4 22.9 %collective-permute-start.8 = (bf16[72,2048]{1,0:T(8,128)(2,1)S(1)}, bf16[72,2048]{1,0:T(8,128)(2,1)S(1)}, u32[]{:S(2)}, u32[]{:S(2)}) collective-permute-start(bf16[72,2048]{1,0:T(8,128)(2,1)S(1)} %get-tuple-element.222), channel_id=1, source_target_pairs={{0,8},{2,10},{4,12},{6,14},{8,0},{10,2},{12,4},{14,6},{1,9},{3,11}... | collective-permute-start | bytes 884744 | tf_op jit(solution)/shard_map/ppermute | solution.py:158
  104.7 19.6 %collective-permute-start.7 = (bf16[72,2048]{1,0:T(8,128)(2,1)S(1)}, bf16[72,2048]{1,0:T(8,128)(2,1)S(1)}, u32[]{:S(2)}, u32[]{:S(2)}) collective-permute-start(bf16[72,2048]{1,0:T(8,128)(2,1)S(1)} %get-tuple-element.223), channel_id=1, source_target_pairs={{0,12},{2,14},{4,0},{6,2},{8,4},{10,6},{12,8},{14,10},{1,13},{3,15... | collective-permute-start | bytes 884744 | tf_op jit(solution)/shard_map/ppermute | solution.py:158
  125.3 6.1 %copy-start.11 = (bf16[1,1,2,1024,384]{4,3,2,1,0:T(8,128)(2,1)S(1)}, bf16[1,1,2,1024,384]{4,3,2,1,0:T(8,128)(2,1)}, u32[]{:S(2)}) copy-start(bf16[1,1,2,1024,384]{4,3,2,1,0:T(8,128)(2,1)} %param.28) | copy-start | bytes 4718596
  125.3 6.1 %copy-start.12 = (bf16[1,1,2,1024,384]{4,3,2,1,0:T(8,128)(2,1)S(1)}, bf16[1,1,2,1024,384]{4,3,2,1,0:T(8,128)(2,1)}, u32[]{:S(2)}) copy-start(bf16[1,1,2,1024,384]{4,3,2,1,0:T(8,128)(2,1)} %param.30) | copy-start | bytes 4718596
  125.3 13.9 %collective-permute-start.10 = (bf16[128,2048]{1,0:T(8,128)(2,1)S(1)}, bf16[128,2048]{1,0:T(8,128)(2,1)S(1)}, u32[]{:S(2)}, u32[]{:S(2)}) collective-permute-start(bf16[128,2048]{1,0:T(8,128)(2,1)S(1)} %fusion.9), channel_id=1, source_target_pairs={{16,0},{0,16},{17,1},{1,17},{18,2},{2,18},{19,3},{3,19},{20,4},{4,... | collective-permute-start | bytes 1572872 | tf_op jit(solution)/shard_map/ppermute | solution.py:35
  127.8 39.3 %collective-permute-start.15 = (bf16[384,1024]{1,0:T(8,128)(2,1)S(1)}, bf16[384,1024]{1,0:T(8,128)(2,1)S(1)}, u32[]{:S(2)}, u32[]{:S(2)}) collective-permute-start(bf16[384,1024]{1,0:T(8,128)(2,1)S(1)} %convolution_convert_fusion.6), channel_id=1, source_target_pairs={{1,0},{0,1},{3,2},{2,3},{5,4},{4,5},{7,6},{6,7},{9,8},{8,9},{11,10... | collective-permute-start | bytes 2359304 | tf_op jit(solution)/shard_map/ppermute | solution.py:35
  132.8 17.3 %copy-start = (bf16[2,1024,384]{2,1,0:T(8,128)(2,1)}, bf16[2,1024,384]{2,1,0:T(8,128)(2,1)S(1)}, u32[]{:S(2)}) copy-start(bf16[2,1024,384]{2,1,0:T(8,128)(2,1)S(1)} %get-tuple-element.151) | copy-start | bytes 4718596
  139.2 1.6 copy-start.9
  139.4 10.7 %copy-start.4 = (f32[1,1,2,1024,384]{4,3,2,1,0:T(8,128)S(1)}, f32[1,1,2,1024,384]{4,3,2,1,0:T(8,128)}, u32[]{:S(2)}) copy-start(f32[1,1,2,1024,384]{4,3,2,1,0:T(8,128)} %param.26) | copy-start | bytes 9437188
  140.8 14.3 %collective-permute-start.18 = (bf16[72,2048]{1,0:T(8,128)(2,1)S(1)}, bf16[72,2048]{1,0:T(8,128)(2,1)S(1)}, u32[]{:S(2)}, u32[]{:S(2)}) collective-permute-start(bf16[72,2048]{1,0:T(8,128)(2,1)S(1)} %get-tuple-element.219), channel_id=1, source_target_pairs={{0,4},{2,6},{4,8},{6,10},{8,12},{10,14},{12,0},{14,2},{1,5},{3,7},... | collective-permute-start | bytes 884744 | tf_op jit(solution)/shard_map/ppermute | solution.py:149
  147.7 17.3 %collective-permute-start.19 = (bf16[72,2048]{1,0:T(8,128)(2,1)S(1)}, bf16[72,2048]{1,0:T(8,128)(2,1)S(1)}, u32[]{:S(2)}, u32[]{:S(2)}) collective-permute-start(bf16[72,2048]{1,0:T(8,128)(2,1)S(1)} %get-tuple-element.218), channel_id=1, source_target_pairs={{0,8},{2,10},{4,12},{6,14},{8,0},{10,2},{12,4},{14,6},{1,9},{3,11}... | collective-permute-start | bytes 884744 | tf_op jit(solution)/shard_map/ppermute | solution.py:149
  147.7 18.3 %collective-permute-start.20 = (bf16[72,2048]{1,0:T(8,128)(2,1)S(1)}, bf16[72,2048]{1,0:T(8,128)(2,1)S(1)}, u32[]{:S(2)}, u32[]{:S(2)}) collective-permute-start(bf16[72,2048]{1,0:T(8,128)(2,1)S(1)} %get-tuple-element.217), channel_id=1, source_target_pairs={{0,12},{2,14},{4,0},{6,2},{8,4},{10,6},{12,8},{14,10},{1,13},{3,15... | collective-permute-start | bytes 884744 | tf_op jit(solution)/shard_map/ppermute | solution.py:149
  152.9 14.2 %copy-start.15 = (bf16[1,1,384,1024]{3,2,1,0:T(8,128)(2,1)S(1)}, bf16[1,1,384,1024]{3,2,1,0:T(8,128)(2,1)}, u32[]{:S(2)}) copy-start(bf16[1,1,384,1024]{3,2,1,0:T(8,128)(2,1)} %param.29) | copy-start | bytes 2359300
  152.9 14.2 %copy-start.16 = (bf16[1,1,384,1024]{3,2,1,0:T(8,128)(2,1)S(1)}, bf16[1,1,384,1024]{3,2,1,0:T(8,128)(2,1)}, u32[]{:S(2)}) copy-start(bf16[1,1,384,1024]{3,2,1,0:T(8,128)(2,1)} %param.31) | copy-start | bytes 2359300
  152.9 197.6 %collective-permute-start.22 = (bf16[2,1024,384]{2,1,0:T(8,128)(2,1)}, bf16[2,1024,384]{2,1,0:T(8,128)(2,1)}, u32[]{:S(2)}, u32[]{:S(2)}) collective-permute-start(bf16[2,1024,384]{2,1,0:T(8,128)(2,1)} %fusion.5), channel_id=1, source_target_pairs={{1,0},{0,1},{3,2},{2,3},{5,4},{4,5},{7,6},{6,7},{9,8},{8,9},{11,10... | collective-permute-start | bytes 4718600 | tf_op jit(solution)/shard_map/ppermute | solution.py:35
  167.1 5.9 %collective-permute-start.21 = (bf16[288,2048]{1,0:T(8,128)(2,1)}, bf16[288,2048]{1,0:T(8,128)(2,1)}, u32[]{:S(2)}, u32[]{:S(2)}) collective-permute-start(bf16[288,2048]{1,0:T(8,128)(2,1)} %pad_maximum_fusion.6), channel_id=1, source_target_pairs={{0,2},{2,0},{4,6},{6,4},{8,10},{10,8},{12,14},{14,12},{1,3},{3,1},... | collective-permute-start | bytes 3538952 | tf_op jit(solution)/shard_map/ppermute | solution.py:164
  167.9 2.3 copy-start.1
  167.9 2.3 copy-start.2
  170.2 180.3 %collective-permute-start.23 = (bf16[384,1024]{1,0:T(8,128)(2,1)}, bf16[384,1024]{1,0:T(8,128)(2,1)}, u32[]{:S(2)}, u32[]{:S(2)}) collective-permute-start(bf16[384,1024]{1,0:T(8,128)(2,1)} %fusion.17.refs_0_), channel_id=1, source_target_pairs={{1,0},{0,1},{3,2},{2,3},{5,4},{4,5},{7,6},{6,7},{9,8},{8,9},{11,10... | collective-permute-start | bytes 2359304 | tf_op jit(solution)/shard_map/ppermute | solution.py:35
  350.6 2.4 copy-start.18
  368.2 11.2 %collective-permute-start.24 = (bf16[288,2048]{1,0:T(8,128)(2,1)}, bf16[288,2048]{1,0:T(8,128)(2,1)}, u32[]{:S(2)}, u32[]{:S(2)}) collective-permute-start(bf16[288,2048]{1,0:T(8,128)(2,1)} %pad_maximum_fusion.7), channel_id=1, source_target_pairs={{0,2},{2,0},{4,6},{6,4},{8,10},{10,8},{12,14},{14,12},{1,3},{3,1},... | collective-permute-start | bytes 3538952 | tf_op jit(solution)/shard_map/ppermute | solution.py:164
  376.0 3.4 copy-start.7
  376.0 3.4 copy-start.8
  381.2 11.9 %collective-permute-start.27 = (bf16[72,2048]{1,0:T(8,128)(2,1)S(1)}, bf16[72,2048]{1,0:T(8,128)(2,1)S(1)}, u32[]{:S(2)}, u32[]{:S(2)}) collective-permute-start(bf16[72,2048]{1,0:T(8,128)(2,1)S(1)} %get-tuple-element.212), channel_id=1, source_target_pairs={{0,4},{2,6},{4,8},{6,10},{8,12},{10,14},{12,0},{14,2},{1,5},{3,7},... | collective-permute-start | bytes 884744 | tf_op jit(solution)/shard_map/ppermute | solution.py:158
  381.3 23.5 %collective-permute-start.26 = (bf16[72,2048]{1,0:T(8,128)(2,1)S(1)}, bf16[72,2048]{1,0:T(8,128)(2,1)S(1)}, u32[]{:S(2)}, u32[]{:S(2)}) collective-permute-start(bf16[72,2048]{1,0:T(8,128)(2,1)S(1)} %get-tuple-element.213), channel_id=1, source_target_pairs={{0,8},{2,10},{4,12},{6,14},{8,0},{10,2},{12,4},{14,6},{1,9},{3,11}... | collective-permute-start | bytes 884744 | tf_op jit(solution)/shard_map/ppermute | solution.py:158
  382.2 22.6 %collective-permute-start.25 = (bf16[72,2048]{1,0:T(8,128)(2,1)S(1)}, bf16[72,2048]{1,0:T(8,128)(2,1)S(1)}, u32[]{:S(2)}, u32[]{:S(2)}) collective-permute-start(bf16[72,2048]{1,0:T(8,128)(2,1)S(1)} %get-tuple-element.214), channel_id=1, source_target_pairs={{0,12},{2,14},{4,0},{6,2},{8,4},{10,6},{12,8},{14,10},{1,13},{3,15... | collective-permute-start | bytes 884744 | tf_op jit(solution)/shard_map/ppermute | solution.py:158
  (4 other events, 4.0 us)
